TPU v7x, 32 devices: a whole 2x2x4 slice. The times are simulated.
32 devices in a mesh: head: 4 (over y, x), seq: 8 (over z, core).
Axes of the slice: x: 2, y: 2, z: 4, core: 2. Of those that a mesh axis runs over, the one named last changes fastest.
Arguments:
- hidden_in: bfloat16 [8192, 2048], P(('head', 'seq')), may hold values from -6 to 6
- cotangent: bfloat16 [8192, 2048], P(('head', 'seq')), may hold values from -6 to 6
- lengths: int32 [2], replicated, may hold values from 1024 to 4096, as said below
- token_order: int32 [8192], replicated, may hold values from 0 to 8191, as said below
- own_map: int32 [4, 192], P('head'), may hold values from 0 to 191, each once within a row
- w_query: bfloat16 [2048, 2048], P('seq', 'head'), may hold values from -0.125 to 0.125
- w_key: bfloat16 [2048, 2048], P('seq', 'head'), may hold values from -0.125 to 0.125
- w_value: bfloat16 [2048, 2048], P('seq', 'head'), may hold values from -0.125 to 0.125
- w_out: bfloat16 [2048, 2048], P('head', 'seq'), may hold values from -3 to 3
- w_up: bfloat16 [2048, 8192], P('seq', 'head'), may hold values from -0.125 to 0.125
- w_down: bfloat16 [8192, 2048], P('head', 'seq'), may hold values from -0.0625 to 0.0625
- gains: float32 [2, 2048], replicated, may hold values from 0.25 to 1.75
- biases: float32 [6, 2048], replicated, may hold values from -4 to 4
- up_bias: float32 [8192], P('head'), may hold values from -4 to 4
- vector_moment: float32 [8, 2048], replicated, may hold values from -48 to 48
- vector_second: float32 [8, 2048], replicated, may hold values from 1 to 20
- bias_moment: float32 [8192], P('head'), may hold values from -24 to 24
- bias_second: float32 [8192], P('head'), may hold values from 0.3 to 6
- step_count: int32 [1], replicated, may hold values from 1 to 20
- stat_left: float32 [768, 256, 256], P(('head', 'seq')), as said below
- stat_right: float32 [768, 256, 256], P(('head', 'seq')), as said below
- root_left: float32 [768, 256, 256], P(('head', 'seq')), as said below
- root_right: float32 [768, 256, 256], P(('head', 'seq')), as said below
- master: float32 [768, 256, 256], P(('head', 'seq')), may hold values from -0.125 to 0.125
Outputs:
- layer_out: bfloat16 [8192, 2048], P(('head', 'seq'))
- input_grad: float32 [8192, 2048], P(('head', 'seq'))
- block_grads: float32 [768, 256, 256], P(('head', 'seq'))
- stat_left_new: float32 [768, 256, 256], P(('head', 'seq'))
- stat_right_new: float32 [768, 256, 256], P(('head', 'seq'))
- master_new: float32 [768, 256, 256], P(('head', 'seq'))
- biases_new: float32 [6, 2048], replicated
- gains_new: float32 [2, 2048], replicated
- up_bias_new: float32 [8192], P('head')
- vector_grad: float32 [8, 2048], replicated
- vector_moment_new: float32 [8, 2048], replicated
- vector_second_new: float32 [8, 2048], replicated
- up_bias_grad: float32 [8192], P('head')
- bias_moment_new: float32 [8192], P('head')
- bias_second_new: float32 [8192], P('head')
Inputs may be any that keep to these rules, and one draw needn't show every extreme that they name: `lengths`: sequences are packed one after another from stream position 0; positions past the last are padding. One sequence has 4096 tokens and another 1024. `token_order`: A permutation of the stream positions that keeps aligned runs of 256 positions whole and in order. `own_map`: each row is a permutation of the 192 canonical blocks of its head group. `stat_left`: each block is symmetric. `stat_right`: each block is symmetric. `root_left`: each block is symmetric. `root_right`: each block is symmetric.
All inputs are finite; a program needn't handle non-finite values.
Results may differ from a plain program's by a relative error of at most 0.02.
Values may be sent and summed in bfloat16 or wider, within the bound.
A program may use at most 320 MiB of HBM per device.

v0:
```python
import math

import jax
import jax.numpy as jnp
from jax import lax
from jax.sharding import PartitionSpec as P

HDIM = 128
QROWS = 512
BLOCK = 256


NEG_LARGE = -1e30
NORM_EPS = 1e-12
ADAM_RATE = 0.4
SHAMPOO_RATE = 0.15


def shifted(array, axis, by):
    length = lax.axis_size(axis)
    return lax.ppermute(array, axis, [(i, (i + by) % length) for i in range(length)])


def segment_table(token_order, lengths):
    seq_count = lengths.shape[0]
    seq_ends = jnp.cumsum(lengths)
    before = jnp.sum((token_order[:, None] >= seq_ends[None, :]).astype(jnp.int32), axis=1)
    is_valid = token_order < seq_ends[seq_count - 1]
    row_ids = jnp.arange(token_order.shape[0], dtype=jnp.int32)
    return (jnp.where(is_valid, before, seq_count + row_ids), is_valid)


def normalize(z_rows, gain, shift):
    average = jnp.mean(z_rows, axis=-1, keepdims=True)
    centered = z_rows - average
    variance = jnp.mean(centered * centered, axis=-1, keepdims=True)
    recip = lax.rsqrt(variance + NORM_EPS)
    normed = centered * recip
    return (normed * gain + shift, normed, recip)


def normalize_back(grad_rows, normed, recip, gain):
    scaled = grad_rows * gain
    dz_rows = recip * (
        scaled
        - jnp.mean(scaled, axis=-1, keepdims=True)
        - normed * jnp.mean(scaled * normed, axis=-1, keepdims=True)
    )
    return (dz_rows, jnp.sum(grad_rows * normed, axis=0), jnp.sum(grad_rows, axis=0))


def presence(seg_rows, seq_count, groups):
    labels = jnp.arange(seq_count, dtype=jnp.int32)
    hits = seg_rows.reshape(groups, -1)[:, :, None] == labels[None, None, :]
    return jnp.max(hits.astype(jnp.float32), axis=1)


def block_flags(pres_query, pres_key, first_step, query_size, key_size):
    shared = jnp.dot(pres_query, pres_key.T) > 0.5
    query_low = jnp.arange(pres_query.shape[0], dtype=jnp.int32) * query_size
    key_low = jnp.arange(pres_key.shape[0], dtype=jnp.int32) * key_size
    touching = (query_low[:, None] < key_low[None, :] + key_size) & (
        key_low[None, :] < query_low[:, None] + query_size
    )
    return shared | touching & first_step


def pass_keys(key_part, value_part):
    return shifted((key_part, value_part), "seq", 1)


def pass_key_grads(key_grad, value_grad):
    return (
        shifted(key_grad.astype(jnp.bfloat16), "seq", 1).astype(key_grad.dtype),
        shifted(value_grad.astype(jnp.bfloat16), "seq", 1).astype(value_grad.dtype),
    )


def group_rows(rows_low):
    return lax.all_gather(rows_low, "head", axis=0, tiled=True)


def group_sums(partial_value):
    return lax.psum_scatter(
        partial_value.astype(jnp.bfloat16), "head", scatter_dimension=0, tiled=True
    ).astype(jnp.float32)


def key_segments(seg_grid, group_index, cycle_step):
    anchor = (group_index - cycle_step) % seg_grid.shape[1]
    return lax.dynamic_index_in_dim(seg_grid, anchor, 1, keepdims=False).reshape(-1)


def forward_pairs(running_state, query_all, seg_query, key_part, value_part, seg_key, pair_flags):
    key_size = key_part.shape[0] // pair_flags.shape[1]
    query_size = query_all.shape[0] // pair_flags.shape[0]
    score_scale = 1.0 / math.sqrt(query_all.shape[2])

    def forward_per_key(key_index, outer_state):
        key_low = key_index * key_size
        key_rows = lax.dynamic_slice_in_dim(key_part, key_low, key_size, 0)
        value_rows = lax.dynamic_slice_in_dim(value_part, key_low, key_size, 0)
        seg_cols = lax.dynamic_slice_in_dim(seg_key, key_low, key_size, 0)

        def forward_per_query(query_index, inner_state):

            def forward_compute(current):
                row_top, row_total, weighted = current
                query_low = query_index * query_size
                query_rows = lax.dynamic_slice_in_dim(query_all, query_low, query_size, 0)
                seg_rows = lax.dynamic_slice_in_dim(seg_query, query_low, query_size, 0)
                old_top = lax.dynamic_slice_in_dim(row_top, query_low, query_size, 0)
                old_total = lax.dynamic_slice_in_dim(row_total, query_low, query_size, 0)
                old_weighted = lax.dynamic_slice_in_dim(weighted, query_low, query_size, 0)
                scores = (
                    jnp.einsum(
                        "qhd,khd->qhk", query_rows, key_rows, preferred_element_type=jnp.float32
                    )
                    * score_scale
                )
                allowed = (seg_rows[:, None] == seg_cols[None, :])[:, None, :]
                scores = jnp.where(allowed, scores, NEG_LARGE)
                new_top = jnp.maximum(old_top, jnp.max(scores, axis=2))
                prob_rows = jnp.where(allowed, jnp.exp(scores - new_top[:, :, None]), 0.0)
                rescale = jnp.exp(old_top - new_top)
                new_total = old_total * rescale + jnp.sum(prob_rows, axis=2)
                new_weighted = old_weighted * rescale[:, :, None] + jnp.einsum(
                    "qhk,khd->qhd",
                    prob_rows.astype(jnp.bfloat16),
                    value_rows,
                    preferred_element_type=jnp.float32,
                )
                return (
                    lax.dynamic_update_slice_in_dim(row_top, new_top, query_low, 0),
                    lax.dynamic_update_slice_in_dim(row_total, new_total, query_low, 0),
                    lax.dynamic_update_slice_in_dim(weighted, new_weighted, query_low, 0),
                )

            return lax.cond(
                pair_flags[query_index, key_index],
                forward_compute,
                lambda current: current,
                inner_state,
            )

        return lax.fori_loop(0, pair_flags.shape[0], forward_per_query, outer_state)

    return lax.fori_loop(0, pair_flags.shape[1], forward_per_key, running_state)


def attend_forward(query_flat, key_flat, value_flat, seg_query, seg_grid, group_index, seq_count):
    row_count = query_flat.shape[0]
    heads_here = query_flat.shape[1] // HDIM
    query_all = query_flat.reshape(row_count, heads_here, HDIM)
    key_all = key_flat.reshape(row_count, heads_here, HDIM)
    value_all = value_flat.reshape(row_count, heads_here, HDIM)
    key_groups = seg_grid.shape[0]
    cycle_size = seg_grid.shape[1]
    pres_query = presence(seg_query, seq_count, row_count // QROWS)

    def process(running_state, key_part, value_part, cycle_step):
        seg_key = key_segments(seg_grid, group_index, cycle_step)
        pres_key = presence(seg_key, seq_count, key_groups)
        pair_flags = block_flags(
            pres_query, pres_key, cycle_step == 0, QROWS, row_count // key_groups
        )
        return forward_pairs(
            running_state, query_all, seg_query, key_part, value_part, seg_key, pair_flags
        )

    initial = (
        jnp.full((row_count, heads_here), NEG_LARGE, jnp.float32),
        jnp.zeros((row_count, heads_here), jnp.float32),
        jnp.zeros((row_count, heads_here, HDIM), jnp.float32),
    )
    running_state = process(initial, key_all, value_all, 0)

    def cycle_turn(cycle_step, cycle_carry):
        state_now, key_part, value_part = cycle_carry
        key_part, value_part = pass_keys(key_part, value_part)
        return (process(state_now, key_part, value_part, cycle_step), key_part, value_part)

    running_state, key_last, value_last = lax.fori_loop(
        1, cycle_size, cycle_turn, (running_state, key_all, value_all)
    )
    row_top, row_total, weighted = running_state
    attended = weighted / row_total[:, :, None]
    log_total = row_top + jnp.log(row_total)
    return (attended.reshape(row_count, heads_here * HDIM), log_total)


def backward_pairs(
    grad_state,
    query_all,
    grad_all,
    seg_query,
    log_total,
    delta,
    key_part,
    value_part,
    seg_key,
    pair_flags,
):
    key_size = key_part.shape[0] // pair_flags.shape[1]
    query_size = query_all.shape[0] // pair_flags.shape[0]
    score_scale = 1.0 / math.sqrt(query_all.shape[2])

    def backward_per_key(key_index, outer_state):
        key_low = key_index * key_size
        key_rows = lax.dynamic_slice_in_dim(key_part, key_low, key_size, 0)
        value_rows = lax.dynamic_slice_in_dim(value_part, key_low, key_size, 0)
        seg_cols = lax.dynamic_slice_in_dim(seg_key, key_low, key_size, 0)

        def backward_per_query(query_index, inner_state):

            def backward_compute(current):
                query_acc, key_acc, value_acc = current
                query_low = query_index * query_size
                query_rows = lax.dynamic_slice_in_dim(query_all, query_low, query_size, 0)
                grad_rows = lax.dynamic_slice_in_dim(grad_all, query_low, query_size, 0)
                seg_rows = lax.dynamic_slice_in_dim(seg_query, query_low, query_size, 0)
                total_rows = lax.dynamic_slice_in_dim(log_total, query_low, query_size, 0)
                delta_rows = lax.dynamic_slice_in_dim(delta, query_low, query_size, 0)
                scores = (
                    jnp.einsum(
                        "qhd,khd->qhk", query_rows, key_rows, preferred_element_type=jnp.float32
                    )
                    * score_scale
                )
                allowed = (seg_rows[:, None] == seg_cols[None, :])[:, None, :]
                prob_rows = jnp.where(allowed, jnp.exp(scores - total_rows[:, :, None]), 0.0)
                value_grad = jnp.einsum(
                    "qhk,qhd->khd",
                    prob_rows.astype(jnp.bfloat16),
                    grad_rows,
                    preferred_element_type=jnp.float32,
                )
                prob_grad = jnp.einsum(
                    "qhd,khd->qhk", grad_rows, value_rows, preferred_element_type=jnp.float32
                )
                score_grad = (prob_rows * (prob_grad - delta_rows[:, :, None])).astype(jnp.bfloat16)
                query_grad = (
                    jnp.einsum(
                        "qhk,khd->qhd", score_grad, key_rows, preferred_element_type=jnp.float32
                    )
                    * score_scale
                )
                key_grad = (
                    jnp.einsum(
                        "qhk,qhd->khd", score_grad, query_rows, preferred_element_type=jnp.float32
                    )
                    * score_scale
                )
                query_acc = lax.dynamic_update_slice_in_dim(
                    query_acc,
                    lax.dynamic_slice_in_dim(query_acc, query_low, query_size, 0) + query_grad,
                    query_low,
                    0,
                )
                key_acc = lax.dynamic_update_slice_in_dim(
                    key_acc,
                    lax.dynamic_slice_in_dim(key_acc, key_low, key_size, 0) + key_grad,
                    key_low,
                    0,
                )
                value_acc = lax.dynamic_update_slice_in_dim(
                    value_acc,
                    lax.dynamic_slice_in_dim(value_acc, key_low, key_size, 0) + value_grad,
                    key_low,
                    0,
                )
                return (query_acc, key_acc, value_acc)

            return lax.cond(
                pair_flags[query_index, key_index],
                backward_compute,
                lambda current: current,
                inner_state,
            )

        return lax.fori_loop(0, pair_flags.shape[0], backward_per_query, outer_state)

    return lax.fori_loop(0, pair_flags.shape[1], backward_per_key, grad_state)


def attend_backward(
    query_flat,
    key_flat,
    value_flat,
    attended,
    log_total,
    grad_low,
    seg_query,
    seg_grid,
    group_index,
    seq_count,
):
    row_count = query_flat.shape[0]
    heads_here = query_flat.shape[1] // HDIM
    query_all = query_flat.reshape(row_count, heads_here, HDIM)
    key_all = key_flat.reshape(row_count, heads_here, HDIM)
    value_all = value_flat.reshape(row_count, heads_here, HDIM)
    grad_all = grad_low.reshape(row_count, heads_here, HDIM)
    delta = jnp.sum(
        grad_all.astype(jnp.float32) * attended.reshape(row_count, heads_here, HDIM), axis=2
    )
    key_groups = seg_grid.shape[0]
    cycle_size = seg_grid.shape[1]
    pres_query = presence(seg_query, seq_count, row_count // QROWS)

    def process(query_acc, key_acc, value_acc, key_part, value_part, cycle_step):
        seg_key = key_segments(seg_grid, group_index, cycle_step)
        pres_key = presence(seg_key, seq_count, key_groups)
        pair_flags = block_flags(
            pres_query, pres_key, cycle_step == 0, QROWS, row_count // key_groups
        )
        return backward_pairs(
            (query_acc, key_acc, value_acc),
            query_all,
            grad_all,
            seg_query,
            log_total,
            delta,
            key_part,
            value_part,
            seg_key,
            pair_flags,
        )

    zeros_rows = jnp.zeros((row_count, heads_here, HDIM), jnp.float32)
    query_acc, key_acc, value_acc = process(
        zeros_rows, zeros_rows, zeros_rows, key_all, value_all, 0
    )

    def cycle_turn(cycle_step, cycle_carry):
        query_now, key_now, value_now, key_part, value_part = cycle_carry
        key_part, value_part = pass_keys(key_part, value_part)
        key_now, value_now = pass_key_grads(key_now, value_now)
        query_now, key_now, value_now = process(
            query_now, key_now, value_now, key_part, value_part, cycle_step
        )
        return (query_now, key_now, value_now, key_part, value_part)

    query_acc, key_acc, value_acc, key_last, value_last = lax.fori_loop(
        1, cycle_size, cycle_turn, (query_acc, key_acc, value_acc, key_all, value_all)
    )
    key_acc, value_acc = pass_key_grads(key_acc, value_acc)
    width_here = heads_here * HDIM
    return (
        query_acc.reshape(row_count, width_here).astype(jnp.bfloat16),
        key_acc.reshape(row_count, width_here).astype(jnp.bfloat16),
        value_acc.reshape(row_count, width_here).astype(jnp.bfloat16),
    )


def to_blocks(panel):
    height, breadth = panel.shape
    shaped = panel.reshape(height // BLOCK, BLOCK, breadth // BLOCK, BLOCK)
    return shaped.transpose(0, 2, 1, 3).reshape(-1, BLOCK, BLOCK)


def adam_step(param, grad, moment, second, step_float):
    moment_new = 0.9 * moment + 0.1 * grad
    second_new = 0.999 * second + 0.001 * grad * grad
    fix_one = 1.0 - jnp.power(jnp.float32(0.9), step_float)
    fix_two = 1.0 - jnp.power(jnp.float32(0.999), step_float)
    update = ADAM_RATE * (moment_new / fix_one) / (jnp.sqrt(second_new / fix_two) + 1e-08)
    return (param - update, moment_new, second_new)


def shards(
    hidden_in,
    cotangent,
    lengths,
    token_order,
    own_map,
    w_query,
    w_key,
    w_value,
    w_out,
    w_up,
    w_down,
    gains,
    biases,
    up_bias,
    vector_moment,
    vector_second,
    bias_moment,
    bias_second,
    step_count,
    stat_left,
    stat_right,
    root_left,
    root_right,
    master,
):
    head_count = lax.axis_size("head")
    seq_size = lax.axis_size("seq")
    head_index = lax.axis_index("head")
    group_index = lax.axis_index("seq")
    tok_count = hidden_in.shape[0]
    width = hidden_in.shape[1]
    panel_width = w_query.shape[1]
    ff_width = w_up.shape[1]
    seq_count = lengths.shape[0]
    seg_all, valid_all = segment_table(token_order, lengths)
    seg_grid = seg_all.reshape(head_count, seq_size, tok_count)
    seg_query = lax.dynamic_index_in_dim(seg_grid, group_index, 1, keepdims=False).reshape(-1)
    own_block = head_index * seq_size + group_index
    valid_here = lax.dynamic_slice_in_dim(valid_all, own_block * tok_count, tok_count, 0)
    inputs_f32 = hidden_in.astype(jnp.float32)

    def gather_weights():
        return (
            lax.all_gather(w_query, "seq", axis=0, tiled=True),
            lax.all_gather(w_key, "seq", axis=0, tiled=True),
            lax.all_gather(w_value, "seq", axis=0, tiled=True),
            lax.all_gather(w_out, "seq", axis=1, tiled=True),
            lax.all_gather(w_up, "seq", axis=0, tiled=True),
            lax.all_gather(w_down, "seq", axis=1, tiled=True),
        )

    def full_weights(q_panel, k_panel, v_panel, o_panel):
        return (
            lax.all_gather(q_panel, "head", axis=1, tiled=True),
            lax.all_gather(k_panel, "head", axis=1, tiled=True),
            lax.all_gather(v_panel, "head", axis=1, tiled=True),
            lax.all_gather(o_panel, "head", axis=0, tiled=True),
        )

    q_panel, k_panel, v_panel, o_panel, up_panel, down_panel = gather_weights()
    q_full, k_full, v_full, o_full = full_weights(q_panel, k_panel, v_panel, o_panel)
    query_tok = (jnp.dot(hidden_in, q_full, preferred_element_type=jnp.float32) + biases[0]).astype(
        jnp.bfloat16
    )
    key_tok = jnp.dot(hidden_in, k_full, preferred_element_type=jnp.float32).astype(jnp.bfloat16)
    value_tok = (jnp.dot(hidden_in, v_full, preferred_element_type=jnp.float32) + biases[1]).astype(
        jnp.bfloat16
    )
    query_grp, key_grp, value_grp = (
        lax.all_to_all(query_tok, "head", split_axis=1, concat_axis=0, tiled=True),
        lax.all_to_all(key_tok, "head", split_axis=1, concat_axis=0, tiled=True),
        lax.all_to_all(value_tok, "head", split_axis=1, concat_axis=0, tiled=True),
    )
    attended, log_total = attend_forward(
        query_grp, key_grp, value_grp, seg_query, seg_grid, group_index, seq_count
    )
    attended_low = attended.astype(jnp.bfloat16)
    attended_tok = lax.all_to_all(attended_low, "head", split_axis=0, concat_axis=1, tiled=True)
    branch_out = jnp.dot(attended_tok, o_full, preferred_element_type=jnp.float32)
    z_one = inputs_f32 + branch_out + biases[2]
    h_one, normed_one, recip_one = normalize(z_one, gains[0], biases[3])
    h_low = h_one.astype(jnp.bfloat16)
    h_grp = group_rows(h_low)
    pre_act = jnp.dot(h_grp, up_panel, preferred_element_type=jnp.float32) + up_bias
    act = jax.nn.gelu(pre_act, approximate=True).astype(jnp.bfloat16)
    ff_out = group_sums(jnp.dot(act, down_panel, preferred_element_type=jnp.float32))
    z_two = h_one + ff_out + biases[4]
    layer_f32, normed_two, recip_two = normalize(z_two, gains[1], biases[5])
    layer_out = layer_f32.astype(jnp.bfloat16)
    grad_y = cotangent.astype(jnp.float32) * valid_here[:, None].astype(jnp.float32)
    dz_two, dgain_two, dshift_two = normalize_back(grad_y, normed_two, recip_two, gains[1])
    dbias_down = jnp.sum(dz_two, axis=0)
    dz_two_grp = group_rows(dz_two.astype(jnp.bfloat16))
    q_panel, k_panel, v_panel, o_panel, up_panel, down_panel = gather_weights()
    dact = jnp.dot(dz_two_grp, down_panel.T, preferred_element_type=jnp.float32)
    grad_down = jnp.dot(act.T, dz_two_grp, preferred_element_type=jnp.float32)
    gelu_value, gelu_pull = jax.vjp(lambda inner: jax.nn.gelu(inner, approximate=True), pre_act)
    dpre = gelu_pull(dact)[0].astype(jnp.bfloat16)
    up_bias_part = jnp.sum(dpre.astype(jnp.float32), axis=0)
    grad_up = jnp.dot(h_grp.T, dpre, preferred_element_type=jnp.float32)
    dh_one = dz_two + group_sums(jnp.dot(dpre, up_panel.T, preferred_element_type=jnp.float32))
    dz_one, dgain_one, dshift_one = normalize_back(dh_one, normed_one, recip_one, gains[0])
    dbias_out = jnp.sum(dz_one, axis=0)
    dz_one_low = dz_one.astype(jnp.bfloat16)
    q_full, k_full, v_full, o_full = full_weights(q_panel, k_panel, v_panel, o_panel)
    dattended_tok = jnp.dot(dz_one_low, o_full.T, preferred_element_type=jnp.float32).astype(
        jnp.bfloat16
    )
    dattended = lax.all_to_all(dattended_tok, "head", split_axis=1, concat_axis=0, tiled=True)
    dquery_grp, dkey_grp, dvalue_grp = attend_backward(
        query_grp,
        key_grp,
        value_grp,
        attended,
        log_total,
        dattended,
        seg_query,
        seg_grid,
        group_index,
        seq_count,
    )
    dquery_tok, dkey_tok, dvalue_tok = (
        lax.all_to_all(dquery_grp, "head", split_axis=0, concat_axis=1, tiled=True),
        lax.all_to_all(dkey_grp, "head", split_axis=0, concat_axis=1, tiled=True),
        lax.all_to_all(dvalue_grp, "head", split_axis=0, concat_axis=1, tiled=True),
    )
    attn_input_grad = (
        jnp.dot(dquery_tok, q_full.T, preferred_element_type=jnp.float32)
        + jnp.dot(dkey_tok, k_full.T, preferred_element_type=jnp.float32)
        + jnp.dot(dvalue_tok, v_full.T, preferred_element_type=jnp.float32)
    )
    inputs_grp = group_rows(hidden_in)
    dz_one_grp = group_rows(dz_one_low)
    grad_out = jnp.dot(attended_low.T, dz_one_grp, preferred_element_type=jnp.float32)
    zero_width = jnp.zeros((width,), jnp.float32)
    dbias_query = lax.dynamic_update_slice_in_dim(
        zero_width, jnp.sum(dquery_grp.astype(jnp.float32), axis=0), head_index * panel_width, 0
    )
    dbias_value = lax.dynamic_update_slice_in_dim(
        zero_width, jnp.sum(dvalue_grp.astype(jnp.float32), axis=0), head_index * panel_width, 0
    )
    grad_query = jnp.dot(inputs_grp.T, dquery_grp, preferred_element_type=jnp.float32)
    grad_key = jnp.dot(inputs_grp.T, dkey_grp, preferred_element_type=jnp.float32)
    grad_value = jnp.dot(inputs_grp.T, dvalue_grp, preferred_element_type=jnp.float32)
    input_grad = dz_one + attn_input_grad
    local_vectors = jnp.stack(
        (
            dbias_query,
            dbias_value,
            dbias_out,
            dshift_one,
            dbias_down,
            dshift_two,
            dgain_one,
            dgain_two,
        )
    )
    up_bias_full = lax.dynamic_update_slice_in_dim(
        jnp.zeros((ff_width * head_count,), jnp.float32), up_bias_part, head_index * ff_width, 0
    )
    vector_grad, up_bias_all = lax.psum((local_vectors, up_bias_full), ("head", "seq"))
    up_bias_grad = lax.dynamic_slice_in_dim(up_bias_all, head_index * ff_width, ff_width, 0)
    canon = jnp.concatenate(
        [
            to_blocks(grad_query),
            to_blocks(grad_key),
            to_blocks(grad_value),
            to_blocks(grad_out),
            to_blocks(grad_up),
            to_blocks(grad_down),
        ],
        axis=0,
    )
    ordered = jnp.take(canon, own_map[0], axis=0)
    block_grads = lax.psum_scatter(
        ordered.astype(jnp.bfloat16), "seq", scatter_dimension=0, tiled=True
    ).astype(jnp.float32)
    stat_left_new = 0.5 * stat_left + 0.5 * jnp.einsum(
        "bij,bkj->bik", block_grads, block_grads, precision=lax.Precision.HIGHEST
    )
    stat_right_new = 0.5 * stat_right + 0.5 * jnp.einsum(
        "bji,bjk->bik", block_grads, block_grads, precision=lax.Precision.HIGHEST
    )
    left_mix = jnp.einsum("bij,bjk->bik", root_left, block_grads, precision=lax.Precision.HIGHEST)
    direction = jnp.einsum("bij,bjk->bik", left_mix, root_right, precision=lax.Precision.HIGHEST)
    master_new = master - SHAMPOO_RATE * direction
    step_float = step_count[0].astype(jnp.float32)
    vector_params = jnp.concatenate([biases, gains], axis=0)
    vector_new, vector_moment_new, vector_second_new = adam_step(
        vector_params, vector_grad, vector_moment, vector_second, step_float
    )
    up_bias_new, bias_moment_new, bias_second_new = adam_step(
        up_bias, up_bias_grad, bias_moment, bias_second, step_float
    )
    return (
        layer_out,
        input_grad,
        block_grads,
        stat_left_new,
        stat_right_new,
        master_new,
        vector_new[0:6],
        vector_new[6:8],
        up_bias_new,
        vector_grad,
        vector_moment_new,
        vector_second_new,
        up_bias_grad,
        bias_moment_new,
        bias_second_new,
    )


def solution(mesh):
    in_specs = (
        P(("head", "seq"), None),
        P(("head", "seq"), None),
        P(),
        P(),
        P("head", None),
        P("seq", "head"),
        P("seq", "head"),
        P("seq", "head"),
        P("head", "seq"),
        P("seq", "head"),
        P("head", "seq"),
        P(),
        P(),
        P("head"),
        P(),
        P(),
        P("head"),
        P("head"),
        P(),
        P(("head", "seq"), None, None),
        P(("head", "seq"), None, None),
        P(("head", "seq"), None, None),
        P(("head", "seq"), None, None),
        P(("head", "seq"), None, None),
    )
    out_specs = (
        P(("head", "seq"), None),
        P(("head", "seq"), None),
        P(("head", "seq"), None, None),
        P(("head", "seq"), None, None),
        P(("head", "seq"), None, None),
        P(("head", "seq"), None, None),
        P(),
        P(),
        P("head"),
        P(),
        P(),
        P(),
        P("head"),
        P("head"),
        P("head"),
    )
    return jax.shard_map(shards, mesh=mesh, in_specs=in_specs, out_specs=out_specs, check_vma=False)
```

profile of v0, /device:TPU:0, one launch (start us, length us, event | category | flops | bytes accessed | tf_op | source)
XLA Modules:
  0.0 2989.0 jit_solution(4188212701486579313)
XLA Ops:
  10.0 31.5 %all-gather.15.cloned.1.call-done = bf16[2048,512]{1,0:T(8,128)(2,1)} async-done(((bf16[256,512]{1,0:T(8,128)(2,1)}), bf16[2048,512]{1,0:T(8,128)(2,1)}) %all-gather.15.cloned.1.call-update) | async-done | bytes 2097168 | tf_op jit(solution)/shard_map/all_gather | solution.py:416
  41.6 30.1 %all-gather.19.cloned.1.call-done = bf16[2048,512]{1,0:T(8,128)(2,1)} async-done(((bf16[256,512]{1,0:T(8,128)(2,1)}), bf16[2048,512]{1,0:T(8,128)(2,1)}) %all-gather.19.cloned.1.call-update) | async-done | bytes 2097168 | tf_op jit(solution)/shard_map/all_gather | solution.py:417
  71.7 30.1 %all-gather.23.cloned.1.call-done = bf16[2048,512]{1,0:T(8,128)(2,1)} async-done(((bf16[256,512]{1,0:T(8,128)(2,1)}), bf16[2048,512]{1,0:T(8,128)(2,1)}) %all-gather.23.cloned.1.call-update) | async-done | bytes 2097168 | tf_op jit(solution)/shard_map/all_gather | solution.py:415
  102.0 31.4 %all-gather.27.cloned.1.call-done = bf16[512,2048]{1,0:T(8,128)(2,1)} async-done(((bf16[512,256]{1,0:T(8,128)(2,1)}), bf16[512,2048]{1,0:T(8,128)(2,1)}) %all-gather.27.cloned.1.call-update) | async-done | bytes 2097168 | tf_op jit(solution)/shard_map/all_gather | solution.py:418
  134.9 86.5 %all-gather.17.cloned.1.call-done = bf16[2048,2048]{1,0:T(8,128)(2,1)} async-done(((bf16[2048,512]{1,0:T(8,128)(2,1)}), bf16[2048,2048]{1,0:T(8,128)(2,1)}) %all-gather.17.cloned.1.call-update) | async-done | bytes 8388624 | tf_op jit(solution)/shard_map/all_gather | solution.py:426
  232.6 88.1 %all-gather.21.cloned.1.call-done = bf16[2048,2048]{1,0:T(8,128)(2,1)} async-done(((bf16[2048,512]{1,0:T(8,128)(2,1)}), bf16[2048,2048]{1,0:T(8,128)(2,1)}) %all-gather.21.cloned.1.call-update) | async-done | bytes 8388624 | tf_op jit(solution)/shard_map/all_gather | solution.py:427
  332.3 87.6 %all-gather.25.cloned.1.call-done = bf16[2048,2048]{1,0:T(8,128)(2,1)} async-done(((bf16[2048,512]{1,0:T(8,128)(2,1)}), bf16[2048,2048]{1,0:T(8,128)(2,1)}) %all-gather.25.cloned.1.call-update) | async-done | bytes 8388624 | tf_op jit(solution)/shard_map/all_gather | solution.py:425
  463.1 37.6 %while.285 = (s32[]{:T(128)}, f32[1024,4]{0,1:T(4,128)S(1)}, f32[1024,4]{0,1:T(4,128)S(1)}, f32[1024,4,128]{2,0,1:T(8,128)}, bf16[1024,4,128]{2,0,1:T(8,128)(2,1...) while((s32[]{:T(128)}, f32[1024,4]{0,1:T(4,128)S(1)}, ...), condition=%wide.region_11.12_spmd, body=%wide.region_4.11_spmd.sunk | while | flops 275910656 | bytes 11339389 | solution.py:148
  501.3 504.7 %while.287 = (s32[]{:T(128)}, f32[1024,4]{0,1:T(4,128)S(1)}, f32[1024,4]{0,1:T(4,128)S(1)}, f32[1024,4,128]{2,0,1:T(8,128)}, bf16[1024,4,128]{2,0,1:T(8,128)(2,1...) while((s32[]{:T(128)}, f32[1024,4]{0,1:T(4,128)S(1)}, ...), condition=%wide.region_22.23_spmd, body=%wide.region_12.22_spmd.sunk | while | flops 275916896 | bytes 23947580 | solution.py:183
  547.1 23.0 collective-permute-start.4
  587.5 33.7 %collective-permute-done.5 = bf16[1024,4,128]{2,0,1:T(8,128)(2,1)S(1)} collective-permute-done((bf16[1024,4,128]{2,0,1:T(8,128)(2,1)}, bf16[1024,4,128]{2,0,1:T(8,128)(2,1)S(1)}, u32[]{:S(2)}, u32[]{:S(2)}) %collective-permute-start.5) | collective-permute-done | bytes 1048608 | tf_op jit(solution)/shard_map/while/body/eval_jaxpr/ppermute | solution.py:21
  621.2 22.1 while.293
  645.2 24.6 collective-permute-start.4
  669.7 21.7 collective-permute-start.5
  693.9 22.0 while.293
  717.9 30.4 %collective-permute-start.4 = (bf16[1024,4,128]{2,0,1:T(8,128)(2,1)}, bf16[1024,4,128]{2,0,1:T(8,128)(2,1)S(1)}, u32[]{:S(2)}, u32[]{:S(2)}) collective-permute-start(bf16[1024,4,128]{2,0,1:T(8,128)(2,1)} %get-tuple-element.4936), channel_id=1, source_target_pairs={{0,1},{1,2},{2,3},{3,4},{4,5},{5,6},{6,7},{7,0},{8,9},{9,10},{10,1... | collective-permute-start | bytes 3145736 | tf_op jit(solution)/shard_map/while/body/eval_jaxpr/ppermute | solution.py:21
  764.5 27.7 while.293
  812.9 47.8 %collective-permute-done.4 = bf16[1024,4,128]{2,0,1:T(8,128)(2,1)S(1)} collective-permute-done((bf16[1024,4,128]{2,0,1:T(8,128)(2,1)}, bf16[1024,4,128]{2,0,1:T(8,128)(2,1)S(1)}, u32[]{:S(2)}, u32[]{:S(2)}) %collective-permute-start.4) | collective-permute-done | bytes 1048608 | tf_op jit(solution)/shard_map/while/body/eval_jaxpr/ppermute | solution.py:21
  872.0 33.3 %while.293 = (s32[]{:T(128)}, f32[1024,4]{0,1:T(4,128)S(1)}, f32[1024,4]{0,1:T(4,128)S(1)}, f32[1024,4,128]{2,0,1:T(8,128)}, bf16[1024,4,128]{2,0,1:T(8,128)(2,1...) while((s32[]{:T(128)}, f32[1024,4]{0,1:T(4,128)S(1)}, ...), condition=%wide.region_21.21_spmd, body=%wide.region_14.20_spmd.sunk | while | flops 275910656 | bytes 11339389 | solution.py:148
  954.1 22.2 collective-permute-done.4
  1039.0 78.9 %all-gather.31.cloned.1.call-done = bf16[1024,2048]{1,0:T(8,128)(2,1)} async-done(((bf16[256,2048]{1,0:T(8,128)(2,1)}), bf16[1024,2048]{1,0:T(8,128)(2,1)}) %all-gather.31.cloned.1.call-update) | async-done | bytes 4194320 | tf_op jit(solution)/shard_map/all_gather | solution.py:80
  1132.5 69.5 %all-gather.35.cloned.1.call-done = bf16[2048,2048]{1,0:T(8,128)(2,1)} async-done(((bf16[2048,256]{1,0:T(8,128)(2,1)}), bf16[2048,2048]{1,0:T(8,128)(2,1)}) %all-gather.35.cloned.1.call-update) | async-done | bytes 8388624 | tf_op jit(solution)/shard_map/all_gather | solution.py:420
  1218.9 50.1 %reduce-scatter.4.cloned.1.call-done = bf16[256,2048]{1,0:T(8,128)(2,1)} async-done(((bf16[1024,2048]{1,0:T(8,128)(2,1)}), bf16[256,2048]{1,0:T(8,128)(2,1)}) %reduce-scatter.4.cloned.1.call-update) | async-done | bytes 1048592 | tf_op jit(solution)/shard_map/reduce_scatter | solution.py:84
  1277.0 52.5 %all-gather.37.cloned.1.call-done = bf16[1024,2048]{1,0:T(8,128)(2,1)} async-done(((bf16[256,2048]{1,0:T(8,128)(2,1)}), bf16[1024,2048]{1,0:T(8,128)(2,1)}) %all-gather.37.cloned.1.call-update) | async-done | bytes 4194320 | tf_op jit(solution)/shard_map/all_gather | solution.py:80
  1366.9 49.4 %reduce-scatter.6.cloned.1.call-done = bf16[256,2048]{1,0:T(8,128)(2,1)} async-done(((bf16[1024,2048]{1,0:T(8,128)(2,1)}), bf16[256,2048]{1,0:T(8,128)(2,1)}) %reduce-scatter.6.cloned.1.call-update) | async-done | bytes 1048592 | tf_op jit(solution)/shard_map/reduce_scatter | solution.py:84
  1473.2 64.3 %while.289 = (s32[]{:T(128)}, f32[1024,4,128]{2,0,1:T(8,128)}, f32[1024,4,128]{0,2,1:T(8,128)}, f32[1024,4,128]{0,2,1:T(8,128)}, bf16[1024,4,128]{2,0,1:T(8,128)...) while((s32[]{:T(128)}, f32[1024,4,128]{2,0,1:T(8,128)}, ...), condition=%wide.region_39.40_spmd, body=%wide.region_34.39_spmd.sunk | while | flops 675807232 | bytes 17884976 | solution.py:283
  1537.5 870.8 %while.291 = (s32[]{:T(128)}, f32[1024,4,128]{2,0,1:T(8,128)}, f32[1024,4,128]{0,2,1:T(8,128)}, f32[1024,4,128]{0,2,1:T(8,128)}, bf16[1024,4,128]{2,0,1:T(8,128)...) while((s32[]{:T(128)}, f32[1024,4,128]{2,0,1:T(8,128)}, ...), condition=%wide.region_48.49_spmd, body=%wide.region_40.0_spmd.sunk | while | flops 677910656 | bytes 51464796 | solution.py:344
  1542.8 43.4 %collective-permute-start.2 = (bf16[1024,4,128]{2,0,1:T(8,128)(2,1)}, bf16[1024,4,128]{2,0,1:T(8,128)(2,1)}, u32[]{:S(2)}, u32[]{:S(2)}) collective-permute-start(bf16[1024,4,128]{2,0,1:T(8,128)(2,1)} %get-tuple-element.5053), channel_id=1, source_target_pairs={{0,1},{1,2},{2,3},{3,4},{4,5},{5,6},{6,7},{7,0},{8,9},{9,10},{10,1... | collective-permute-start | bytes 3145736 | tf_op jit(solution)/shard_map/while/body/eval_jaxpr/ppermute | solution.py:21
  1602.5 28.6 while.295
  1637.4 29.0 collective-permute-start
  1677.6 68.1 %collective-permute-start.3 = (bf16[1024,4,128]{2,0,1:T(8,128)(2,1)}, bf16[1024,4,128]{2,0,1:T(8,128)(2,1)}, u32[]{:S(2)}, u32[]{:S(2)}) collective-permute-start(bf16[1024,4,128]{2,0,1:T(8,128)(2,1)} %get-tuple-element.5054), channel_id=1, source_target_pairs={{0,1},{1,2},{2,3},{3,4},{4,5},{5,6},{6,7},{7,0},{8,9},{9,10},{10,1... | collective-permute-start | bytes 3145736 | tf_op jit(solution)/shard_map/while/body/eval_jaxpr/ppermute | solution.py:21
  1751.0 39.5 %while.295 = (s32[]{:T(128)}, f32[1024,4,128]{2,0,1:T(8,128)}, f32[1024,4,128]{0,2,1:T(8,128)}, f32[1024,4,128]{0,2,1:T(8,128)}, bf16[1024,4,128]{2,0,1:T(8,128)...) while((s32[]{:T(128)}, f32[1024,4,128]{2,0,1:T(8,128)}, ...), condition=%wide.region_47.47_spmd, body=%wide.region_42.46_spmd.sunk | while | flops 675807232 | bytes 17884968 | solution.py:283
  1796.8 29.0 collective-permute-start
  1866.2 39.5 %while.295 = (s32[]{:T(128)}, f32[1024,4,128]{2,0,1:T(8,128)}, f32[1024,4,128]{0,2,1:T(8,128)}, f32[1024,4,128]{0,2,1:T(8,128)}, bf16[1024,4,128]{2,0,1:T(8,128)...) while((s32[]{:T(128)}, f32[1024,4,128]{2,0,1:T(8,128)}, ...), condition=%wide.region_47.47_spmd, body=%wide.region_42.46_spmd.sunk | while | flops 675807232 | bytes 17884968 | solution.py:283
  1924.5 44.1 %collective-permute-start.2 = (bf16[1024,4,128]{2,0,1:T(8,128)(2,1)}, bf16[1024,4,128]{2,0,1:T(8,128)(2,1)}, u32[]{:S(2)}, u32[]{:S(2)}) collective-permute-start(bf16[1024,4,128]{2,0,1:T(8,128)(2,1)} %get-tuple-element.5053), channel_id=1, source_target_pairs={{0,1},{1,2},{2,3},{3,4},{4,5},{5,6},{6,7},{7,0},{8,9},{9,10},{10,1... | collective-permute-start | bytes 3145736 | tf_op jit(solution)/shard_map/while/body/eval_jaxpr/ppermute | solution.py:21
  1984.9 50.4 %while.295 = (s32[]{:T(128)}, f32[1024,4,128]{2,0,1:T(8,128)}, f32[1024,4,128]{0,2,1:T(8,128)}, f32[1024,4,128]{0,2,1:T(8,128)}, bf16[1024,4,128]{2,0,1:T(8,128)...) while((s32[]{:T(128)}, f32[1024,4,128]{2,0,1:T(8,128)}, ...), condition=%wide.region_47.47_spmd, body=%wide.region_42.46_spmd.sunk | while | flops 675807232 | bytes 17884968 | solution.py:283
  2050.5 26.7 collective-permute-start.1
  2095.2 24.3 collective-permute-start.3
  2142.2 61.3 %while.295 = (s32[]{:T(128)}, f32[1024,4,128]{2,0,1:T(8,128)}, f32[1024,4,128]{0,2,1:T(8,128)}, f32[1024,4,128]{0,2,1:T(8,128)}, bf16[1024,4,128]{2,0,1:T(8,128)...) while((s32[]{:T(128)}, f32[1024,4,128]{2,0,1:T(8,128)}, ...), condition=%wide.region_47.47_spmd, body=%wide.region_42.46_spmd.sunk | while | flops 675807232 | bytes 17884968 | solution.py:283
  2211.7 21.1 collective-permute-start.2
  2259.7 28.6 while.295
  2294.6 40.3 %collective-permute-start = (bf16[1024,4,128]{0,2,1:T(8,128)(2,1)S(1)}, bf16[1024,4,128]{0,2,1:T(8,128)(2,1)S(1)}, u32[]{:S(2)}, u32[]{:S(2)}) collective-permute-start(bf16[1024,4,128]{0,2,1:T(8,128)(2,1)S(1)} %convert_element_type.381), channel_id=1, source_target_pairs={{0,1},{1,2},{2,3},{3,4},{4,5},{5,6},{6,7},{7,0},{8,9},{9,10},{10,1... | collective-permute-start | bytes 3145736 | tf_op jit(solution)/shard_map/while/body/eval_jaxpr/ppermute | solution.py:21
  2375.2 28.6 while.295
  2473.5 35.5 %collective-permute-start.7 = (bf16[1024,4,128]{0,2,1:T(8,128)(2,1)}, bf16[1024,4,128]{0,2,1:T(8,128)(2,1)}, u32[]{:S(2)}, u32[]{:S(2)}) collective-permute-start(bf16[1024,4,128]{0,2,1:T(8,128)(2,1)} %convert_element_type.284), channel_id=1, source_target_pairs={{0,1},{1,2},{2,3},{3,4},{4,5},{5,6},{6,7},{7,0},{8,9},{9,10},{10,1... | collective-permute-start | bytes 3145736 | tf_op jit(solution)/shard_map/ppermute | solution.py:21
  2576.2 19.8 gather_fusion
  2596.0 22.5 select_convert_fusion
  2638.7 78.3 %psum.15 = f32[8192]{0:T(1024)S(1)} all-reduce(f32[8192]{0:T(1024)S(1)} %dynamic_update_slice.49), channel_id=1, replica_groups=mesh['head'=4,'seq'=8] {'head','seq'}, use_global_device_ids=true, to_apply=%region_60.61 | all-reduce | flops 8192 | bytes 65536 | tf_op jit(solution)/shard_map/psum | solution.py:532
  2754.0 195.4 %reduce-scatter.8.cloned.1.call-done = bf16[24,256,256]{2,1,0:T(8,128)(2,1)} async-done(((bf16[192,256,256]{2,1,0:T(8,128)(2,1)}), bf16[24,256,256]{2,1,0:T(8,128)(2,1)}) %reduce-scatter.8.cloned.1.call-update) | async-done | bytes 3145744 | tf_op jit(solution)/shard_map/reduce_scatter | solution.py:546
  (1259 shorter events, 2129.9 us)
Async XLA Ops:
  7.2 34.3 %all-gather.15.cloned.1.call-start = ((), (), s32[]{:S(2)}) async-start(), calls=%async_computation.11 | async-start | bytes 2359296 | tf_op jit(solution)/shard_map/all_gather | solution.py:416
  7.9 63.8 %all-gather.19.cloned.1.call-start = ((), (), s32[]{:S(2)}) async-start(), calls=%async_computation.13 | async-start | bytes 2359296 | tf_op jit(solution)/shard_map/all_gather | solution.py:417
  8.7 93.2 %all-gather.23.cloned.1.call-start = ((), (), s32[]{:S(2)}) async-start(), calls=%async_computation.15 | async-start | bytes 2359296 | tf_op jit(solution)/shard_map/all_gather | solution.py:415
  9.4 123.9 %all-gather.27.cloned.1.call-start = ((), (), s32[]{:S(2)}) async-start(), calls=%async_computation.17 | async-start | bytes 2359296 | tf_op jit(solution)/shard_map/all_gather | solution.py:418
  10.0 211.4 %all-gather.17.cloned.1.call-start = ((), (), s32[]{:S(2)}) async-start(), calls=%async_computation.12 | async-start | bytes 10485760 | tf_op jit(solution)/shard_map/all_gather | solution.py:426
  41.5 279.1 %all-gather.21.cloned.1.call-start = ((), (), s32[]{:S(2)}) async-start(), calls=%async_computation.14 | async-start | bytes 10485760 | tf_op jit(solution)/shard_map/all_gather | solution.py:427
  71.7 348.2 %all-gather.25.cloned.1.call-start = ((), (), s32[]{:S(2)}) async-start(), calls=%async_computation.16 | async-start | bytes 10485760 | tf_op jit(solution)/shard_map/all_gather | solution.py:425
  101.9 927.7 %all-gather.29.cloned.1.call-start = ((), (), s32[]{:S(2)}) async-start(), calls=%async_computation.18 | async-start | bytes 10485760 | tf_op jit(solution)/shard_map/all_gather | solution.py:428
  133.4 905.7 %all-gather.33.cloned.1.call-start = ((), (), s32[]{:S(2)}) async-start(), calls=%async_computation.20 | async-start | bytes 9437184 | tf_op jit(solution)/shard_map/all_gather | solution.py:419
  228.2 99.3 %all-to-all-start = ((bf16[256,4,512]{2,0,1:T(8,128)(2,1)}), bf16[256,4,512]{2,0,1:T(8,128)(2,1)S(1)}, u32[]{:S(2)}, u32[]{:S(2)}) async-start(bf16[256,4,512]{2,0,1:T(8,128)(2,1)} %bitcast.302), calls=%async_computation | async-start | bytes 2097152 | tf_op jit(solution)/shard_map/all_to_all | solution.py:442
  327.5 99.3 %all-to-all-start.1 = ((bf16[256,4,512]{2,0,1:T(8,128)(2,1)}), bf16[256,4,512]{2,0,1:T(8,128)(2,1)S(1)}, u32[]{:S(2)}, u32[]{:S(2)}) async-start(bf16[256,4,512]{2,0,1:T(8,128)(2,1)} %bitcast.301), calls=%async_computation.1 | async-start | bytes 2097152 | tf_op jit(solution)/shard_map/all_to_all | solution.py:443
  547.1 40.3 %collective-permute-start.4 = (bf16[1024,4,128]{2,0,1:T(8,128)(2,1)}, bf16[1024,4,128]{2,0,1:T(8,128)(2,1)S(1)}, u32[]{:S(2)}, u32[]{:S(2)}) collective-permute-start(bf16[1024,4,128]{2,0,1:T(8,128)(2,1)} %get-tuple-element.4936), channel_id=1, source_target_pairs={{0,1},{1,2},{2,3},{3,4},{4,5},{5,6},{6,7},{7,0},{8,9},{9,10},{10,1... | collective-permute-start | bytes 3145736 | tf_op jit(solution)/shard_map/while/body/eval_jaxpr/ppermute | solution.py:21
  570.2 51.0 %collective-permute-start.5 = (bf16[1024,4,128]{2,0,1:T(8,128)(2,1)}, bf16[1024,4,128]{2,0,1:T(8,128)(2,1)S(1)}, u32[]{:S(2)}, u32[]{:S(2)}) collective-permute-start(bf16[1024,4,128]{2,0,1:T(8,128)(2,1)} %get-tuple-element.4937), channel_id=1, source_target_pairs={{0,1},{1,2},{2,3},{3,4},{4,5},{5,6},{6,7},{7,0},{8,9},{9,10},{10,1... | collective-permute-start | bytes 3145736 | tf_op jit(solution)/shard_map/while/body/eval_jaxpr/ppermute | solution.py:21
  645.2 46.5 %collective-permute-start.4 = (bf16[1024,4,128]{2,0,1:T(8,128)(2,1)}, bf16[1024,4,128]{2,0,1:T(8,128)(2,1)S(1)}, u32[]{:S(2)}, u32[]{:S(2)}) collective-permute-start(bf16[1024,4,128]{2,0,1:T(8,128)(2,1)} %get-tuple-element.4936), channel_id=1, source_target_pairs={{0,1},{1,2},{2,3},{3,4},{4,5},{5,6},{6,7},{7,0},{8,9},{9,10},{10,1... | collective-permute-start | bytes 3145736 | tf_op jit(solution)/shard_map/while/body/eval_jaxpr/ppermute | solution.py:21
  717.9 32.9 %collective-permute-start.4 = (bf16[1024,4,128]{2,0,1:T(8,128)(2,1)}, bf16[1024,4,128]{2,0,1:T(8,128)(2,1)S(1)}, u32[]{:S(2)}, u32[]{:S(2)}) collective-permute-start(bf16[1024,4,128]{2,0,1:T(8,128)(2,1)} %get-tuple-element.4936), channel_id=1, source_target_pairs={{0,1},{1,2},{2,3},{3,4},{4,5},{5,6},{6,7},{7,0},{8,9},{9,10},{10,1... | collective-permute-start | bytes 3145736 | tf_op jit(solution)/shard_map/while/body/eval_jaxpr/ppermute | solution.py:21
  794.1 66.6 %collective-permute-start.4 = (bf16[1024,4,128]{2,0,1:T(8,128)(2,1)}, bf16[1024,4,128]{2,0,1:T(8,128)(2,1)S(1)}, u32[]{:S(2)}, u32[]{:S(2)}) collective-permute-start(bf16[1024,4,128]{2,0,1:T(8,128)(2,1)} %get-tuple-element.4936), channel_id=1, source_target_pairs={{0,1},{1,2},{2,3},{3,4},{4,5},{5,6},{6,7},{7,0},{8,9},{9,10},{10,1... | collective-permute-start | bytes 3145736 | tf_op jit(solution)/shard_map/while/body/eval_jaxpr/ppermute | solution.py:21
  810.3 61.6 %collective-permute-start.5 = (bf16[1024,4,128]{2,0,1:T(8,128)(2,1)}, bf16[1024,4,128]{2,0,1:T(8,128)(2,1)S(1)}, u32[]{:S(2)}, u32[]{:S(2)}) collective-permute-start(bf16[1024,4,128]{2,0,1:T(8,128)(2,1)} %get-tuple-element.4937), channel_id=1, source_target_pairs={{0,1},{1,2},{2,3},{3,4},{4,5},{5,6},{6,7},{7,0},{8,9},{9,10},{10,1... | collective-permute-start | bytes 3145736 | tf_op jit(solution)/shard_map/while/body/eval_jaxpr/ppermute | solution.py:21
  953.8 33.7 %collective-permute-start.5 = (bf16[1024,4,128]{2,0,1:T(8,128)(2,1)}, bf16[1024,4,128]{2,0,1:T(8,128)(2,1)S(1)}, u32[]{:S(2)}, u32[]{:S(2)}) collective-permute-start(bf16[1024,4,128]{2,0,1:T(8,128)(2,1)} %get-tuple-element.4937), channel_id=1, source_target_pairs={{0,1},{1,2},{2,3},{3,4},{4,5},{5,6},{6,7},{7,0},{8,9},{9,10},{10,1... | collective-permute-start | bytes 3145736 | tf_op jit(solution)/shard_map/while/body/eval_jaxpr/ppermute | solution.py:21
  1018.9 99.0 %all-gather.31.cloned.1.call-start = ((), (), s32[]{:S(2)}) async-start(), calls=%async_computation.19 | async-start | bytes 5242880 | tf_op jit(solution)/shard_map/all_gather | solution.py:80
  1038.2 163.8 %all-gather.35.cloned.1.call-start = ((), (), s32[]{:S(2)}) async-start(), calls=%async_computation.21 | async-start | bytes 9437184 | tf_op jit(solution)/shard_map/all_gather | solution.py:420
  1039.0 230.0 %reduce-scatter.4.cloned.1.call-start = ((), (), s32[]{:S(2)}) async-start(), calls=%async_computation.22 | async-start | bytes 5242880 | tf_op jit(solution)/shard_map/reduce_scatter | solution.py:84
  1218.0 111.5 %all-gather.37.cloned.1.call-start = ((), (), s32[]{:S(2)}) async-start(), calls=%async_computation.23 | async-start | bytes 5242880 | tf_op jit(solution)/shard_map/all_gather | solution.py:80
  1276.8 139.6 %reduce-scatter.6.cloned.1.call-start = ((), (), s32[]{:S(2)}) async-start(), calls=%async_computation.24 | async-start | bytes 5242880 | tf_op jit(solution)/shard_map/reduce_scatter | solution.py:84
  1363.5 1145.5 %all-gather.39.cloned.1.call-start = ((), (), s32[]{:S(2)}) async-start(), calls=%async_computation.25 | async-start | bytes 5242880 | tf_op jit(solution)/shard_map/all_gather | solution.py:80
  1434.6 1113.6 %all-gather.41.cloned.1.call-start = ((), (), s32[]{:S(2)}) async-start(), calls=%async_computation.26 | async-start | bytes 5242880 | tf_op jit(solution)/shard_map/all_gather | solution.py:80
  1450.6 1282.3 %all-reduce.2.cloned.1.call-start = ((), (), s32[]{:S(2)}) async-start(), calls=%async_computation.28 | async-start | bytes 131072 | tf_op jit(solution)/shard_map/psum | solution.py:532
  1539.3 47.9 %collective-permute-start = (bf16[1024,4,128]{0,2,1:T(8,128)(2,1)S(1)}, bf16[1024,4,128]{0,2,1:T(8,128)(2,1)S(1)}, u32[]{:S(2)}, u32[]{:S(2)}) collective-permute-start(bf16[1024,4,128]{0,2,1:T(8,128)(2,1)S(1)} %convert_element_type.381), channel_id=1, source_target_pairs={{0,1},{1,2},{2,3},{3,4},{4,5},{5,6},{6,7},{7,0},{8,9},{9,10},{10,1... | collective-permute-start | bytes 3145736 | tf_op jit(solution)/shard_map/while/body/eval_jaxpr/ppermute | solution.py:21
  1541.1 47.7 %collective-permute-start.1 = (bf16[1024,4,128]{0,2,1:T(8,128)(2,1)S(1)}, bf16[1024,4,128]{0,2,1:T(8,128)(2,1)}, u32[]{:S(2)}, u32[]{:S(2)}) collective-permute-start(bf16[1024,4,128]{0,2,1:T(8,128)(2,1)S(1)} %convert_element_type.383), channel_id=1, source_target_pairs={{0,1},{1,2},{2,3},{3,4},{4,5},{5,6},{6,7},{7,0},{8,9},{9,10},{10,1... | collective-permute-start | bytes 3145736 | tf_op jit(solution)/shard_map/while/body/eval_jaxpr/ppermute | solution.py:21
  1542.8 48.8 %collective-permute-start.2 = (bf16[1024,4,128]{2,0,1:T(8,128)(2,1)}, bf16[1024,4,128]{2,0,1:T(8,128)(2,1)}, u32[]{:S(2)}, u32[]{:S(2)}) collective-permute-start(bf16[1024,4,128]{2,0,1:T(8,128)(2,1)} %get-tuple-element.5053), channel_id=1, source_target_pairs={{0,1},{1,2},{2,3},{3,4},{4,5},{5,6},{6,7},{7,0},{8,9},{9,10},{10,1... | collective-permute-start | bytes 3145736 | tf_op jit(solution)/shard_map/while/body/eval_jaxpr/ppermute | solution.py:21
  1637.4 109.2 %collective-permute-start = (bf16[1024,4,128]{0,2,1:T(8,128)(2,1)S(1)}, bf16[1024,4,128]{0,2,1:T(8,128)(2,1)S(1)}, u32[]{:S(2)}, u32[]{:S(2)}) collective-permute-start(bf16[1024,4,128]{0,2,1:T(8,128)(2,1)S(1)} %convert_element_type.381), channel_id=1, source_target_pairs={{0,1},{1,2},{2,3},{3,4},{4,5},{5,6},{6,7},{7,0},{8,9},{9,10},{10,1... | collective-permute-start | bytes 3145736 | tf_op jit(solution)/shard_map/while/body/eval_jaxpr/ppermute | solution.py:21
  1668.1 80.1 %collective-permute-start.1 = (bf16[1024,4,128]{0,2,1:T(8,128)(2,1)S(1)}, bf16[1024,4,128]{0,2,1:T(8,128)(2,1)}, u32[]{:S(2)}, u32[]{:S(2)}) collective-permute-start(bf16[1024,4,128]{0,2,1:T(8,128)(2,1)S(1)} %convert_element_type.383), channel_id=1, source_target_pairs={{0,1},{1,2},{2,3},{3,4},{4,5},{5,6},{6,7},{7,0},{8,9},{9,10},{10,1... | collective-permute-start | bytes 3145736 | tf_op jit(solution)/shard_map/while/body/eval_jaxpr/ppermute | solution.py:21
  1668.2 82.8 %collective-permute-start.2 = (bf16[1024,4,128]{2,0,1:T(8,128)(2,1)}, bf16[1024,4,128]{2,0,1:T(8,128)(2,1)}, u32[]{:S(2)}, u32[]{:S(2)}) collective-permute-start(bf16[1024,4,128]{2,0,1:T(8,128)(2,1)} %get-tuple-element.5053), channel_id=1, source_target_pairs={{0,1},{1,2},{2,3},{3,4},{4,5},{5,6},{6,7},{7,0},{8,9},{9,10},{10,1... | collective-permute-start | bytes 3145736 | tf_op jit(solution)/shard_map/while/body/eval_jaxpr/ppermute | solution.py:21
  1677.6 73.4 %collective-permute-start.3 = (bf16[1024,4,128]{2,0,1:T(8,128)(2,1)}, bf16[1024,4,128]{2,0,1:T(8,128)(2,1)}, u32[]{:S(2)}, u32[]{:S(2)}) collective-permute-start(bf16[1024,4,128]{2,0,1:T(8,128)(2,1)} %get-tuple-element.5054), channel_id=1, source_target_pairs={{0,1},{1,2},{2,3},{3,4},{4,5},{5,6},{6,7},{7,0},{8,9},{9,10},{10,1... | collective-permute-start | bytes 3145736 | tf_op jit(solution)/shard_map/while/body/eval_jaxpr/ppermute | solution.py:21
  1796.8 43.7 %collective-permute-start = (bf16[1024,4,128]{0,2,1:T(8,128)(2,1)S(1)}, bf16[1024,4,128]{0,2,1:T(8,128)(2,1)S(1)}, u32[]{:S(2)}, u32[]{:S(2)}) collective-permute-start(bf16[1024,4,128]{0,2,1:T(8,128)(2,1)S(1)} %convert_element_type.381), channel_id=1, source_target_pairs={{0,1},{1,2},{2,3},{3,4},{4,5},{5,6},{6,7},{7,0},{8,9},{9,10},{10,1... | collective-permute-start | bytes 3145736 | tf_op jit(solution)/shard_map/while/body/eval_jaxpr/ppermute | solution.py:21
  1912.0 57.6 %collective-permute-start = (bf16[1024,4,128]{0,2,1:T(8,128)(2,1)S(1)}, bf16[1024,4,128]{0,2,1:T(8,128)(2,1)S(1)}, u32[]{:S(2)}, u32[]{:S(2)}) collective-permute-start(bf16[1024,4,128]{0,2,1:T(8,128)(2,1)S(1)} %convert_element_type.381), channel_id=1, source_target_pairs={{0,1},{1,2},{2,3},{3,4},{4,5},{5,6},{6,7},{7,0},{8,9},{9,10},{10,1... | collective-permute-start | bytes 3145736 | tf_op jit(solution)/shard_map/while/body/eval_jaxpr/ppermute | solution.py:21
  1924.4 46.7 %collective-permute-start.1 = (bf16[1024,4,128]{0,2,1:T(8,128)(2,1)S(1)}, bf16[1024,4,128]{0,2,1:T(8,128)(2,1)}, u32[]{:S(2)}, u32[]{:S(2)}) collective-permute-start(bf16[1024,4,128]{0,2,1:T(8,128)(2,1)S(1)} %convert_element_type.383), channel_id=1, source_target_pairs={{0,1},{1,2},{2,3},{3,4},{4,5},{5,6},{6,7},{7,0},{8,9},{9,10},{10,1... | collective-permute-start | bytes 3145736 | tf_op jit(solution)/shard_map/while/body/eval_jaxpr/ppermute | solution.py:21
  1924.5 49.5 %collective-permute-start.2 = (bf16[1024,4,128]{2,0,1:T(8,128)(2,1)}, bf16[1024,4,128]{2,0,1:T(8,128)(2,1)}, u32[]{:S(2)}, u32[]{:S(2)}) collective-permute-start(bf16[1024,4,128]{2,0,1:T(8,128)(2,1)} %get-tuple-element.5053), channel_id=1, source_target_pairs={{0,1},{1,2},{2,3},{3,4},{4,5},{5,6},{6,7},{7,0},{8,9},{9,10},{10,1... | collective-permute-start | bytes 3145736 | tf_op jit(solution)/shard_map/while/body/eval_jaxpr/ppermute | solution.py:21
  2041.6 78.8 %collective-permute-start = (bf16[1024,4,128]{0,2,1:T(8,128)(2,1)S(1)}, bf16[1024,4,128]{0,2,1:T(8,128)(2,1)S(1)}, u32[]{:S(2)}, u32[]{:S(2)}) collective-permute-start(bf16[1024,4,128]{0,2,1:T(8,128)(2,1)S(1)} %convert_element_type.381), channel_id=1, source_target_pairs={{0,1},{1,2},{2,3},{3,4},{4,5},{5,6},{6,7},{7,0},{8,9},{9,10},{10,1... | collective-permute-start | bytes 3145736 | tf_op jit(solution)/shard_map/while/body/eval_jaxpr/ppermute | solution.py:21
  2050.5 71.5 %collective-permute-start.1 = (bf16[1024,4,128]{0,2,1:T(8,128)(2,1)S(1)}, bf16[1024,4,128]{0,2,1:T(8,128)(2,1)}, u32[]{:S(2)}, u32[]{:S(2)}) collective-permute-start(bf16[1024,4,128]{0,2,1:T(8,128)(2,1)S(1)} %convert_element_type.383), channel_id=1, source_target_pairs={{0,1},{1,2},{2,3},{3,4},{4,5},{5,6},{6,7},{7,0},{8,9},{9,10},{10,1... | collective-permute-start | bytes 3145736 | tf_op jit(solution)/shard_map/while/body/eval_jaxpr/ppermute | solution.py:21
  2077.2 53.8 %collective-permute-start.2 = (bf16[1024,4,128]{2,0,1:T(8,128)(2,1)}, bf16[1024,4,128]{2,0,1:T(8,128)(2,1)}, u32[]{:S(2)}, u32[]{:S(2)}) collective-permute-start(bf16[1024,4,128]{2,0,1:T(8,128)(2,1)} %get-tuple-element.5053), channel_id=1, source_target_pairs={{0,1},{1,2},{2,3},{3,4},{4,5},{5,6},{6,7},{7,0},{8,9},{9,10},{10,1... | collective-permute-start | bytes 3145736 | tf_op jit(solution)/shard_map/while/body/eval_jaxpr/ppermute | solution.py:21
  2095.2 47.0 %collective-permute-start.3 = (bf16[1024,4,128]{2,0,1:T(8,128)(2,1)}, bf16[1024,4,128]{2,0,1:T(8,128)(2,1)}, u32[]{:S(2)}, u32[]{:S(2)}) collective-permute-start(bf16[1024,4,128]{2,0,1:T(8,128)(2,1)} %get-tuple-element.5054), channel_id=1, source_target_pairs={{0,1},{1,2},{2,3},{3,4},{4,5},{5,6},{6,7},{7,0},{8,9},{9,10},{10,1... | collective-permute-start | bytes 3145736 | tf_op jit(solution)/shard_map/while/body/eval_jaxpr/ppermute | solution.py:21
  2211.7 36.8 %collective-permute-start.2 = (bf16[1024,4,128]{2,0,1:T(8,128)(2,1)}, bf16[1024,4,128]{2,0,1:T(8,128)(2,1)}, u32[]{:S(2)}, u32[]{:S(2)}) collective-permute-start(bf16[1024,4,128]{2,0,1:T(8,128)(2,1)} %get-tuple-element.5053), channel_id=1, source_target_pairs={{0,1},{1,2},{2,3},{3,4},{4,5},{5,6},{6,7},{7,0},{8,9},{9,10},{10,1... | collective-permute-start | bytes 3145736 | tf_op jit(solution)/shard_map/while/body/eval_jaxpr/ppermute | solution.py:21
  2294.6 54.9 %collective-permute-start = (bf16[1024,4,128]{0,2,1:T(8,128)(2,1)S(1)}, bf16[1024,4,128]{0,2,1:T(8,128)(2,1)S(1)}, u32[]{:S(2)}, u32[]{:S(2)}) collective-permute-start(bf16[1024,4,128]{0,2,1:T(8,128)(2,1)S(1)} %convert_element_type.381), channel_id=1, source_target_pairs={{0,1},{1,2},{2,3},{3,4},{4,5},{5,6},{6,7},{7,0},{8,9},{9,10},{10,1... | collective-permute-start | bytes 3145736 | tf_op jit(solution)/shard_map/while/body/eval_jaxpr/ppermute | solution.py:21
  2346.0 29.2 collective-permute-start.3
  2411.0 109.2 %collective-permute-start.6 = (bf16[1024,4,128]{0,2,1:T(8,128)(2,1)}, bf16[1024,4,128]{0,2,1:T(8,128)(2,1)}, u32[]{:S(2)}, u32[]{:S(2)}) collective-permute-start(bf16[1024,4,128]{0,2,1:T(8,128)(2,1)} %convert_element_type.282), channel_id=1, source_target_pairs={{0,1},{1,2},{2,3},{3,4},{4,5},{5,6},{6,7},{7,0},{8,9},{9,10},{10,1... | collective-permute-start | bytes 3145736 | tf_op jit(solution)/shard_map/ppermute | solution.py:21
  2473.5 56.8 %collective-permute-start.7 = (bf16[1024,4,128]{0,2,1:T(8,128)(2,1)}, bf16[1024,4,128]{0,2,1:T(8,128)(2,1)}, u32[]{:S(2)}, u32[]{:S(2)}) collective-permute-start(bf16[1024,4,128]{0,2,1:T(8,128)(2,1)} %convert_element_type.284), channel_id=1, source_target_pairs={{0,1},{1,2},{2,3},{3,4},{4,5},{5,6},{6,7},{7,0},{8,9},{9,10},{10,1... | collective-permute-start | bytes 3145736 | tf_op jit(solution)/shard_map/ppermute | solution.py:21
  2547.7 401.7 %reduce-scatter.8.cloned.1.call-start = ((), (), s32[]{:S(2)}) async-start(), calls=%async_computation.27 | async-start | bytes 28311552 | tf_op jit(solution)/shard_map/reduce_scatter | solution.py:546
  2634.1 87.7 %all-to-all-start.6 = ((bf16[4,256,512]{2,1,0:T(8,128)(2,1)}), bf16[4,256,512]{2,1,0:T(8,128)(2,1)S(1)}, u32[]{:S(2)}, u32[]{:S(2)}) async-start(bf16[4,256,512]{2,1,0:T(8,128)(2,1)} %copy.292), calls=%async_computation.8 | async-start | bytes 2097152 | tf_op jit(solution)/shard_map/all_to_all | solution.py:495
  (73 other events, 1458.0 us)
Sparse Core Ops, SparseCore 0:
  9.6 31.8 all-gather.14
  43.1 28.5 all-gather.18
  73.3 28.5 all-gather.22
  103.3 29.9 all-gather.26
  135.0 86.3 all-gather.16
  223.1 97.5 all-gather.20
  322.5 97.3 all-gather.24
  421.8 97.7 all-gather.28
  521.2 104.1 all-gather.32
  1038.3 79.5 all-gather.30
  1119.5 82.4 all-gather.34
  1218.2 50.7 reduce-scatter.3
  1276.9 52.5 all-gather.36
  1363.7 52.6 reduce-scatter.5
  1418.0 60.7 all-gather.38
  1480.5 52.6 all-gather.40
  2547.8 150.8 all-reduce.1
  2701.0 248.3 reduce-scatter.7
where the time goes:
time: 2980 us; the launch traced here: 2990 us
  waiting for transfers between devices  1240 us (42%)
  starting transfers between devices  590 us (20%)
  matrix products  471 us (16%)
  local copies, waits for them, and re-layouts  355 us (12%)
  other arithmetic  148 us (5%)
  loops' own time  88.7 us (3%)
  blocking collectives  78.3 us (3%)
    ppermute x44, starting transfers between devices, shifted(): lax.ppermute(array, axis, [(i, (i + by) % length) for i in range(length)])  559 us
    ppermute x44, waiting for transfers between devices, shifted(): lax.ppermute(array, axis, [(i, (i + by) % length) for i in range(length)])  318 us
    reduce_scatter x1, waiting for transfers between devices, shards(): lax.psum_scatter(ordered.astype(jnp.bfloat16), 'seq', scatter_dimension=0...  195 us
    all_gather x4, waiting for transfers between devices, group_rows(): return lax.all_gather(rows_low, 'head', axis=0, tiled=True)  131 us
    reduce_scatter x2, waiting for transfers between devices, group_sums(): lax.psum_scatter(partial_value.astype(jnp.bfloat16), 'head', scatter_dime...  99.5 us
    all_gather x1, waiting for transfers between devices, full_weights(): lax.all_gather(v_panel, 'head', axis=1, tiled=True)  88.1 us
    all_gather x1, waiting for transfers between devices, full_weights(): lax.all_gather(q_panel, 'head', axis=1, tiled=True)  87.6 us
    all_gather x1, waiting for transfers between devices, full_weights(): lax.all_gather(k_panel, 'head', axis=1, tiled=True)  86.5 us
  transfers between devices with their start and end apart: 70, of which 44 were waited for; matrix products, arithmetic and copies ran while one was open for 29% of the time, Pallas kernels for 0%

commit v1 on v0

v1 whole, which is shorter than its diff:
```python
import functools
import math

import jax
import jax.numpy as jnp
from jax import lax
from jax.experimental import pallas as pl
from jax.experimental.pallas import tpu as pltpu
from jax.sharding import PartitionSpec as P

HDIM = 128
BLOCK = 256
RUN = 256

NEG_LARGE = -1e30
NORM_EPS = 1e-12
ADAM_RATE = 0.4
SHAMPOO_RATE = 0.15
MESH = pl.DeviceIdType.MESH
VMEM_MOST = 60 * 1024 * 1024

ANY = pl.BlockSpec(memory_space=pl.ANY)
IN_SMEM = pl.BlockSpec(memory_space=pltpu.SMEM)
IN_VMEM = pl.BlockSpec(memory_space=pltpu.VMEM)


def seq_barrier(me, heads, parts):
    own_head, own_part = me // parts, me % parts
    barrier = pltpu.get_barrier_semaphore()
    for step in range(1, heads):
        pl.semaphore_signal(
            barrier,
            inc=1,
            device_id={"seq": (own_head + step) % heads * parts + own_part},
            device_id_type=MESH,
        )
    for step in range(1, parts):
        pl.semaphore_signal(
            barrier,
            inc=1,
            device_id={"seq": own_head * parts + (own_part + step) % parts},
            device_id_type=MESH,
        )
    pl.semaphore_wait(barrier, heads - 1 + parts - 1)


def spread_kernel(
    fields, heads, parts, x_ref, y_ref, own_sem, send_sem, recv_sem, pass_sem, take_sem
):
    me = lax.axis_index("seq")
    own_head, own_part = me // parts, me % parts
    seq_barrier(me, heads, parts)

    def columns(field, head):
        return pl.ds(pl.multiple_of((field * heads + head) * HDIM, HDIM), HDIM)

    sends = []
    for step in range(1, heads):
        head = (own_head + step) % heads
        for field in range(fields):
            copy = pltpu.make_async_remote_copy(
                src_ref=x_ref.at[:, columns(field, head)],
                dst_ref=y_ref.at[field, me],
                send_sem=send_sem.at[step - 1, field],
                recv_sem=recv_sem.at[step - 1, field],
                device_id={"seq": head * parts + own_part},
                device_id_type=MESH,
            )
            copy.start()
            sends.append(copy)
    owns = []
    for field in range(fields):
        copy = pltpu.make_async_copy(
            x_ref.at[:, columns(field, own_head)], y_ref.at[field, me], own_sem.at[field]
        )
        copy.start()
        owns.append(copy)
    passes = []

    def pass_on(step, field, source):
        origin = (own_head - step + heads) % heads * parts + own_part
        for other in range(1, parts):
            copy = pltpu.make_async_remote_copy(
                src_ref=source,
                dst_ref=y_ref.at[field, origin],
                send_sem=pass_sem.at[other - 1, step, field],
                recv_sem=take_sem.at[other - 1, step, field],
                device_id={"seq": own_head * parts + (own_part + other) % parts},
                device_id_type=MESH,
            )
            copy.start()
            passes.append(copy)

    for field in range(fields):
        pass_on(0, field, x_ref.at[:, columns(field, own_head)])
    for step in range(1, heads):
        origin = (own_head - step + heads) % heads * parts + own_part
        for field in range(fields):
            sends[(step - 1) * fields + field].wait_recv()
            pass_on(step, field, y_ref.at[field, origin])
    for copy in owns:
        copy.wait()
    for copy in sends:
        copy.wait_send()
    for copy in passes:
        copy.wait()


def spread(x_rows, fields, heads, parts, seq_size, collective_id):
    rows = x_rows.shape[0]
    return pl.pallas_call(
        functools.partial(spread_kernel, fields, heads, parts),
        out_shape=jax.ShapeDtypeStruct((fields, seq_size, rows, HDIM), x_rows.dtype),
        in_specs=[IN_VMEM],
        out_specs=ANY,
        scratch_shapes=[
            pltpu.SemaphoreType.DMA((fields,)),
            pltpu.SemaphoreType.DMA((max(heads - 1, 1), fields)),
            pltpu.SemaphoreType.DMA((max(heads - 1, 1), fields)),
            pltpu.SemaphoreType.DMA((max(parts - 1, 1), heads, fields)),
            pltpu.SemaphoreType.DMA((max(parts - 1, 1), heads, fields)),
        ],
        compiler_params=pltpu.CompilerParams(
            collective_id=collective_id, has_side_effects=True, vmem_limit_bytes=24 * 1024 * 1024
        ),
        name="spread",
    )(x_rows)


def collect_kernel(
    fields,
    heads,
    parts,
    x_ref,
    y_ref,
    own,
    got,
    ready,
    own_sem,
    pass_sem,
    take_sem,
    send_sem,
    recv_sem,
    keep_sem,
):
    me = lax.axis_index("seq")
    own_head, own_part = me // parts, me % parts
    seq_barrier(me, heads, parts)
    order = list(range(1, heads)) + [0]

    def home(step, part):
        return (own_head + step) % heads * parts + part

    passes, owns = {}, {}
    for step in order:
        for field in range(fields):
            for other in range(1, parts):
                part = (own_part + other) % parts
                copy = pltpu.make_async_remote_copy(
                    src_ref=x_ref.at[field, home(step, part)],
                    dst_ref=got.at[other - 1, step, field],
                    send_sem=pass_sem.at[other - 1, step, field],
                    recv_sem=take_sem.at[other - 1, step, field],
                    device_id={"seq": own_head * parts + part},
                    device_id_type=MESH,
                )
                copy.start()
                passes[step, field, other] = copy
            copy = pltpu.make_async_copy(
                x_ref.at[field, home(step, own_part)], own.at[step, field], own_sem.at[step, field]
            )
            copy.start()
            owns[step, field] = copy

    sends = []
    for step in order:
        for field in range(fields):
            owns[step, field].wait()
            for other in range(1, parts):
                passes[step, field, other].wait_recv()
            total = own[step, field].astype(jnp.float32)
            for other in range(1, parts):
                total = total + got[other - 1, step, field].astype(jnp.float32)
            ready[step, field] = total.astype(ready.dtype)
            columns = pl.ds(pl.multiple_of((field * heads + own_head) * HDIM, HDIM), HDIM)
            if step == 0:
                copy = pltpu.make_async_copy(
                    ready.at[step, field], y_ref.at[:, columns], keep_sem.at[field]
                )
            else:
                copy = pltpu.make_async_remote_copy(
                    src_ref=ready.at[step, field],
                    dst_ref=y_ref.at[:, columns],
                    send_sem=send_sem.at[step - 1, field],
                    recv_sem=recv_sem.at[step - 1, field],
                    device_id={"seq": home(step, own_part)},
                    device_id_type=MESH,
                )
            copy.start()
            sends.append(copy)
    for copy in sends:
        copy.wait()
    for copy in passes.values():
        copy.wait_send()


def collect(x_parts, heads, parts, collective_id):
    fields, seq_size, rows, _ = x_parts.shape
    kind = x_parts.dtype
    few = max(parts - 1, 1)
    return pl.pallas_call(
        functools.partial(collect_kernel, fields, heads, parts),
        out_shape=jax.ShapeDtypeStruct((rows, fields * heads * HDIM), kind),
        in_specs=[ANY],
        out_specs=ANY,
        scratch_shapes=[
            pltpu.VMEM((heads, fields, rows, HDIM), kind),
            pltpu.VMEM((few, heads, fields, rows, HDIM), kind),
            pltpu.VMEM((heads, fields, rows, HDIM), kind),
            pltpu.SemaphoreType.DMA((heads, fields)),
            pltpu.SemaphoreType.DMA((few, heads, fields)),
            pltpu.SemaphoreType.DMA((few, heads, fields)),
            pltpu.SemaphoreType.DMA((max(heads - 1, 1), fields)),
            pltpu.SemaphoreType.DMA((max(heads - 1, 1), fields)),
            pltpu.SemaphoreType.DMA((fields,)),
        ],
        compiler_params=pltpu.CompilerParams(
            collective_id=collective_id, has_side_effects=True, vmem_limit_bytes=VMEM_MOST
        ),
        name="collect",
    )(x_parts)


def allowed_tile(ends_ref, seq_count, key_low, query_low, shape):
    key_pos = key_low + lax.broadcasted_iota(jnp.int32, shape, 0)
    query_pos = query_low + lax.broadcasted_iota(jnp.int32, shape, 1)
    key_seg = jnp.zeros(shape, jnp.int32)
    query_seg = jnp.zeros(shape, jnp.int32)
    for index in range(seq_count):
        key_seg += (key_pos >= ends_ref[index]).astype(jnp.int32)
        query_seg += (query_pos >= ends_ref[index]).astype(jnp.int32)
    last = ends_ref[seq_count - 1]
    key_seg = jnp.where(key_pos < last, key_seg, seq_count + key_pos)
    query_seg = jnp.where(query_pos < last, query_seg, seq_count + query_pos)
    return key_seg == query_seg


def nt(left, right):
    return lax.dot_general(
        left, right, (((1,), (1,)), ((), ())), preferred_element_type=jnp.float32
    )


def nn(left, right):
    return lax.dot_general(
        left, right, (((1,), (0,)), ((), ())), preferred_element_type=jnp.float32
    )


def forward_kernel(
    setup,
    where_ref,
    low_ref,
    high_ref,
    ends_ref,
    part_ref,
    qkv_ref,
    out_ref,
    exact_ref,
    log_ref,
    q_buf,
    k_buf,
    v_buf,
    vt_buf,
    sem,
):
    parts, tile, seq_count, aligned, runs = setup
    turn = pl.program_id(0)
    part = part_ref[0]
    scale2 = math.log2(math.e) / math.sqrt(HDIM)

    @pl.when(turn == 0)
    def _():
        def fetch(field, run, buf, slot):
            return pltpu.make_async_copy(
                qkv_ref.at[field, where_ref[run]],
                buf.at[pl.ds(pl.multiple_of(slot * RUN, RUN), RUN), :],
                sem.at[field],
            )

        def start(run, carry):
            fetch(1, run, k_buf, run).start()
            fetch(2, run, v_buf, run).start()
            return carry

        def start_own(index, carry):
            fetch(0, index * parts + part, q_buf, index).start()
            return carry

        def finish(run, carry):
            fetch(1, run, k_buf, run).wait()
            fetch(2, run, v_buf, run).wait()
            return carry

        def finish_own(index, carry):
            fetch(0, index * parts + part, q_buf, index).wait()
            return carry

        lax.fori_loop(0, runs, start, 0)
        lax.fori_loop(0, runs // parts, start_own, 0)
        out_ref[...] = jnp.zeros_like(out_ref)
        lax.fori_loop(0, runs, finish, 0)
        lax.fori_loop(0, runs // parts, finish_own, 0)
        if aligned:

            def turn_tile(index, carry):
                low = pl.multiple_of(index * RUN, RUN)
                vt_buf[:, pl.ds(low, RUN)] = v_buf[pl.ds(low, RUN), :].T
                return carry

            lax.fori_loop(0, runs, turn_tile, 0)

    run = turn * parts + part
    place = where_ref[run]
    queries = q_buf[pl.ds(pl.multiple_of(turn * RUN, RUN), RUN), :]

    def attend():
        def key_step(index, carry):
            top, total, acc = carry
            low = pl.multiple_of(index * tile, tile)
            scores = nt(k_buf[pl.ds(low, tile), :], queries)
            if not aligned:
                allowed = allowed_tile(ends_ref, seq_count, low, run * RUN, scores.shape)
                scores = jnp.where(allowed, scores, NEG_LARGE)
            new_top = jnp.maximum(top, jnp.max(scores, axis=0, keepdims=True))
            prob = jnp.exp2((scores - new_top) * scale2)
            if not aligned:
                prob = jnp.where(allowed, prob, 0.0)
            fade = jnp.exp2((top - new_top) * scale2)
            total = total * fade + jnp.sum(prob, axis=0, keepdims=True)
            if aligned:
                turned = vt_buf[:, pl.ds(low, tile)]
            else:
                turned = v_buf[pl.ds(low, tile), :].T
            acc = acc * fade + nn(turned, prob.astype(jnp.bfloat16))
            return new_top, total, acc

        top, total, acc = lax.fori_loop(
            low_ref[run],
            high_ref[run],
            key_step,
            (
                jnp.full((1, RUN), NEG_LARGE, jnp.float32),
                jnp.zeros((1, RUN), jnp.float32),
                jnp.zeros((HDIM, RUN), jnp.float32),
            ),
        )
        result = (acc / total).T
        exact_ref[0] = result
        out_ref[place] = result.astype(out_ref.dtype)
        log_ref[0] = top * scale2 + jnp.log2(total)

    if aligned:
        is_valid = run * RUN < ends_ref[seq_count - 1]
        pl.when(is_valid)(attend)

        @pl.when(jnp.logical_not(is_valid))
        def _():
            values = v_buf[pl.ds(pl.multiple_of(run * RUN, RUN), RUN), :]
            exact_ref[0] = values.astype(jnp.float32)
            out_ref[place] = values
            log_ref[0] = jnp.zeros((1, RUN), jnp.float32)
    else:
        attend()


def attend_forward(qkv, tables, setup):
    parts, tile, seq_count, aligned, runs = setup
    own = runs // parts
    rows = runs * RUN
    return pl.pallas_call(
        functools.partial(forward_kernel, setup),
        grid=(own,),
        out_shape=(
            jax.ShapeDtypeStruct((runs, RUN, HDIM), jnp.bfloat16),
            jax.ShapeDtypeStruct((own, RUN, HDIM), jnp.float32),
            jax.ShapeDtypeStruct((own, 1, RUN), jnp.float32),
        ),
        in_specs=[IN_SMEM] * 5 + [ANY],
        out_specs=(
            pl.BlockSpec((runs, RUN, HDIM), lambda i: (0, 0, 0), pipeline_mode=pl.Buffered(1)),
            pl.BlockSpec((1, RUN, HDIM), lambda i: (i, 0, 0)),
            pl.BlockSpec((1, 1, RUN), lambda i: (i, 0, 0)),
        ),
        scratch_shapes=[
            pltpu.VMEM((own * RUN, HDIM), jnp.bfloat16),
            pltpu.VMEM((rows, HDIM), jnp.bfloat16),
            pltpu.VMEM((rows, HDIM), jnp.bfloat16),
            pltpu.VMEM((HDIM, rows if aligned else RUN), jnp.bfloat16),
            pltpu.SemaphoreType.DMA((3,)),
        ],
        compiler_params=pltpu.CompilerParams(
            dimension_semantics=("arbitrary",), vmem_limit_bytes=VMEM_MOST
        ),
        name="attend_forward",
    )(*tables, qkv)


def backward_kernel(
    setup,
    where_ref,
    low_ref,
    high_ref,
    ends_ref,
    part_ref,
    qkv_ref,
    grad_ref,
    exact_ref,
    log_ref,
    out_ref,
    q_buf,
    k_buf,
    v_buf,
    kt_buf,
    g_buf,
    dk_acc,
    dv_acc,
    stage,
    sem,
    out_sem,
):
    parts, tile, seq_count, aligned, runs = setup
    own = runs // parts
    turn = pl.program_id(0)
    part = part_ref[0]
    scale = 1.0 / math.sqrt(HDIM)
    scale2 = math.log2(math.e) * scale

    @pl.when(turn == 0)
    def _():
        def fetch(source, index, buf, slot, lane):
            return pltpu.make_async_copy(
                source.at[index],
                buf.at[pl.ds(pl.multiple_of(slot * RUN, RUN), RUN), :],
                sem.at[lane],
            )

        def pair(run):
            place = where_ref[run]
            return (
                fetch(qkv_ref.at[1], place, k_buf, run, 1),
                fetch(qkv_ref.at[2], place, v_buf, run, 2),
            )

        def own_pair(index):
            place = where_ref[index * parts + part]
            return (
                fetch(qkv_ref.at[0], place, q_buf, index, 0),
                fetch(grad_ref, place, g_buf, index, 3),
            )

        def start(run, carry):
            for copy in pair(run):
                copy.start()
            return carry

        def start_own(index, carry):
            for copy in own_pair(index):
                copy.start()
            return carry

        def finish(run, carry):
            for copy in pair(run):
                copy.wait()
            return carry

        def finish_own(index, carry):
            for copy in own_pair(index):
                copy.wait()
            return carry

        lax.fori_loop(0, runs, start, 0)
        lax.fori_loop(0, own, start_own, 0)
        dk_acc[...] = jnp.zeros_like(dk_acc)
        dv_acc[...] = jnp.zeros_like(dv_acc)
        lax.fori_loop(0, runs, finish, 0)
        lax.fori_loop(0, own, finish_own, 0)
        if aligned:

            def turn_tile(index, carry):
                low = pl.multiple_of(index * RUN, RUN)
                kt_buf[:, pl.ds(low, RUN)] = k_buf[pl.ds(low, RUN), :].T
                return carry

            lax.fori_loop(0, runs, turn_tile, 0)

    run = turn * parts + part
    low_row = pl.multiple_of(turn * RUN, RUN)

    def attend():
        queries = q_buf[pl.ds(low_row, RUN), :]
        grads = g_buf[pl.ds(low_row, RUN), :]
        delta = jnp.sum((grads.astype(jnp.float32) * exact_ref[0]).T, axis=0, keepdims=True)
        log_total = log_ref[0]

        def key_step(index, acc):
            low = pl.multiple_of(index * tile, tile)
            keys = k_buf[pl.ds(low, tile), :]
            values = v_buf[pl.ds(low, tile), :]
            scores = nt(keys, queries)
            prob = jnp.exp2(scores * scale2 - log_total)
            if not aligned:
                allowed = allowed_tile(ends_ref, seq_count, low, run * RUN, scores.shape)
                prob = jnp.where(allowed, prob, 0.0)
            prob_grad = nt(values, grads)
            dv_acc[pl.ds(low, tile), :] += nn(prob.astype(jnp.bfloat16), grads)
            score_grad = (prob * (prob_grad - delta)).astype(jnp.bfloat16)
            dk_acc[pl.ds(low, tile), :] += nn(score_grad, queries)
            turned = kt_buf[:, pl.ds(low, tile)] if aligned else keys.T
            return acc + nn(turned, score_grad)

        acc = lax.fori_loop(
            low_ref[run], high_ref[run], key_step, jnp.zeros((HDIM, RUN), jnp.float32)
        )
        q_buf[pl.ds(low_row, RUN), :] = (acc.T * scale).astype(jnp.bfloat16)

    if aligned:
        is_valid = run * RUN < ends_ref[seq_count - 1]
        pl.when(is_valid)(attend)

        @pl.when(jnp.logical_not(is_valid))
        def _():
            q_buf[pl.ds(low_row, RUN), :] = jnp.zeros((RUN, HDIM), jnp.bfloat16)
    else:
        attend()

    @pl.when(turn == own - 1)
    def _():
        def key_copies(run_index, slot):
            place = where_ref[run_index]
            return (
                pltpu.make_async_copy(stage.at[slot, 0], out_ref.at[1, place], out_sem.at[slot, 0]),
                pltpu.make_async_copy(stage.at[slot, 1], out_ref.at[2, place], out_sem.at[slot, 1]),
            )

        v_buf[pl.ds(0, RUN), :] = jnp.zeros((RUN, HDIM), jnp.bfloat16)

        def query_copy(run_index):
            mine = run_index % parts == part
            place = where_ref[run_index]
            index = jnp.where(mine, run_index // parts, 0)
            return mine, (
                pltpu.make_async_copy(
                    q_buf.at[pl.ds(pl.multiple_of(index * RUN, RUN), RUN), :],
                    out_ref.at[0, place],
                    sem.at[0],
                ),
                pltpu.make_async_copy(
                    v_buf.at[pl.ds(0, RUN), :], out_ref.at[0, place], sem.at[0]
                ),
            )

        def start_query(run_index, carry):
            mine, (copy, blank) = query_copy(run_index)
            pl.when(mine)(copy.start)
            pl.when(jnp.logical_not(mine))(blank.start)
            return carry

        def finish_query(run_index, carry):
            _, (copy, blank) = query_copy(run_index)
            blank.wait()
            return carry

        lax.fori_loop(0, runs, start_query, 0)

        def write(run_index, carry):
            slot = run_index % 2

            @pl.when(run_index >= 2)
            def _():
                for copy in key_copies(run_index - 2, slot):
                    copy.wait()

            low = pl.multiple_of(run_index * RUN, RUN)
            stage[slot, 0] = (dk_acc[pl.ds(low, RUN), :] * scale).astype(jnp.bfloat16)
            stage[slot, 1] = dv_acc[pl.ds(low, RUN), :].astype(jnp.bfloat16)
            for copy in key_copies(run_index, slot):
                copy.start()
            return carry

        lax.fori_loop(0, runs, write, 0)
        for back in (2, 1):
            for copy in key_copies(runs - back, (runs - back) % 2):
                copy.wait()
        lax.fori_loop(0, runs, finish_query, 0)


def attend_backward(qkv, grads, exact, log_total, tables, setup):
    parts, tile, seq_count, aligned, runs = setup
    own = runs // parts
    rows = runs * RUN
    return pl.pallas_call(
        functools.partial(backward_kernel, setup),
        grid=(own,),
        out_shape=jax.ShapeDtypeStruct((3, runs, RUN, HDIM), jnp.bfloat16),
        in_specs=[IN_SMEM] * 5
        + [
            ANY,
            ANY,
            pl.BlockSpec((1, RUN, HDIM), lambda i: (i, 0, 0)),
            pl.BlockSpec((1, 1, RUN), lambda i: (i, 0, 0)),
        ],
        out_specs=ANY,
        scratch_shapes=[
            pltpu.VMEM((own * RUN, HDIM), jnp.bfloat16),
            pltpu.VMEM((rows, HDIM), jnp.bfloat16),
            pltpu.VMEM((rows, HDIM), jnp.bfloat16),
            pltpu.VMEM((HDIM, rows if aligned else RUN), jnp.bfloat16),
            pltpu.VMEM((own * RUN, HDIM), jnp.bfloat16),
            pltpu.VMEM((rows, HDIM), jnp.float32),
            pltpu.VMEM((rows, HDIM), jnp.float32),
            pltpu.VMEM((2, 2, RUN, HDIM), jnp.bfloat16),
            pltpu.SemaphoreType.DMA((4,)),
            pltpu.SemaphoreType.DMA((2, 2)),
        ],
        compiler_params=pltpu.CompilerParams(
            dimension_semantics=("arbitrary",), vmem_limit_bytes=VMEM_MOST
        ),
        name="attend_backward",
    )(*tables, qkv, grads, exact, log_total)


def stream_tables(token_order, lengths, head_count, seq_size, parts, tile, part):
    runs = token_order.shape[0] // RUN
    stream = (token_order.reshape(head_count, seq_size, RUN)[:, :, 0] // RUN).T.reshape(-1)
    places = jnp.arange(runs, dtype=jnp.int32)
    where = jnp.sum(jnp.where(stream[None, :] == places[:, None], places[None, :], 0), axis=1)
    ends = jnp.cumsum(lengths)
    starts = ends - lengths
    first = places * RUN
    last = first + RUN - 1

    def bound(position, of_seq, of_pad):
        inside = (position[:, None] >= starts[None, :]) & (position[:, None] < ends[None, :])
        found = jnp.sum(jnp.where(inside, of_seq[None, :], 0), axis=1)
        return jnp.where(position < ends[-1], found, of_pad)

    low = bound(first, starts, first) // tile
    high = (bound(last, ends, last + 1) + tile - 1) // tile
    return (
        where.astype(jnp.int32),
        low.astype(jnp.int32),
        high.astype(jnp.int32),
        ends.astype(jnp.int32),
        part.reshape(1).astype(jnp.int32),
    )


def normalize(z_rows, gain, shift):
    average = jnp.mean(z_rows, axis=-1, keepdims=True)
    centered = z_rows - average
    variance = jnp.mean(centered * centered, axis=-1, keepdims=True)
    recip = lax.rsqrt(variance + NORM_EPS)
    normed = centered * recip
    return (normed * gain + shift, normed, recip)


def normalize_back(grad_rows, normed, recip, gain):
    scaled = grad_rows * gain
    dz_rows = recip * (
        scaled
        - jnp.mean(scaled, axis=-1, keepdims=True)
        - normed * jnp.mean(scaled * normed, axis=-1, keepdims=True)
    )
    return (dz_rows, jnp.sum(grad_rows * normed, axis=0), jnp.sum(grad_rows, axis=0))


def group_rows(rows_low):
    return lax.all_gather(rows_low, "head", axis=0, tiled=True)


def group_sums(partial_value):
    return lax.psum_scatter(
        partial_value.astype(jnp.bfloat16), "head", scatter_dimension=0, tiled=True
    ).astype(jnp.float32)


def to_blocks(panel):
    height, breadth = panel.shape
    shaped = panel.reshape(height // BLOCK, BLOCK, breadth // BLOCK, BLOCK)
    return shaped.transpose(0, 2, 1, 3).reshape(-1, BLOCK, BLOCK)


def weight_grad(rows, grads):
    return lax.dot_general(
        rows, grads, (((0,), (0,)), ((), ())), preferred_element_type=jnp.float32
    ).astype(jnp.bfloat16)


def adam_step(param, grad, moment, second, step_float):
    moment_new = 0.9 * moment + 0.1 * grad
    second_new = 0.999 * second + 0.001 * grad * grad
    fix_one = 1.0 - jnp.power(jnp.float32(0.9), step_float)
    fix_two = 1.0 - jnp.power(jnp.float32(0.999), step_float)
    update = ADAM_RATE * (moment_new / fix_one) / (jnp.sqrt(second_new / fix_two) + 1e-08)
    return (param - update, moment_new, second_new)


def shards(
    hidden_in,
    cotangent,
    lengths,
    token_order,
    own_map,
    w_query,
    w_key,
    w_value,
    w_out,
    w_up,
    w_down,
    gains,
    biases,
    up_bias,
    vector_moment,
    vector_second,
    bias_moment,
    bias_second,
    step_count,
    stat_left,
    stat_right,
    root_left,
    root_right,
    master,
):
    head_count = lax.axis_size("head")
    seq_size = lax.axis_size("seq")
    head_index = lax.axis_index("head")
    group_index = lax.axis_index("seq")
    tok_count = hidden_in.shape[0]
    width = hidden_in.shape[1]
    panel_width = w_query.shape[1]
    ff_width = w_up.shape[1]
    seq_count = lengths.shape[0]
    heads = panel_width // HDIM
    parts = seq_size // heads
    runs = token_order.shape[0] // RUN
    aligned = seq_count == 2
    tile = 1024 if aligned else RUN
    setup = (parts, tile, seq_count, aligned, runs)
    tables = stream_tables(
        token_order, lengths, head_count, seq_size, parts, tile, group_index % parts
    )
    own_block = head_index * seq_size + group_index
    order_here = lax.dynamic_slice_in_dim(token_order, own_block * tok_count, tok_count, 0)
    valid_here = order_here < tables[3][seq_count - 1]
    inputs_f32 = hidden_in.astype(jnp.float32)

    qkv_panel = lax.all_gather(
        jnp.concatenate([w_query, w_key, w_value], axis=1), "seq", axis=0, tiled=True
    )
    inputs_grp = group_rows(hidden_in)
    o_panel = lax.all_gather(w_out, "seq", axis=1, tiled=True)
    up_panel = lax.all_gather(w_up, "seq", axis=0, tiled=True)
    down_panel = lax.all_gather(w_down, "seq", axis=1, tiled=True)

    def own_columns(row):
        return lax.dynamic_slice_in_dim(row, head_index * panel_width, panel_width, 0)

    qkv_bias = jnp.concatenate(
        [own_columns(biases[0]), jnp.zeros((panel_width,), jnp.float32), own_columns(biases[1])]
    )
    qkv_grp = (
        jnp.dot(inputs_grp, qkv_panel, preferred_element_type=jnp.float32) + qkv_bias
    ).astype(jnp.bfloat16)
    qkv_head = spread(qkv_grp, 3, heads, parts, seq_size, 0).reshape(3, runs, RUN, HDIM)
    attended_part, attended_exact, log_total = attend_forward(qkv_head, tables, setup)
    rows_grp = head_count * tok_count
    attended_grp = collect(
        attended_part.reshape(1, seq_size, rows_grp, HDIM), heads, parts, 1
    )
    branch_out = group_sums(jnp.dot(attended_grp, o_panel, preferred_element_type=jnp.float32))
    z_one = inputs_f32 + branch_out + biases[2]
    h_one, normed_one, recip_one = normalize(z_one, gains[0], biases[3])
    h_low = h_one.astype(jnp.bfloat16)
    h_grp = group_rows(h_low)
    pre_act = jnp.dot(h_grp, up_panel, preferred_element_type=jnp.float32) + up_bias
    act = jax.nn.gelu(pre_act, approximate=True).astype(jnp.bfloat16)
    ff_out = group_sums(jnp.dot(act, down_panel, preferred_element_type=jnp.float32))
    z_two = h_one + ff_out + biases[4]
    layer_f32, normed_two, recip_two = normalize(z_two, gains[1], biases[5])
    layer_out = layer_f32.astype(jnp.bfloat16)
    grad_y = cotangent.astype(jnp.float32) * valid_here[:, None].astype(jnp.float32)
    dz_two, dgain_two, dshift_two = normalize_back(grad_y, normed_two, recip_two, gains[1])
    dbias_down = jnp.sum(dz_two, axis=0)
    dz_two_grp = group_rows(dz_two.astype(jnp.bfloat16))
    dact = jnp.dot(dz_two_grp, down_panel.T, preferred_element_type=jnp.float32)
    gelu_value, gelu_pull = jax.vjp(lambda inner: jax.nn.gelu(inner, approximate=True), pre_act)
    dpre = gelu_pull(dact)[0].astype(jnp.bfloat16)
    up_bias_part = jnp.sum(dpre.astype(jnp.float32), axis=0)
    dh_one = dz_two + group_sums(jnp.dot(dpre, up_panel.T, preferred_element_type=jnp.float32))
    dz_one, dgain_one, dshift_one = normalize_back(dh_one, normed_one, recip_one, gains[0])
    dbias_out = jnp.sum(dz_one, axis=0)
    dz_one_grp = group_rows(dz_one.astype(jnp.bfloat16))
    dattended = jnp.dot(dz_one_grp, o_panel.T, preferred_element_type=jnp.float32).astype(
        jnp.bfloat16
    )
    dattended_head = spread(dattended, 1, heads, parts, seq_size, 2).reshape(runs, RUN, HDIM)
    dqkv_part = attend_backward(
        qkv_head, dattended_head, attended_exact, log_total, tables, setup
    )
    dqkv_grp = collect(dqkv_part.reshape(3, seq_size, rows_grp, HDIM), heads, parts, 3)
    input_grad = dz_one + group_sums(
        jnp.dot(dqkv_grp, qkv_panel.T, preferred_element_type=jnp.float32)
    )
    grad_down = weight_grad(act, dz_two_grp)
    grad_up = weight_grad(h_grp, dpre)
    grad_out = weight_grad(attended_grp, dz_one_grp)
    grad_qkv = weight_grad(inputs_grp, dqkv_grp)
    bias_qkv = jnp.sum(dqkv_grp.astype(jnp.float32), axis=0)
    zero_width = jnp.zeros((width,), jnp.float32)
    dbias_query = lax.dynamic_update_slice_in_dim(
        zero_width, bias_qkv[:panel_width], head_index * panel_width, 0
    )
    dbias_value = lax.dynamic_update_slice_in_dim(
        zero_width, bias_qkv[2 * panel_width :], head_index * panel_width, 0
    )
    local_vectors = jnp.stack(
        (
            dbias_query,
            dbias_value,
            dbias_out,
            dshift_one,
            dbias_down,
            dshift_two,
            dgain_one,
            dgain_two,
        )
    )
    up_bias_grad = lax.psum(up_bias_part, "seq")
    vector_grad = lax.psum(local_vectors, ("head", "seq"))
    canon = jnp.concatenate(
        [
            to_blocks(grad_qkv[:, :panel_width]),
            to_blocks(grad_qkv[:, panel_width : 2 * panel_width]),
            to_blocks(grad_qkv[:, 2 * panel_width :]),
            to_blocks(grad_out),
            to_blocks(grad_up),
            to_blocks(grad_down),
        ],
        axis=0,
    )
    ordered = jnp.take(canon, own_map[0], axis=0)
    low_grads = lax.psum_scatter(ordered, "seq", scatter_dimension=0, tiled=True)
    block_grads = low_grads.astype(jnp.float32)
    stat_left_new = 0.5 * stat_left + 0.5 * jnp.einsum(
        "bij,bkj->bik", low_grads, low_grads, preferred_element_type=jnp.float32
    )
    stat_right_new = 0.5 * stat_right + 0.5 * jnp.einsum(
        "bji,bjk->bik", low_grads, low_grads, preferred_element_type=jnp.float32
    )
    left_mix = jnp.einsum("bij,bjk->bik", root_left, block_grads, precision=lax.Precision.HIGHEST)
    direction = jnp.einsum("bij,bjk->bik", left_mix, root_right, precision=lax.Precision.HIGHEST)
    master_new = master - SHAMPOO_RATE * direction
    step_float = step_count[0].astype(jnp.float32)
    vector_params = jnp.concatenate([biases, gains], axis=0)
    vector_new, vector_moment_new, vector_second_new = adam_step(
        vector_params, vector_grad, vector_moment, vector_second, step_float
    )
    up_bias_new, bias_moment_new, bias_second_new = adam_step(
        up_bias, up_bias_grad, bias_moment, bias_second, step_float
    )
    return (
        layer_out,
        input_grad,
        block_grads,
        stat_left_new,
        stat_right_new,
        master_new,
        vector_new[0:6],
        vector_new[6:8],
        up_bias_new,
        vector_grad,
        vector_moment_new,
        vector_second_new,
        up_bias_grad,
        bias_moment_new,
        bias_second_new,
    )


def solution(mesh):
    rows = P(("head", "seq"), None)
    blocks = P(("head", "seq"), None, None)
    in_specs = (
        rows,
        rows,
        P(),
        P(),
        P("head", None),
        P("seq", "head"),
        P("seq", "head"),
        P("seq", "head"),
        P("head", "seq"),
        P("seq", "head"),
        P("head", "seq"),
        P(),
        P(),
        P("head"),
        P(),
        P(),
        P("head"),
        P("head"),
        P(),
        blocks,
        blocks,
        blocks,
        blocks,
        blocks,
    )
    out_specs = (
        rows,
        rows,
        blocks,
        blocks,
        blocks,
        blocks,
        P(),
        P(),
        P("head"),
        P(),
        P(),
        P(),
        P("head"),
        P("head"),
        P("head"),
    )
    return jax.shard_map(shards, mesh=mesh, in_specs=in_specs, out_specs=out_specs, check_vma=False)
```

time: 2980 us -> 1480 us (0.50)
  starting transfers between devices: 590 us -> 1.36 us
  waiting for transfers between devices: 1240 us -> 802 us
  matrix products: 471 us -> 164 us
  Pallas kernels: 0 us -> 281 us
  local copies, waits for them, and re-layouts: 355 us -> 122 us
  other arithmetic: 148 us -> 56.4 us
  loops' own time: 88.7 us -> 0 us
  blocking collectives: 78.3 us -> 32.7 us
    ppermute x44 -> x0, starting transfers between devices: 559 us -> none  [shifted(): lax.ppermute(array, axis, [(i, (i + by) % length) for i in range(length)])]
    ppermute x44 -> x0, waiting for transfers between devices: 318 us -> none  [shifted(): lax.ppermute(array, axis, [(i, (i + by) % length) for i in range(length)])]
    dot_general x157 -> x10, matrix products: 387 us -> 80.2 us  [the longest x4 40.3 us: weight_grad(): lax.dot_general(rows, grads, (((0,), (0,)), ((), ())), preferred_element_...]
    pallas_call x0 -> x6, Pallas kernels: none -> 281 us  [the longest x2 100 us: collect(): pl.pallas_call(functools.partial(collect_kernel, fields, heads, parts), o...]
    all_gather x10 -> x4, waiting for transfers between devices: 455 us -> 214 us  [the longest x1 77.3 us: shards(): up_panel = lax.all_gather(w_up, 'seq', axis=0, tiled=True)]
    dynamic_slice x311 -> x1, local copies, waits for them, and re-layouts: 150 us -> 0.01 us  [own_columns(): lax.dynamic_slice_in_dim(row, head_index * panel_width, panel_width, 0)]
    convert_element_type x34 -> x2, other arithmetic: 93.9 us -> 4.57 us  [the longest x1 3.46 us: shards(): block_grads = low_grads.astype(jnp.float32)]
    another operation x210 -> x0, loops' own time: 88.7 us -> none  [the longest x32 43.2 us: forward_per_key(): return lax.fori_loop(0, pair_flags.shape[0], forward_per_query, outer_state)]
  transfers between devices with their start and end apart: 70 -> 14, of which waited for: 44 -> 12; matrix products, arithmetic and copies ran while one was open for 29% -> 15% of each run, Pallas kernels for 0% -> 10%
where the time goes in v1:
time: 1480 us
  waiting for transfers between devices  802 us (54%)
  Pallas kernels  281 us (19%)
  matrix products  164 us (11%)
  local copies, waits for them, and re-layouts  122 us (8%)
  other arithmetic  56.4 us (4%)
  blocking collectives  32.7 us (2%)
  between operations  15.9 us (1%)
    reduce_scatter x1, waiting for transfers between devices, shards(): lax.psum_scatter(ordered, 'seq', scatter_dimension=0, tiled=True)  247 us
    all_gather x4, waiting for transfers between devices, group_rows(): return lax.all_gather(rows_low, 'head', axis=0, tiled=True)  170 us
    reduce_scatter x4, waiting for transfers between devices, group_sums(): lax.psum_scatter(partial_value.astype(jnp.bfloat16), 'head', scatter_dime...  169 us
    pallas_call x2, Pallas kernels, collect(): pl.pallas_call(functools.partial(collect_kernel, fields, heads, parts), o...  100 us
    pallas_call x2, Pallas kernels, spread(): pl.pallas_call(functools.partial(spread_kernel, fields, heads, parts), ou...  95 us
    all_gather x1, waiting for transfers between devices, shards(): up_panel = lax.all_gather(w_up, 'seq', axis=0, tiled=True)  77.3 us
    all_gather x1, waiting for transfers between devices, shards(): down_panel = lax.all_gather(w_down, 'seq', axis=1, tiled=True)  69.5 us
    all_gather x1, waiting for transfers between devices, shards(): lax.all_gather(jnp.concatenate([w_query, w_key, w_value], axis=1), 'seq',...  66.9 us
  transfers between devices with their start and end apart: 14, of which 12 were waited for; matrix products, arithmetic and copies ran while one was open for 15% of the time, Pallas kernels for 10%

profile of v1, /device:TPU:0, one launch (start us, length us, event | category | flops | bytes accessed | tf_op | source)
XLA Modules:
  0.0 1475.9 jit_solution(11358756372248364006)
XLA Ops:
  17.1 48.1 %all-gather.11.cloned.1.call-done = bf16[1024,2048]{1,0:T(8,128)(2,1)} async-done(((bf16[256,2048]{1,0:T(8,128)(2,1)}), bf16[1024,2048]{1,0:T(8,128)(2,1)}) %all-gather.11.cloned.1.call-update) | async-done | bytes 4194320 | tf_op jit(solution)/shard_map/all_gather | solution.py:679
  65.2 66.9 %all-gather.9.cloned.1.call-done = bf16[2048,1536]{1,0:T(8,128)(2,1)} async-done(((bf16[256,1536]{1,0:T(8,128)(2,1)}), bf16[2048,1536]{1,0:T(8,128)(2,1)}) %all-gather.9.cloned.1.call-update) | async-done | bytes 6291472 | tf_op jit(solution)/shard_map/all_gather | solution.py:758
  132.1 10.0 fusion.8.x_ref
  142.1 71.6 %spread.2 = bf16[3,8,1024,128]{3,2,1,0:T(8,128)(2,1)S(1)} custom-call(bf16[1024,1536]{1,0:T(8,128)(2,1)S(1)} %fusion.8.x_ref), custom_call_target="tpu_custom_call" | custom-call | tf_op jit(solution)/shard_map/spread/pallas_call | solution.py:111
  216.4 35.8 %attend_forward.1 = (bf16[32,256,128]{2,1,0:T(8,128)(2,1)}, f32[16,256,128]{2,1,0:T(8,128)}, f32[16,1,256]{2,1,0:T(1,128)}) custom-call(s32[32]{0:T(128)} %select_reduce_fusion.where_ref, s32[32]{0:T(128)} %get-tuple-element.63.low_ref, s32[32]{0:T(128)} %get-tuple-element.62.high_ref, s32[2]{0:T(128)} %bitcast.165, s32[1]{0:T(128)} %bitcast.4.part_ref, ...), custom_call_target="tpu_custom_call" | custom-call | tf_op jit(solution)/shard_map/attend_forward/pallas_call | solution.py:381
  252.2 38.6 %collect.2 = bf16[1024,512]{1,0:T(8,128)(2,1)} custom-call(bf16[1,8,1024,128]{3,2,1,0:T(8,128)(2,1)} %bitcast.135), custom_call_target="tpu_custom_call" | custom-call | tf_op jit(solution)/shard_map/collect/pallas_call | solution.py:211
  290.8 6.3 convolution_convert_fusion.6
  297.9 57.6 %reduce-scatter.6.cloned.1.call-done = bf16[256,2048]{1,0:T(8,128)(2,1)} async-done(((bf16[1024,2048]{1,0:T(8,128)(2,1)}), bf16[256,2048]{1,0:T(8,128)(2,1)}) %reduce-scatter.6.cloned.1.call-update) | async-done | bytes 1048592 | tf_op jit(solution)/shard_map/reduce_scatter | solution.py:683
  361.7 77.3 %all-gather.17.cloned.1.call-done = bf16[2048,2048]{1,0:T(8,128)(2,1)} async-done(((bf16[256,2048]{1,0:T(8,128)(2,1)}), bf16[2048,2048]{1,0:T(8,128)(2,1)}) %all-gather.17.cloned.1.call-update) | async-done | bytes 8388624 | tf_op jit(solution)/shard_map/all_gather | solution.py:763
  439.0 53.4 %all-gather.15.cloned.1.call-done = bf16[1024,2048]{1,0:T(8,128)(2,1)} async-done(((bf16[256,2048]{1,0:T(8,128)(2,1)}), bf16[1024,2048]{1,0:T(8,128)(2,1)}) %all-gather.15.cloned.1.call-update) | async-done | bytes 4194320 | tf_op jit(solution)/shard_map/all_gather | solution.py:679
  492.3 14.6 fusion.33
  506.9 69.5 %all-gather.19.cloned.1.call-done = bf16[2048,2048]{1,0:T(8,128)(2,1)} async-done(((bf16[2048,256]{1,0:T(8,128)(2,1)}), bf16[2048,2048]{1,0:T(8,128)(2,1)}) %all-gather.19.cloned.1.call-update) | async-done | bytes 8388624 | tf_op jit(solution)/shard_map/all_gather | solution.py:764
  576.4 16.0 %convolution_convert_fusion.5 = bf16[1024,2048]{1,0:T(8,128)(2,1)} fusion(bf16[2048,2048]{1,0:T(8,128)(2,1)} %all-gather.19.cloned.1.call-done, f32[1024,2048]{1,0:T(8,128)} %fusion.33, f32[2048]{0:T(1024)S(1)} %copy-done.22), kind=kOutput, calls=%fused_computation.24 | convolution fusion | flops 8613003264 | bytes 20979712 | tf_op jit(solution)/shard_map/dot_general | solution.py:788
  594.0 49.4 %reduce-scatter.8.cloned.1.call-done = bf16[256,2048]{1,0:T(8,128)(2,1)} async-done(((bf16[1024,2048]{1,0:T(8,128)(2,1)}), bf16[256,2048]{1,0:T(8,128)(2,1)}) %reduce-scatter.8.cloned.1.call-update) | async-done | bytes 1048592 | tf_op jit(solution)/shard_map/reduce_scatter | solution.py:683
  650.6 52.3 %all-gather.21.cloned.1.call-done = bf16[1024,2048]{1,0:T(8,128)(2,1)} async-done(((bf16[256,2048]{1,0:T(8,128)(2,1)}), bf16[1024,2048]{1,0:T(8,128)(2,1)}) %all-gather.21.cloned.1.call-update) | async-done | bytes 4194320 | tf_op jit(solution)/shard_map/all_gather | solution.py:679
  702.9 19.2 %convert_reduce_fusion = (f32[2048]{0:T(1024)}, bf16[1024,2048]{1,0:T(8,128)(2,1)S(1)}) fusion(f32[1024,2048]{1,0:T(8,128)} %fusion.33, f32[2048]{0:T(1024)S(1)} %copy-done.22, bf16[1024,2048]{1,0:T(8,128)(2,1)} %all-gather.21.cloned.1.call-done, bf16[2048,2048]{1,0:T(8,128)(2,1)} %all-gather.19.cloned.1.call-done), kind=kOutput, calls=%fused_computation.11 | convolution fusion | flops 8638167040 | bytes 25182208 | tf_op jit(solution)/shard_map/dot_general | solution.py:796
  724.1 12.8 convolution_convert_fusion.4
  737.1 52.5 %reduce-scatter.10.cloned.1.call-done = bf16[256,2048]{1,0:T(8,128)(2,1)} async-done(((bf16[1024,2048]{1,0:T(8,128)(2,1)}), bf16[256,2048]{1,0:T(8,128)(2,1)}) %reduce-scatter.10.cloned.1.call-update) | async-done | bytes 1048592 | tf_op jit(solution)/shard_map/reduce_scatter | solution.py:683
  796.8 16.2 %convolution_convert_fusion = bf16[2048,2048]{1,0:T(8,128)(2,1)} fusion(bf16[1024,2048]{1,0:T(8,128)(2,1)} %all-gather.21.cloned.1.call-done, f32[1024,2048]{1,0:T(8,128)} %fusion.33, f32[2048]{0:T(1024)S(1)} %copy-done.22), kind=kOutput, calls=%fused_computation.13 | convolution fusion | flops 8615100416 | bytes 20979712 | tf_op jit(solution)/shard_map/dot_general | solution.py:695
  813.0 10.3 copy.82
  823.3 9.7 copy.69
  833.0 16.4 %all-gather.23.cloned.1.call-done = bf16[1024,2048]{1,0:T(8,128)(2,1)} async-done(((bf16[256,2048]{1,0:T(8,128)(2,1)}), bf16[1024,2048]{1,0:T(8,128)(2,1)}) %all-gather.23.cloned.1.call-update) | async-done | bytes 4194320 | tf_op jit(solution)/shard_map/all_gather | solution.py:679
  849.5 4.5 convolution_convert_fusion.8.x_ref
  854.0 23.4 %spread.3 = bf16[1,8,1024,128]{3,2,1,0:T(8,128)(2,1)S(1)} custom-call(bf16[1024,512]{1,0:T(8,128)(2,1)S(1)} %convolution_convert_fusion.8.x_ref), custom_call_target="tpu_custom_call" | custom-call | tf_op jit(solution)/shard_map/spread/pallas_call | solution.py:111
  878.8 49.7 %attend_backward.1 = bf16[3,32,256,128]{3,2,1,0:T(8,128)(2,1)} custom-call(s32[32]{0:T(128)} %select_reduce_fusion.where_ref, s32[32]{0:T(128)} %get-tuple-element.63.low_ref, s32[32]{0:T(128)} %get-tuple-element.62.high_ref, s32[2]{0:T(128)} %bitcast.166, s32[1]{0:T(128)} %bitcast.4.part_ref, bf16[3,32,256,128]{3,2,1,0:T(8,128)(2,1)} %bitcast.111, ...), custom_call_target="tpu_custom_call" | custom-call | tf_op jit(solution)/shard_map/attend_backward/pallas_call | solution.py:602
  928.5 61.6 %collect.3 = bf16[1024,1536]{1,0:T(8,128)(2,1)} custom-call(bf16[3,8,1024,128]{3,2,1,0:T(8,128)(2,1)} %bitcast.117), custom_call_target="tpu_custom_call" | custom-call | tf_op jit(solution)/shard_map/collect/pallas_call | solution.py:211
  993.4 11.3 convolution_convert_fusion.3
  1004.7 14.0 convolution_convert_fusion.1
  1018.7 10.3 copy.81
  1029.0 9.0 copy.68
  1043.7 7.6 fusion.7
  1056.4 4.3 copy.66
  1060.7 3.6 copy.78
  1064.3 4.3 copy.65
  1068.6 3.6 copy.77
  1072.2 4.3 copy.64
  1084.2 7.6 constant_dynamic-update-slice_fusion.1
  1091.8 7.6 constant_dynamic-update-slice_fusion
  1099.5 19.4 %gather_fusion = bf16[192,256,256]{2,1,0:T(8,128)(2,1)} fusion(bf16[192,256,256]{2,1,0:T(8,128)(2,1)} %constant_dynamic-update-slice_fusion, s32[1024]{0:T(1024)S(1)} %pad_clamp_fusion), kind=kCustom, calls=%fused_computation | custom fusion | bytes 50332416 | tf_op jit(solution)/shard_map/jit(_take)/gather | solution.py:852
  1118.9 21.1 %broadcast_select_fusion = bf16[192,256,256]{2,1,0:T(8,128)(2,1)} fusion(bf16[192,256,256]{2,1,0:T(8,128)(2,1)} %gather_fusion, pred[192]{0:T(512)(128)(4,1)S(1)} %compare_and_fusion), kind=kLoop, calls=%fused_computation.1 | loop fusion | flops 12582912 | bytes 50331840 | tf_op jit(solution)/shard_map/jit(_take)/select_n | solution.py:852
  1141.1 32.7 %psum.15 = f32[2048]{0:T(1024)S(1)} all-reduce(f32[2048]{0:T(1024)S(1)} %copy-done.25), channel_id=1, replica_groups=mesh['head'=4,'seq'=8] {'seq'}, use_global_device_ids=true, to_apply=%region_26.27 | all-reduce | flops 2048 | bytes 16384 | tf_op jit(solution)/shard_map/psum | solution.py:839
  1176.7 9.6 reduce-scatter.12.cloned.1.call-done
  1189.1 246.5 %reduce-scatter.14.cloned.1.call-done = bf16[24,256,256]{2,1,0:T(8,128)(2,1)} async-done(((bf16[192,256,256]{2,1,0:T(8,128)(2,1)}), bf16[24,256,256]{2,1,0:T(8,128)(2,1)}) %reduce-scatter.14.cloned.1.call-update) | async-done | bytes 3145744 | tf_op jit(solution)/shard_map/reduce_scatter | solution.py:853
  1435.6 7.1 fusion.34
  1442.8 14.2 multiply_subtract_fusion
  1457.0 3.5 convert_element_type.113
  1460.5 4.1 add_multiply_fusion
  1464.6 3.7 add_multiply_fusion.1
  (166 shorter events, 66.8 us)
Async XLA Ops:
  7.2 58.0 %all-gather.11.cloned.1.call-start = ((), (), s32[]{:S(2)}) async-start(), calls=%async_computation.6 | async-start | bytes 5242880 | tf_op jit(solution)/shard_map/all_gather | solution.py:679
  7.9 124.2 %all-gather.9.cloned.1.call-start = ((), (), s32[]{:S(2)}) async-start(), calls=%async_computation.5 | async-start | bytes 7077888 | tf_op jit(solution)/shard_map/all_gather | solution.py:758
  10.0 280.8 %all-gather.13.cloned.1.call-start = ((), (), s32[]{:S(2)}) async-start(), calls=%async_computation.7 | async-start | bytes 2359296 | tf_op jit(solution)/shard_map/all_gather | solution.py:762
  10.8 344.7 %reduce-scatter.6.cloned.1.call-start = ((), (), s32[]{:S(2)}) async-start(), calls=%async_computation.8 | async-start | bytes 5242880 | tf_op jit(solution)/shard_map/reduce_scatter | solution.py:683
  12.6 129.5 %copy-start.26 = (s32[2,1]{0,1:T(1,128)}, s32[2,1]{0,1:T(1,128)S(1)}, u32[]{:S(2)}) copy-start(s32[2,1]{0,1:T(1,128)S(1)} %reduce-window.4) | copy-start | bytes 28
  213.7 2.7 copy-start
  297.1 58.3 %copy-start.3 = (bf16[256,2048]{1,0:T(8,128)(2,1)S(1)}, bf16[256,2048]{1,0:T(8,128)(2,1)}, u32[]{:S(2)}) copy-start(bf16[256,2048]{1,0:T(8,128)(2,1)} %param.24) | copy-start | bytes 3145732
  297.2 141.8 %all-gather.17.cloned.1.call-start = ((), (), s32[]{:S(2)}) async-start(), calls=%async_computation.10 | async-start | bytes 9437184 | tf_op jit(solution)/shard_map/all_gather | solution.py:763
  297.7 194.6 %all-gather.15.cloned.1.call-start = ((), (), s32[]{:S(2)}) async-start(), calls=%async_computation.9 | async-start | bytes 5242880 | tf_op jit(solution)/shard_map/all_gather | solution.py:679
  355.5 3.5 copy-start.4
  360.7 215.7 %all-gather.19.cloned.1.call-start = ((), (), s32[]{:S(2)}) async-start(), calls=%async_computation.11 | async-start | bytes 9437184 | tf_op jit(solution)/shard_map/all_gather | solution.py:764
  361.4 215.0 %copy-start.22 = (f32[2048]{0:T(1024)S(1)}, f32[2048]{0:T(1024)}, u32[]{:S(2)}) copy-start(f32[2048]{0:T(1024)} %param.37) | copy-start | bytes 24580
  361.4 281.9 %reduce-scatter.8.cloned.1.call-start = ((), (), s32[]{:S(2)}) async-start(), calls=%async_computation.12 | async-start | bytes 5242880 | tf_op jit(solution)/shard_map/reduce_scatter | solution.py:683
  592.4 53.5 %copy-start.11 = (bf16[256,2048]{1,0:T(8,128)(2,1)S(1)}, bf16[256,2048]{1,0:T(8,128)(2,1)}, u32[]{:S(2)}) copy-start(bf16[256,2048]{1,0:T(8,128)(2,1)} %param.25) | copy-start | bytes 3145732
  592.5 110.4 %all-gather.21.cloned.1.call-start = ((), (), s32[]{:S(2)}) async-start(), calls=%async_computation.13 | async-start | bytes 5242880 | tf_op jit(solution)/shard_map/all_gather | solution.py:679
  650.1 139.5 %reduce-scatter.10.cloned.1.call-start = ((), (), s32[]{:S(2)}) async-start(), calls=%async_computation.14 | async-start | bytes 5242880 | tf_op jit(solution)/shard_map/reduce_scatter | solution.py:683
  722.1 2.0 copy-start.31
  736.9 112.6 %all-gather.23.cloned.1.call-start = ((), (), s32[]{:S(2)}) async-start(), calls=%async_computation.15 | async-start | bytes 5242880 | tf_op jit(solution)/shard_map/all_gather | solution.py:679
  789.6 3.5 copy-start.5
  789.6 3.5 copy-start.12
  793.1 3.7 copy-start.27
  794.3 1.3 copy-start.6
  796.7 377.8 %all-reduce.2.cloned.1.call-start = ((), (), s32[]{:S(2)}) async-start(), calls=%async_computation.18 | async-start | bytes 131072 | tf_op jit(solution)/shard_map/psum | solution.py:840
  823.3 26.1 %copy-start.30 = (bf16[512,2048]{1,0:T(8,128)(2,1)S(1)}, bf16[512,2048]{1,0:T(8,128)(2,1)}, u32[]{:S(2)}) copy-start(bf16[512,2048]{1,0:T(8,128)(2,1)} %all-gather.13.cloned.1.call-done) | copy-start | bytes 6291460
  877.4 1.3 copy-start.1
  993.3 193.0 %reduce-scatter.12.cloned.1.call-start = ((), (), s32[]{:S(2)}) async-start(), calls=%async_computation.16 | async-start | bytes 5242880 | tf_op jit(solution)/shard_map/reduce_scatter | solution.py:683
  1004.6 431.0 %reduce-scatter.14.cloned.1.call-start = ((), (), s32[]{:S(2)}) async-start(), calls=%async_computation.17 | async-start | bytes 28311552 | tf_op jit(solution)/shard_map/reduce_scatter | solution.py:853
  1029.0 9.0 copy-start.13
  1029.0 9.0 copy-start.29
  1040.5 1.9 copy-start.8
  1040.5 3.2 copy-start.28
  1076.5 3.3 copy-start.10
  1076.5 4.8 copy-start.9
  1140.0 33.8 %copy-start.23 = (f32[2048]{0:T(1024)S(1)}, f32[2048]{0:T(1024)}, u32[]{:S(2)}) copy-start(f32[2048]{0:T(1024)} %param.40) | copy-start | bytes 24580
  1140.0 33.9 %copy-start.24 = (f32[2048]{0:T(1024)S(1)}, f32[2048]{0:T(1024)}, u32[]{:S(2)}) copy-start(f32[2048]{0:T(1024)} %param.41) | copy-start | bytes 24580
  1140.0 34.5 %copy-start.15 = (f32[6,2048]{1,0:T(8,128)S(1)}, f32[6,2048]{1,0:T(8,128)}, u32[]{:S(2)}) copy-start(f32[6,2048]{1,0:T(8,128)} %param.36) | copy-start | bytes 147460
  1140.0 34.5 %copy-start.17 = (f32[8,2048]{1,0:T(8,128)S(1)}, f32[8,2048]{1,0:T(8,128)}, u32[]{:S(2)}) copy-start(f32[8,2048]{1,0:T(8,128)} %param.38) | copy-start | bytes 196612
  1140.0 34.5 %copy-start.18 = (f32[8,2048]{1,0:T(8,128)S(1)}, f32[8,2048]{1,0:T(8,128)}, u32[]{:S(2)}) copy-start(f32[8,2048]{1,0:T(8,128)} %param.39) | copy-start | bytes 196612
  1140.0 34.5 %copy-start.20 = (f32[2,2048]{1,0:T(2,128)S(1)}, f32[2,2048]{1,0:T(2,128)}, u32[]{:S(2)}) copy-start(f32[2,2048]{1,0:T(2,128)} %param.35) | copy-start | bytes 49156
  1140.0 46.2 %copy-start.7 = (f32[256,2048]{1,0:T(8,128)S(1)}, f32[256,2048]{1,0:T(8,128)}, u32[]{:S(2)}) copy-start(f32[256,2048]{1,0:T(8,128)} %copy-done.6) | copy-start | bytes 6291460
  1173.8 268.9 %copy-start.21 = (f32[2048]{0:T(1024)}, f32[2048]{0:T(1024)S(1)}, u32[]{:S(2)}) copy-start(f32[2048]{0:T(1024)S(1)} %psum.15) | copy-start | bytes 24580
  1176.0 266.7 %copy-start.16 = (f32[8,2048]{1,0:T(8,128)}, f32[8,2048]{1,0:T(8,128)S(1)}, u32[]{:S(2)}) copy-start(f32[8,2048]{1,0:T(8,128)S(1)} %get-tuple-element.37) | copy-start | bytes 196612
  1435.6 24.8 %slice-start = ((s8[6291456]{0:T(1024)(128)(4,1)}), s8[4194304]{0:T(1024)(128)(4,1)S(1)}, s32[]{:S(2)}) async-start(s8[6291456]{0:T(1024)(128)(4,1)} %bitcast.131), calls=%async_computation.19 | async-start | bytes 8388608
  1442.8 14.2 copy-start.2
  1442.8 17.7 %slice-start.1 = ((s8[6291456]{0:T(1024)(128)(4,1)}), s8[2097152]{0:T(1024)(128)(4,1)S(1)}, s32[]{:S(2)}) async-start(s8[6291456]{0:T(1024)(128)(4,1)} %bitcast.131), calls=%async_computation.20 | async-start | bytes 4194304
  1457.0 7.6 slice-start.2
  1460.4 4.1 slice-start.3
  1464.6 3.7 copy-start.14
  (2 other events, 1.8 us)
Sparse Core Ops, SparseCore 0:
  9.8 55.2 all-gather.10
  67.4 64.6 all-gather.8
  133.7 69.8 all-gather.12
  297.3 58.1 reduce-scatter.5
  356.9 82.0 all-gather.16
  441.2 51.0 all-gather.14
  493.9 82.4 all-gather.18
  592.6 50.7 reduce-scatter.7
  650.2 52.5 all-gather.20
  737.0 52.5 reduce-scatter.9
  796.8 52.5 all-gather.22
  993.4 135.3 all-reduce.1
  1132.4 53.8 reduce-scatter.11
  1188.5 247.0 reduce-scatter.13

commit v2 on v1

--- a/solution.py
+++ b/solution.py
@@ -656,6 +656,332 @@
     )
 
 
+PAIR = 2
+DEPTH = 4
+
+
+def grads_kernel(spec, left_ref, right_ref, *refs):
+    chips, slots, left_strips, right_strips = spec
+    lefts, refs = refs[: len(left_strips)], refs[len(left_strips) :]
+    rights, refs = refs[: len(right_strips)], refs[len(right_strips) :]
+    (
+        out_ref,
+        left_buf,
+        right_buf,
+        strip_buf,
+        pair_out,
+        pair_in,
+        line_out,
+        line_in,
+        last_in,
+        own_sum,
+        load_sem,
+        pair_send,
+        pair_recv,
+        line_send,
+        line_recv,
+        last_recv,
+        pair_free,
+        line_free,
+    ) = refs
+    me = lax.axis_index("seq")
+    chip, core = me // PAIR, me % PAIR
+    sibling = chip * PAIR + (1 - core)
+    neighbours = ((chip + 1) * PAIR + core, (chip - 1) * PAIR + core)
+    has_next = (chip < chips - 1, chip > 0)
+
+    barrier = pltpu.get_barrier_semaphore()
+    pl.semaphore_signal(barrier, inc=1, device_id={"seq": sibling}, device_id_type=MESH)
+    for way in range(2):
+
+        @pl.when(has_next[way])
+        def _():
+            pl.semaphore_signal(
+                barrier, inc=1, device_id={"seq": neighbours[way]}, device_id_type=MESH
+            )
+
+    ends = (chip == 0).astype(jnp.int32) + (chip == chips - 1).astype(jnp.int32)
+    pl.semaphore_wait(barrier, 3 - ends)
+
+    def strip(source, index):
+        return source.at[:, pl.ds(pl.multiple_of(index * BLOCK, BLOCK), BLOCK)]
+
+    low = 0
+    for source, count in zip(rights, right_strips):
+
+        def load_right(index, carry, source=source, low=low):
+            pltpu.make_async_copy(
+                strip(source, index), right_buf.at[low + index], load_sem.at[2]
+            ).start()
+            return carry
+
+        lax.fori_loop(0, count, load_right, 0)
+        low += count
+    rows = left_buf.shape[2]
+    low = 0
+    for source, count in zip(lefts, left_strips):
+
+        def fetch(index, slot, source=source):
+            return pltpu.make_async_copy(strip(source, index), strip_buf.at[slot], load_sem.at[slot])
+
+        def turn_strip(index, carry, count=count, low=low, fetch=fetch):
+            slot = index % 2
+
+            @pl.when(index + 1 < count)
+            def _():
+                fetch(index + 1, 1 - slot).start()
+
+            fetch(index, slot).wait()
+            for part in range(rows // BLOCK):
+                span = pl.ds(part * BLOCK, BLOCK)
+                left_buf[low + index, :, span] = strip_buf[slot, span, :].T
+            return carry
+
+        fetch(0, 0).start()
+        lax.fori_loop(0, count, turn_strip, 0)
+        low += count
+    low = 0
+    for source, count in zip(rights, right_strips):
+
+        def wait_right(index, carry, source=source, low=low):
+            pltpu.make_async_copy(
+                strip(source, index), right_buf.at[low + index], load_sem.at[2]
+            ).wait()
+            return carry
+
+        lax.fori_loop(0, count, wait_right, 0)
+        low += count
+
+    def product(owner_chip, owner_core, k):
+        slot = (owner_chip * PAIR + owner_core) * slots + k
+        return nn(left_buf[left_ref[slot]], right_buf[right_ref[slot]])
+
+    counts = ((chips - 1 - chip) * slots, chip * slots, slots)
+
+    def owner(stream, step):
+        if stream == 0:
+            return chips - 1 - step // slots
+        if stream == 1:
+            return step // slots
+        return chip
+
+    def pair_copy(stream, step):
+        slot = step % DEPTH
+        return pltpu.make_async_remote_copy(
+            src_ref=pair_out.at[stream, slot],
+            dst_ref=pair_in.at[stream, slot],
+            send_sem=pair_send.at[stream, slot],
+            recv_sem=pair_recv.at[stream, slot],
+            device_id={"seq": sibling},
+            device_id_type=MESH,
+        )
+
+    def line_copy(stream, step):
+        slot = step % DEPTH
+        return pltpu.make_async_remote_copy(
+            src_ref=line_out.at[stream, slot],
+            dst_ref=line_in.at[stream, slot],
+            send_sem=line_send.at[stream, slot],
+            recv_sem=line_recv.at[stream, slot],
+            device_id={"seq": neighbours[stream]},
+            device_id_type=MESH,
+        )
+
+    def last_copy(stream, step):
+        slot, k = step % DEPTH, step % slots
+        return pltpu.make_async_remote_copy(
+            src_ref=line_out.at[stream, slot],
+            dst_ref=last_in.at[stream, k],
+            send_sem=line_send.at[stream, slot],
+            recv_sem=last_recv.at[stream, k],
+            device_id={"seq": neighbours[stream]},
+            device_id_type=MESH,
+        )
+
+    def give(stream, step):
+        slot = step % DEPTH
+
+        @pl.when(step >= DEPTH)
+        def _():
+            pair_copy(stream, step).wait_send()
+            pl.semaphore_wait(pair_free.at[stream], 1)
+
+        pair_out[stream, slot] = product(owner(stream, step), 1 - core, step % slots).astype(
+            jnp.bfloat16
+        )
+        pair_copy(stream, step).start()
+
+    def take(stream, step):
+        slot = step % DEPTH
+        total = product(owner(stream, step), core, step % slots)
+        pair_copy(stream, step).wait_recv()
+        total = total + pair_in[stream, slot].astype(jnp.float32)
+
+        @pl.when(step + DEPTH < counts[stream])
+        def _():
+            pl.semaphore_signal(
+                pair_free.at[stream], inc=1, device_id={"seq": sibling}, device_id_type=MESH
+            )
+
+        return total
+
+    def forward(stream, step):
+        slot = step % DEPTH
+        target = chip + 1 if stream == 0 else chip - 1
+        ends_there = owner(stream, step) == target
+        has_source = has_next[1 - stream]
+        total = take(stream, step)
+
+        @pl.when(step >= DEPTH)
+        def _():
+            line_copy(stream, step).wait_send()
+
+        @pl.when(has_source)
+        def _():
+            line_copy(stream, step).wait_recv()
+            line_out[stream, slot] = (total + line_in[stream, slot].astype(jnp.float32)).astype(
+                jnp.bfloat16
+            )
+
+            @pl.when(step + DEPTH < counts[stream])
+            def _():
+                pl.semaphore_signal(
+                    line_free.at[stream],
+                    inc=1,
+                    device_id={"seq": neighbours[1 - stream]},
+                    device_id_type=MESH,
+                )
+
+        @pl.when(jnp.logical_not(has_source))
+        def _():
+            line_out[stream, slot] = total.astype(jnp.bfloat16)
+
+        @pl.when(ends_there)
+        def _():
+            last_copy(stream, step).start()
+
+        @pl.when(jnp.logical_not(ends_there))
+        def _():
+            @pl.when(step >= DEPTH)
+            def _():
+                pl.semaphore_wait(line_free.at[stream], 1)
+
+            line_copy(stream, step).start()
+
+    def keep(step):
+        own_sum[step] = take(2, step).astype(jnp.bfloat16)
+
+    for stream in range(2):
+        pl.when(counts[stream] > 0)(functools.partial(give, stream, 0))
+
+    def body(step, carry):
+        for stream in range(2):
+            pl.when(step + 1 < counts[stream])(functools.partial(give, stream, step + 1))
+        own_step = step - slots
+
+        @pl.when((own_step + 1 >= 0) & (own_step + 1 < slots))
+        def _():
+            give(2, own_step + 1)
+
+        for stream in range(2):
+            pl.when(step < counts[stream])(functools.partial(forward, stream, step))
+
+        @pl.when((own_step >= 0) & (own_step < slots))
+        def _():
+            keep(own_step)
+
+        return carry
+
+    lax.fori_loop(0, (chips - 1) * slots, body, 0)
+
+    def finish(k, carry):
+        out_ref[k] = own_sum[k]
+        for stream in range(2):
+
+            @pl.when(has_next[1 - stream])
+            def _():
+                last_copy(stream, k).wait_recv()
+                out_ref[k] = (
+                    out_ref[k].astype(jnp.float32) + last_in[stream, k].astype(jnp.float32)
+                ).astype(jnp.bfloat16)
+
+        return carry
+
+    lax.fori_loop(0, slots, finish, 0)
+    for slot in range(DEPTH):
+        for stream in range(2):
+
+            @pl.when(counts[stream] > 0)
+            def _():
+                line_copy(stream, slot).wait_send()
+                pair_copy(stream, slot).wait_send()
+
+        pair_copy(2, slot).wait_send()
+
+
+def owned_grads(left_index, right_index, lefts, rights, seq_size, collective_id):
+    rows = lefts[0].shape[0]
+    left_strips = tuple(array.shape[1] // BLOCK for array in lefts)
+    right_strips = tuple(array.shape[1] // BLOCK for array in rights)
+    chips = seq_size // PAIR
+    slots = left_index.shape[0] // seq_size
+    kind = jnp.bfloat16
+    block = (BLOCK, BLOCK)
+    products = chips * PAIR * slots
+    return pl.pallas_call(
+        functools.partial(grads_kernel, (chips, slots, left_strips, right_strips)),
+        out_shape=jax.ShapeDtypeStruct((slots,) + block, kind),
+        in_specs=[IN_SMEM] * 2 + [ANY] * (len(lefts) + len(rights)),
+        out_specs=IN_VMEM,
+        scratch_shapes=[
+            pltpu.VMEM((sum(left_strips), BLOCK, rows), kind),
+            pltpu.VMEM((sum(right_strips), rows, BLOCK), kind),
+            pltpu.VMEM((2, rows, BLOCK), kind),
+            pltpu.VMEM((3, DEPTH) + block, kind),
+            pltpu.VMEM((3, DEPTH) + block, kind),
+            pltpu.VMEM((2, DEPTH) + block, kind),
+            pltpu.VMEM((2, DEPTH) + block, kind),
+            pltpu.VMEM((2, slots) + block, kind),
+            pltpu.VMEM((slots,) + block, kind),
+            pltpu.SemaphoreType.DMA((3,)),
+            pltpu.SemaphoreType.DMA((3, DEPTH)),
+            pltpu.SemaphoreType.DMA((3, DEPTH)),
+            pltpu.SemaphoreType.DMA((2, DEPTH)),
+            pltpu.SemaphoreType.DMA((2, DEPTH)),
+            pltpu.SemaphoreType.DMA((2, slots)),
+            pltpu.SemaphoreType.REGULAR((3,)),
+            pltpu.SemaphoreType.REGULAR((2,)),
+        ],
+        compiler_params=pltpu.CompilerParams(
+            collective_id=collective_id, has_side_effects=True, vmem_limit_bytes=VMEM_MOST
+        ),
+        cost_estimate=pl.CostEstimate(
+            flops=products * 2 * rows * BLOCK * BLOCK,
+            bytes_accessed=2 * (sum(left_strips) + sum(right_strips)) * rows * BLOCK,
+            transcendentals=0,
+        ),
+        name="owned_grads",
+    )(left_index, right_index, *lefts, *rights)
+
+
+def block_operands(own_map, width, panel_width, ff_width):
+    deep, narrow, wide = width // BLOCK, panel_width // BLOCK, ff_width // BLOCK
+    left = jnp.zeros_like(own_map)
+    right = jnp.zeros_like(own_map)
+    first, left_low, right_low = 0, 0, 0
+    panels = [(deep, narrow, 0, 0), (deep, narrow, 0, narrow), (deep, narrow, 0, 2 * narrow)]
+    panels.append((narrow, deep, deep, 3 * narrow))
+    panels.append((deep, wide, deep + narrow, 3 * narrow + deep))
+    panels.append((wide, deep, 2 * deep + narrow, 3 * narrow + deep + wide))
+    for high, broad, left_low, right_low in panels:
+        inside = (own_map >= first) & (own_map < first + high * broad)
+        within = own_map - first
+        left = jnp.where(inside, left_low + within // broad, left)
+        right = jnp.where(inside, right_low + within % broad, right)
+        first += high * broad
+    return left.astype(jnp.int32), right.astype(jnp.int32)
+
+
 def normalize(z_rows, gain, shift):
     average = jnp.mean(z_rows, axis=-1, keepdims=True)
     centered = z_rows - average
@@ -683,18 +1009,6 @@
     return lax.psum_scatter(
         partial_value.astype(jnp.bfloat16), "head", scatter_dimension=0, tiled=True
     ).astype(jnp.float32)
-
-
-def to_blocks(panel):
-    height, breadth = panel.shape
-    shaped = panel.reshape(height // BLOCK, BLOCK, breadth // BLOCK, BLOCK)
-    return shaped.transpose(0, 2, 1, 3).reshape(-1, BLOCK, BLOCK)
-
-
-def weight_grad(rows, grads):
-    return lax.dot_general(
-        rows, grads, (((0,), (0,)), ((), ())), preferred_element_type=jnp.float32
-    ).astype(jnp.bfloat16)
 
 
 def adam_step(param, grad, moment, second, step_float):
@@ -812,10 +1126,6 @@
     input_grad = dz_one + group_sums(
         jnp.dot(dqkv_grp, qkv_panel.T, preferred_element_type=jnp.float32)
     )
-    grad_down = weight_grad(act, dz_two_grp)
-    grad_up = weight_grad(h_grp, dpre)
-    grad_out = weight_grad(attended_grp, dz_one_grp)
-    grad_qkv = weight_grad(inputs_grp, dqkv_grp)
     bias_qkv = jnp.sum(dqkv_grp.astype(jnp.float32), axis=0)
     zero_width = jnp.zeros((width,), jnp.float32)
     dbias_query = lax.dynamic_update_slice_in_dim(
@@ -838,19 +1148,15 @@
     )
     up_bias_grad = lax.psum(up_bias_part, "seq")
     vector_grad = lax.psum(local_vectors, ("head", "seq"))
-    canon = jnp.concatenate(
-        [
-            to_blocks(grad_qkv[:, :panel_width]),
-            to_blocks(grad_qkv[:, panel_width : 2 * panel_width]),
-            to_blocks(grad_qkv[:, 2 * panel_width :]),
-            to_blocks(grad_out),
-            to_blocks(grad_up),
-            to_blocks(grad_down),
-        ],
-        axis=0,
-    )
-    ordered = jnp.take(canon, own_map[0], axis=0)
-    low_grads = lax.psum_scatter(ordered, "seq", scatter_dimension=0, tiled=True)
+    left_index, right_index = block_operands(own_map[0], width, panel_width, ff_width)
+    low_grads = owned_grads(
+        left_index,
+        right_index,
+        (inputs_grp, attended_grp, h_grp, act),
+        (dqkv_grp, dz_one_grp, dpre, dz_two_grp),
+        seq_size,
+        4,
+    )
     block_grads = low_grads.astype(jnp.float32)
     stat_left_new = 0.5 * stat_left + 0.5 * jnp.einsum(
         "bij,bkj->bik", low_grads, low_grads, preferred_element_type=jnp.float32

time: 1480 us -> 1520 us (1.027)
  Pallas kernels: 281 us -> 707 us
  waiting for transfers between devices: 802 us -> 584 us
  local copies, waits for them, and re-layouts: 122 us -> 10.5 us
  matrix products: 164 us -> 122 us
  other arithmetic: 56.4 us -> 36.1 us
    pallas_call x0 -> x1, Pallas kernels: none -> 426 us  [owned_grads(): pl.pallas_call(functools.partial(grads_kernel, (chips, slots, left_strips...]
    reduce_scatter x1 -> x0, waiting for transfers between devices: 247 us -> none  [shards(): lax.psum_scatter(ordered, 'seq', scatter_dimension=0, tiled=True)]
    unnamed x84 -> x67, local copies, waits for them, and re-layouts: 55.9 us -> 8.13 us
    dot_general x4 -> x0, matrix products: 40.3 us -> none  [weight_grad(): lax.dot_general(rows, grads, (((0,), (0,)), ((), ())), preferred_element_...]
    all_gather x4, waiting for transfers between devices: 170 us -> 210 us  [group_rows(): return lax.all_gather(rows_low, 'head', axis=0, tiled=True)]
    reshape x6 -> x0, local copies, waits for them, and re-layouts: 32.1 us -> none  [to_blocks(): shaped = panel.reshape(height // BLOCK, BLOCK, breadth // BLOCK, BLOCK)]
    select_n x2 -> x1, other arithmetic: 21.1 us -> 0.59 us  [block_operands(): right = jnp.where(inside, right_low + within % broad, right)]
    gather x1 -> x0, local copies, waits for them, and re-layouts: 19.4 us -> none  [shards(): ordered = jnp.take(canon, own_map[0], axis=0)]
  transfers between devices with their start and end apart: 14 -> 13, of which waited for: 12 -> 10; matrix products, arithmetic and copies ran while one was open for 15% -> 6% of each run, Pallas kernels for 10% -> 38%
where the time goes in v2:
time: 1520 us; the launch traced here: 1510 us
  Pallas kernels  707 us (47%)
  waiting for transfers between devices  584 us (38%)
  matrix products  122 us (8%)
  other arithmetic  36.1 us (2%)
  blocking collectives  32.6 us (2%)
  between operations  15.6 us (1%)
    pallas_call x1, Pallas kernels, owned_grads(): pl.pallas_call(functools.partial(grads_kernel, (chips, slots, left_strips...  426 us
    all_gather x4, waiting for transfers between devices, group_rows(): return lax.all_gather(rows_low, 'head', axis=0, tiled=True)  210 us
    reduce_scatter x4, waiting for transfers between devices, group_sums(): lax.psum_scatter(partial_value.astype(jnp.bfloat16), 'head', scatter_dime...  160 us
    pallas_call x2, Pallas kernels, collect(): pl.pallas_call(functools.partial(collect_kernel, fields, heads, parts), o...  100 us
    pallas_call x2, Pallas kernels, spread(): pl.pallas_call(functools.partial(spread_kernel, fields, heads, parts), ou...  95 us
    all_gather x1, waiting for transfers between devices, shards(): up_panel = lax.all_gather(w_up, 'seq', axis=0, tiled=True)  77 us
    all_gather x1, waiting for transfers between devices, shards(): down_panel = lax.all_gather(w_down, 'seq', axis=1, tiled=True)  67.4 us
    all_gather x1, waiting for transfers between devices, shards(): lax.all_gather(jnp.concatenate([w_query, w_key, w_value], axis=1), 'seq',...  66.9 us
  transfers between devices with their start and end apart: 13, of which 10 were waited for; matrix products, arithmetic and copies ran while one was open for 6% of the time, Pallas kernels for 38%

profile of v2, /device:TPU:0, one launch (start us, length us, event | category | flops | bytes accessed | tf_op | source)
XLA Modules:
  0.0 1508.6 jit_solution(5871337557736303956)
XLA Ops:
  8.0 2.0 pad_maximum_fusion
  12.8 1.2 and_select_fusion.12
  14.0 51.3 %all-gather.11.cloned.1.call-done.refs_0_ = bf16[1024,2048]{1,0:T(8,128)(2,1)} async-done(((bf16[256,2048]{1,0:T(8,128)(2,1)}), bf16[1024,2048]{1,0:T(8,128)(2,1)}) %all-gather.11.cloned.1.call-update) | async-done | bytes 4194320 | tf_op jit(solution)/shard_map/all_gather | solution.py:1005
  65.2 66.9 %all-gather.9.cloned.1.call-done = bf16[2048,1536]{1,0:T(8,128)(2,1)} async-done(((bf16[256,1536]{1,0:T(8,128)(2,1)}), bf16[2048,1536]{1,0:T(8,128)(2,1)}) %all-gather.9.cloned.1.call-update) | async-done | bytes 6291472 | tf_op jit(solution)/shard_map/all_gather | solution.py:1072
  132.2 10.0 fusion.7.x_ref
  142.2 71.6 %spread.2 = bf16[3,8,1024,128]{3,2,1,0:T(8,128)(2,1)S(1)} custom-call(bf16[1024,1536]{1,0:T(8,128)(2,1)S(1)} %fusion.7.x_ref), custom_call_target="tpu_custom_call" | custom-call | tf_op jit(solution)/shard_map/spread/pallas_call | solution.py:111
  213.8 2.7 copy-done
  216.5 35.8 %attend_forward.1 = (bf16[32,256,128]{2,1,0:T(8,128)(2,1)}, f32[16,256,128]{2,1,0:T(8,128)}, f32[16,1,256]{2,1,0:T(1,128)}) custom-call(s32[32]{0:T(128)} %select_reduce_fusion.where_ref, s32[32]{0:T(128)} %get-tuple-element.64.low_ref, s32[32]{0:T(128)} %get-tuple-element.63.high_ref, s32[2]{0:T(128)} %bitcast.94, s32[1]{0:T(128)} %bitcast.4.part_ref, ...), custom_call_target="tpu_custom_call" | custom-call | tf_op jit(solution)/shard_map/attend_forward/pallas_call | solution.py:381
  252.3 38.6 %collect.2.refs_1_ = bf16[1024,512]{1,0:T(8,128)(2,1)} custom-call(bf16[1,8,1024,128]{3,2,1,0:T(8,128)(2,1)} %bitcast.65), custom_call_target="tpu_custom_call" | custom-call | tf_op jit(solution)/shard_map/collect/pallas_call | solution.py:211
  290.9 6.3 convolution_convert_fusion.3
  297.9 57.6 %reduce-scatter.5.cloned.1.call-done = bf16[256,2048]{1,0:T(8,128)(2,1)} async-done(((bf16[1024,2048]{1,0:T(8,128)(2,1)}), bf16[256,2048]{1,0:T(8,128)(2,1)}) %reduce-scatter.5.cloned.1.call-update) | async-done | bytes 1048592 | tf_op jit(solution)/shard_map/reduce_scatter | solution.py:1009
  355.5 1.7 fusion.12
  357.3 1.8 multiply_reduce_fusion.5
  359.1 1.6 fusion.11
  362.0 77.0 %all-gather.17.cloned.1.call-done = bf16[2048,2048]{1,0:T(8,128)(2,1)} async-done(((bf16[256,2048]{1,0:T(8,128)(2,1)}), bf16[2048,2048]{1,0:T(8,128)(2,1)}) %all-gather.17.cloned.1.call-update) | async-done | bytes 8388624 | tf_op jit(solution)/shard_map/all_gather | solution.py:1077
  439.0 53.4 %all-gather.15.cloned.1.call-done.refs_2_ = bf16[1024,2048]{1,0:T(8,128)(2,1)} async-done(((bf16[256,2048]{1,0:T(8,128)(2,1)}), bf16[1024,2048]{1,0:T(8,128)(2,1)}) %all-gather.15.cloned.1.call-update) | async-done | bytes 4194320 | tf_op jit(solution)/shard_map/all_gather | solution.py:1005
  492.4 16.7 %multiply_convert_fusion = (bf16[1024,2048]{1,0:T(8,128)(2,1)}, f32[1024,2048]{1,0:T(8,128)}) fusion(f32[2048]{0:T(1024)S(1)} %copy-done.21, bf16[1024,2048]{1,0:T(8,128)(2,1)} %all-gather.15.cloned.1.call-done.refs_2_, bf16[2048,2048]{1,0:T(8,128)(2,1)} %all-gather.17.cloned.1.call-done), kind=kOutput, calls=%fused_computation.10 | convolution fusion | flops 8610906112 | bytes 25174016 | tf_op jit(solution)/shard_map/dot_general | solution.py:1100
  509.1 67.4 %all-gather.19.cloned.1.call-done = bf16[2048,2048]{1,0:T(8,128)(2,1)} async-done(((bf16[2048,256]{1,0:T(8,128)(2,1)}), bf16[2048,2048]{1,0:T(8,128)(2,1)}) %all-gather.19.cloned.1.call-update) | async-done | bytes 8388624 | tf_op jit(solution)/shard_map/all_gather | solution.py:1078
  576.5 13.8 convolution_convert_fusion.2
  591.1 50.2 %reduce-scatter.7.cloned.1.call-done = bf16[256,2048]{1,0:T(8,128)(2,1)} async-done(((bf16[1024,2048]{1,0:T(8,128)(2,1)}), bf16[256,2048]{1,0:T(8,128)(2,1)}) %reduce-scatter.7.cloned.1.call-update) | async-done | bytes 1048592 | tf_op jit(solution)/shard_map/reduce_scatter | solution.py:1009
  641.2 2.3 fusion.41
  645.0 3.0 fusion.40
  648.3 52.5 %all-gather.21.cloned.1.call-done.refs_7_ = bf16[1024,2048]{1,0:T(8,128)(2,1)} async-done(((bf16[256,2048]{1,0:T(8,128)(2,1)}), bf16[1024,2048]{1,0:T(8,128)(2,1)}) %all-gather.21.cloned.1.call-update) | async-done | bytes 4194320 | tf_op jit(solution)/shard_map/all_gather | solution.py:1005
  700.8 18.6 %convert_reduce_fusion = (f32[2048]{0:T(1024)S(1)}, bf16[1024,2048]{1,0:T(8,128)(2,1)S(1)}) fusion(f32[1024,2048]{1,0:T(8,128)} %get-tuple-element.60, f32[2048]{0:T(1024)S(1)} %copy-done.21, bf16[1024,2048]{1,0:T(8,128)(2,1)} %all-gather.21.cloned.1.call-done.refs_7_, bf16[2048,2048]{1,0:T(8,128)(2,1)} %all-gather.19.cloned.1.call-done), kind=kOutput, calls=%fused_computation.9 | convolution fusion | flops 8638167040 | bytes 25182208 | tf_op jit(solution)/shard_map/dot_general | solution.py:1110
  719.4 2.0 copy-done.28
  721.4 12.8 convolution_convert_fusion.1
  734.5 52.5 %reduce-scatter.9.cloned.1.call-done = bf16[256,2048]{1,0:T(8,128)(2,1)} async-done(((bf16[1024,2048]{1,0:T(8,128)(2,1)}), bf16[256,2048]{1,0:T(8,128)(2,1)}) %reduce-scatter.9.cloned.1.call-update) | async-done | bytes 1048592 | tf_op jit(solution)/shard_map/reduce_scatter | solution.py:1009
  787.0 3.4 multiply_reduce_fusion.1
  790.5 1.1 fusion.39
  791.6 1.3 copy-done.6
  792.9 1.1 convert_element_type.89
  794.1 52.7 %all-gather.23.cloned.1.call-done.refs_5_ = bf16[1024,2048]{1,0:T(8,128)(2,1)} async-done(((bf16[256,2048]{1,0:T(8,128)(2,1)}), bf16[1024,2048]{1,0:T(8,128)(2,1)}) %all-gather.23.cloned.1.call-update) | async-done | bytes 4194320 | tf_op jit(solution)/shard_map/all_gather | solution.py:1005
  846.8 4.5 convolution_convert_fusion.4.x_ref
  851.3 23.4 %spread.3 = bf16[1,8,1024,128]{3,2,1,0:T(8,128)(2,1)S(1)} custom-call(bf16[1024,512]{1,0:T(8,128)(2,1)S(1)} %convolution_convert_fusion.4.x_ref), custom_call_target="tpu_custom_call" | custom-call | tf_op jit(solution)/shard_map/spread/pallas_call | solution.py:111
  874.8 1.3 copy-done.1
  876.1 49.7 %attend_backward.1 = bf16[3,32,256,128]{3,2,1,0:T(8,128)(2,1)} custom-call(s32[32]{0:T(128)} %select_reduce_fusion.where_ref, s32[32]{0:T(128)} %get-tuple-element.64.low_ref, s32[32]{0:T(128)} %get-tuple-element.63.high_ref, s32[2]{0:T(128)} %bitcast.95, s32[1]{0:T(128)} %bitcast.4.part_ref, bf16[3,32,256,128]{3,2,1,0:T(8,128)(2,1)} %bitcast.58, ...), custom_call_target="tpu_custom_call" | custom-call | tf_op jit(solution)/shard_map/attend_backward/pallas_call | solution.py:602
  925.8 61.6 %collect.3.refs_4_ = bf16[1024,1536]{1,0:T(8,128)(2,1)} custom-call(bf16[3,8,1024,128]{3,2,1,0:T(8,128)(2,1)} %bitcast.60), custom_call_target="tpu_custom_call" | custom-call | tf_op jit(solution)/shard_map/collect/pallas_call | solution.py:211
  987.4 2.5 convert_reduce_fusion.1
  990.9 11.0 convolution_convert_fusion
  1003.3 32.6 %psum.15 = f32[2048]{0:T(1024)S(1)} all-reduce(f32[2048]{0:T(1024)S(1)} %get-tuple-element.35), channel_id=1, replica_groups=mesh['head'=4,'seq'=8] {'seq'}, use_global_device_ids=true, to_apply=%region_25.26 | all-reduce | flops 2048 | bytes 16384 | tf_op jit(solution)/shard_map/psum | solution.py:1149
  1036.5 425.9 %owned_grads.1 = bf16[24,256,256]{2,1,0:T(8,128)(2,1)} custom-call(s32[192]{0:T(256)} %get-tuple-element.58.left_ref, s32[192]{0:T(256)} %get-tuple-element.57.right_ref, bf16[1024,2048]{1,0:T(8,128)(2,1)} %all-gather.11.cloned.1.call-done.refs_0_, bf16[1024,512]{1,0:T(8,128)(2,1)} %collect.2.refs_1_, ...), custom_call_target="tpu_custom_call" | custom-call | flops 25769803776 | bytes 29360128 | tf_op jit(solution)/shard_map/owned_grads/pallas_call | solution.py:931
  1462.5 5.5 convert_element_type.93
  1468.0 5.6 fusion.45
  1473.6 3.9 add_multiply_fusion.1
  1477.5 4.1 add_multiply_fusion
  1481.7 14.2 multiply_subtract_fusion
  1495.9 1.6 maximum_subtract_fusion
  1498.2 2.8 convert_add_fusion
  (131 shorter events, 11.7 us)
Async XLA Ops:
  7.2 3.7 copy-start.19
  7.2 4.0 copy-start.27
  7.2 4.8 copy-start.12
  7.2 58.0 %all-gather.11.cloned.1.call-start = ((), (), s32[]{:S(2)}) async-start(), calls=%async_computation.5 | async-start | bytes 5242880 | tf_op jit(solution)/shard_map/all_gather | solution.py:1005
  7.9 124.2 %all-gather.9.cloned.1.call-start = ((), (), s32[]{:S(2)}) async-start(), calls=%async_computation.4 | async-start | bytes 7077888 | tf_op jit(solution)/shard_map/all_gather | solution.py:1072
  10.1 280.8 %all-gather.13.cloned.1.call-start = ((), (), s32[]{:S(2)}) async-start(), calls=%async_computation.6 | async-start | bytes 2359296 | tf_op jit(solution)/shard_map/all_gather | solution.py:1076
  10.8 344.7 %reduce-scatter.5.cloned.1.call-start = ((), (), s32[]{:S(2)}) async-start(), calls=%async_computation.7 | async-start | bytes 5242880 | tf_op jit(solution)/shard_map/reduce_scatter | solution.py:1009
  11.4 130.8 %copy-start.24 = (s32[2,1]{0,1:T(1,128)}, s32[2,1]{0,1:T(1,128)S(1)}, u32[]{:S(2)}) copy-start(s32[2,1]{0,1:T(1,128)S(1)} %reduce-window.4) | copy-start | bytes 28
  213.8 2.7 copy-start
  297.2 0.7 copy-start.17
  297.2 58.3 %copy-start.3 = (bf16[256,2048]{1,0:T(8,128)(2,1)S(1)}, bf16[256,2048]{1,0:T(8,128)(2,1)}, u32[]{:S(2)}) copy-start(bf16[256,2048]{1,0:T(8,128)(2,1)} %param.24) | copy-start | bytes 3145732
  297.2 141.8 %all-gather.17.cloned.1.call-start = ((), (), s32[]{:S(2)}) async-start(), calls=%async_computation.9 | async-start | bytes 9437184 | tf_op jit(solution)/shard_map/all_gather | solution.py:1077
  297.8 194.6 %all-gather.15.cloned.1.call-start = ((), (), s32[]{:S(2)}) async-start(), calls=%async_computation.8 | async-start | bytes 5242880 | tf_op jit(solution)/shard_map/all_gather | solution.py:1005
  355.5 3.6 copy-start.4
  359.0 133.4 %copy-start.21 = (f32[2048]{0:T(1024)S(1)}, f32[2048]{0:T(1024)}, u32[]{:S(2)}) copy-start(f32[2048]{0:T(1024)} %param.37) | copy-start | bytes 24580
  360.7 215.8 %all-gather.19.cloned.1.call-start = ((), (), s32[]{:S(2)}) async-start(), calls=%async_computation.10 | async-start | bytes 9437184 | tf_op jit(solution)/shard_map/all_gather | solution.py:1078
  361.5 279.7 %reduce-scatter.7.cloned.1.call-start = ((), (), s32[]{:S(2)}) async-start(), calls=%async_computation.11 | async-start | bytes 5242880 | tf_op jit(solution)/shard_map/reduce_scatter | solution.py:1009
  590.3 110.5 %all-gather.21.cloned.1.call-start = ((), (), s32[]{:S(2)}) async-start(), calls=%async_computation.12 | async-start | bytes 5242880 | tf_op jit(solution)/shard_map/all_gather | solution.py:1005
  641.2 2.7 copy-start.9
  648.1 138.9 %reduce-scatter.9.cloned.1.call-start = ((), (), s32[]{:S(2)}) async-start(), calls=%async_computation.13 | async-start | bytes 5242880 | tf_op jit(solution)/shard_map/reduce_scatter | solution.py:1009
  719.4 2.0 copy-start.28
  734.2 112.6 %all-gather.23.cloned.1.call-start = ((), (), s32[]{:S(2)}) async-start(), calls=%async_computation.14 | async-start | bytes 5242880 | tf_op jit(solution)/shard_map/all_gather | solution.py:1005
  787.0 3.5 copy-start.5
  787.0 3.5 copy-start.10
  791.6 1.3 copy-start.6
  791.6 55.2 %copy-start.26 = (bf16[512,2048]{1,0:T(8,128)(2,1)S(1)}, bf16[512,2048]{1,0:T(8,128)(2,1)}, u32[]{:S(2)}) copy-start(bf16[512,2048]{1,0:T(8,128)(2,1)} %all-gather.13.cloned.1.call-done) | copy-start | bytes 6291460
  794.1 701.8 %all-reduce.2.cloned.1.call-start = ((), (), s32[]{:S(2)}) async-start(), calls=%async_computation.16 | async-start | bytes 131072 | tf_op jit(solution)/shard_map/psum | solution.py:1150
  874.8 1.3 copy-start.1
  987.4 3.4 copy-start.8
  990.8 507.4 %reduce-scatter.11.cloned.1.call-start = ((), (), s32[]{:S(2)}) async-start(), calls=%async_computation.15 | async-start | bytes 5242880 | tf_op jit(solution)/shard_map/reduce_scatter | solution.py:1009
  1001.9 0.8 copy-start.25
  1001.9 34.0 %copy-start.22 = (f32[2048]{0:T(1024)S(1)}, f32[2048]{0:T(1024)}, u32[]{:S(2)}) copy-start(f32[2048]{0:T(1024)} %param.40) | copy-start | bytes 24580
  1001.9 34.0 %copy-start.23 = (f32[2048]{0:T(1024)S(1)}, f32[2048]{0:T(1024)}, u32[]{:S(2)}) copy-start(f32[2048]{0:T(1024)} %param.41) | copy-start | bytes 24580
  1035.9 426.6 %copy-start.20 = (f32[2048]{0:T(1024)}, f32[2048]{0:T(1024)S(1)}, u32[]{:S(2)}) copy-start(f32[2048]{0:T(1024)S(1)} %psum.15) | copy-start | bytes 24580
  1462.5 5.5 copy-start.2
  1462.5 11.1 slice-start
  1468.0 5.6 slice-start.1
  1468.0 9.5 slice-start.2
  1473.6 3.9 slice-start.3
  1481.7 14.2 copy-start.13
  1481.7 14.2 copy-start.15
  1481.7 14.2 copy-start.16
  1481.7 14.2 copy-start.18
  1481.7 16.5 %copy-start.7 = (f32[256,2048]{1,0:T(8,128)S(1)}, f32[256,2048]{1,0:T(8,128)}, u32[]{:S(2)}) copy-start(f32[256,2048]{1,0:T(8,128)} %copy-done.6) | copy-start | bytes 6291460
  1495.9 5.0 copy-start.11
  1497.5 4.1 copy-start.14
Sparse Core Ops, SparseCore 0:
  9.9 55.3 all-gather.10
  67.4 64.6 all-gather.8
  133.8 69.8 all-gather.12
  297.3 58.1 reduce-scatter.4
  357.0 82.0 all-gather.16
  441.3 51.0 all-gather.14
  494.0 82.4 all-gather.18
  590.4 50.7 reduce-scatter.6
  648.2 52.5 all-gather.20
  734.3 52.5 reduce-scatter.8
  794.2 52.5 all-gather.22
  990.9 135.4 all-reduce.1
  1129.4 53.7 reduce-scatter.10

commit v3 on v2

--- a/solution.py
+++ b/solution.py
@@ -22,6 +22,12 @@
 ANY = pl.BlockSpec(memory_space=pl.ANY)
 IN_SMEM = pl.BlockSpec(memory_space=pltpu.SMEM)
 IN_VMEM = pl.BlockSpec(memory_space=pltpu.VMEM)
+
+
+def busy(microseconds):
+    return pl.CostEstimate(
+        flops=microseconds * 800_000_000, bytes_accessed=1_000_000, transcendentals=0
+    )
 
 
 def seq_barrier(me, heads, parts):
@@ -123,6 +129,7 @@
         compiler_params=pltpu.CompilerParams(
             collective_id=collective_id, has_side_effects=True, vmem_limit_bytes=24 * 1024 * 1024
         ),
+        cost_estimate=busy(fields * 24),
         name="spread",
     )(x_rows)
 
@@ -227,6 +234,7 @@
         compiler_params=pltpu.CompilerParams(
             collective_id=collective_id, has_side_effects=True, vmem_limit_bytes=VMEM_MOST
         ),
+        cost_estimate=busy(fields * 24),
         name="collect",
     )(x_parts)
 
@@ -402,6 +410,7 @@
         compiler_params=pltpu.CompilerParams(
             dimension_semantics=("arbitrary",), vmem_limit_bytes=VMEM_MOST
         ),
+        cost_estimate=busy(36),
         name="attend_forward",
     )(*tables, qkv)
 
@@ -626,6 +635,7 @@
         compiler_params=pltpu.CompilerParams(
             dimension_semantics=("arbitrary",), vmem_limit_bytes=VMEM_MOST
         ),
+        cost_estimate=busy(50),
         name="attend_backward",
     )(*tables, qkv, grads, exact, log_total)
 
@@ -657,7 +667,8 @@
 
 
 PAIR = 2
-DEPTH = 4
+DEPTH = 6
+LAG = 2
 
 
 def grads_kernel(spec, left_ref, right_ref, *refs):
@@ -873,26 +884,31 @@
 
     for stream in range(2):
         pl.when(counts[stream] > 0)(functools.partial(give, stream, 0))
-
-    def body(step, carry):
-        for stream in range(2):
-            pl.when(step + 1 < counts[stream])(functools.partial(give, stream, step + 1))
-        own_step = step - slots
-
-        @pl.when((own_step + 1 >= 0) & (own_step + 1 < slots))
-        def _():
-            give(2, own_step + 1)
-
-        for stream in range(2):
-            pl.when(step < counts[stream])(functools.partial(forward, stream, step))
-
-        @pl.when((own_step >= 0) & (own_step < slots))
-        def _():
-            keep(own_step)
+    give(2, 0)
+
+    delays = (chip * LAG, (chips - 1 - chip) * LAG, slots)
+
+    def body(turn, carry):
+        for stream in range(3):
+            step = turn - delays[stream] + 1
+
+            @pl.when((step > 0) & (step < counts[stream]))
+            def _():
+                give(stream, step)
+
+        for stream in range(3):
+            step = turn - delays[stream]
+
+            @pl.when((step >= 0) & (step < counts[stream]))
+            def _():
+                if stream < 2:
+                    forward(stream, step)
+                else:
+                    keep(step)
 
         return carry
 
-    lax.fori_loop(0, (chips - 1) * slots, body, 0)
+    lax.fori_loop(0, (chips - 1) * slots + (chips - 1) * LAG, body, 0)
 
     def finish(k, carry):
         out_ref[k] = own_sum[k]
@@ -927,7 +943,6 @@
     slots = left_index.shape[0] // seq_size
     kind = jnp.bfloat16
     block = (BLOCK, BLOCK)
-    products = chips * PAIR * slots
     return pl.pallas_call(
         functools.partial(grads_kernel, (chips, slots, left_strips, right_strips)),
         out_shape=jax.ShapeDtypeStruct((slots,) + block, kind),
@@ -955,11 +970,7 @@
         compiler_params=pltpu.CompilerParams(
             collective_id=collective_id, has_side_effects=True, vmem_limit_bytes=VMEM_MOST
         ),
-        cost_estimate=pl.CostEstimate(
-            flops=products * 2 * rows * BLOCK * BLOCK,
-            bytes_accessed=2 * (sum(left_strips) + sum(right_strips)) * rows * BLOCK,
-            transcendentals=0,
-        ),
+        cost_estimate=busy(240),
         name="owned_grads",
     )(left_index, right_index, *lefts, *rights)
 
@@ -980,6 +991,205 @@
         right = jnp.where(inside, right_low + within % broad, right)
         first += high * broad
     return left.astype(jnp.int32), right.astype(jnp.int32)
+
+
+def group_peer(me, count, slot, way):
+    far, near = slot // 2, slot % 2
+    half = count // 2
+    return (me // 2 + way * far + half) % half * 2 + (me % 2 + near) % 2
+
+
+def group_barrier(me, count):
+    barrier = pltpu.get_barrier_semaphore()
+    for slot in range(1, count):
+        pl.semaphore_signal(
+            barrier, inc=1, device_id={"head": group_peer(me, count, slot, 1)}, device_id_type=MESH
+        )
+    pl.semaphore_wait(barrier, count - 1)
+
+
+GELU_SCALE = 0.7978845608028654
+GELU_CUBIC = 0.044715
+WIDE = 512
+
+
+def gelu(u):
+    return 0.5 * u * (1.0 + jnp.tanh(GELU_SCALE * (u + GELU_CUBIC * (u * u * u))))
+
+
+def gelu_slope(u):
+    square = u * u
+    bend = jnp.tanh(GELU_SCALE * (u + GELU_CUBIC * (square * u)))
+    inner = GELU_SCALE * (1.0 + 3.0 * GELU_CUBIC * square)
+    return 0.5 * (1.0 + bend) + 0.5 * u * (1.0 - bend * bend) * inner
+
+
+def feed_kernel(is_forward, count, x_ref, up_ref, down_ref, side_ref, *refs):
+    if is_forward:
+        rows_ref, mid_ref, pre_ref, sum_ref = refs[:4]
+        refs = refs[4:]
+    else:
+        rows_ref, mid_ref, sum_ref = refs[:3]
+        refs = refs[3:]
+    (
+        land,
+        up_buf,
+        down_buf,
+        mid_buf,
+        pre_buf,
+        part_buf,
+        got,
+        load_sem,
+        send_sem,
+        recv_sem,
+        back_sem,
+        got_sem,
+        out_sem,
+    ) = refs
+    me = lax.axis_index("head")
+    width, ff_width = up_buf.shape
+    loads = [
+        pltpu.make_async_copy(up_ref, up_buf, load_sem.at[0]),
+        pltpu.make_async_copy(down_ref, down_buf, load_sem.at[1]),
+    ]
+    if not is_forward:
+        loads.append(pltpu.make_async_copy(side_ref, pre_buf, load_sem.at[2]))
+    for copy in loads:
+        copy.start()
+    group_barrier(me, count)
+
+    def push(slot):
+        return pltpu.make_async_remote_copy(
+            src_ref=x_ref,
+            dst_ref=land.at[slot],
+            send_sem=send_sem.at[slot],
+            recv_sem=recv_sem.at[slot],
+            device_id={"head": group_peer(me, count, slot, 1)},
+            device_id_type=MESH,
+        )
+
+    def give_back(slot):
+        return pltpu.make_async_remote_copy(
+            src_ref=part_buf.at[slot],
+            dst_ref=got.at[slot],
+            send_sem=back_sem.at[slot],
+            recv_sem=got_sem.at[slot],
+            device_id={"head": group_peer(me, count, slot, -1)},
+            device_id_type=MESH,
+        )
+
+    def outs(slot):
+        copies = [
+            pltpu.make_async_copy(land.at[slot], rows_ref.at[slot], out_sem.at[0, slot]),
+            pltpu.make_async_copy(mid_buf.at[slot], mid_ref.at[slot], out_sem.at[1, slot]),
+        ]
+        if is_forward:
+            copies.append(
+                pltpu.make_async_copy(pre_buf.at[slot], pre_ref.at[slot], out_sem.at[2, slot])
+            )
+        return copies
+
+    for slot in range(1, count):
+        push(slot).start()
+    land[0] = x_ref[...]
+    for copy in loads:
+        copy.wait()
+
+    def work(slot, carry):
+        @pl.when(slot > 0)
+        def _():
+            push(slot).wait_recv()
+
+        def hidden(index, inner):
+            span = pl.ds(pl.multiple_of(index * WIDE, WIDE), WIDE)
+            if is_forward:
+                pre = nn(land[slot], up_buf[:, span]) + side_ref[:, span]
+                pre_buf[slot, :, span] = pre.astype(jnp.bfloat16)
+                mid_buf[slot, :, span] = gelu(pre).astype(jnp.bfloat16)
+            else:
+                grad = nt(land[slot], down_buf[span, :])
+                slope = gelu_slope(pre_buf[slot, :, span].astype(jnp.float32))
+                mid_buf[slot, :, span] = (grad * slope).astype(jnp.bfloat16)
+            return inner
+
+        def result(index, inner):
+            span = pl.ds(pl.multiple_of(index * WIDE, WIDE), WIDE)
+            if is_forward:
+                part = nn(mid_buf[slot], down_buf[:, span])
+            else:
+                part = nt(mid_buf[slot], up_buf[span, :])
+
+            @pl.when(slot == 0)
+            def _():
+                sum_ref[:, span] = part
+
+            @pl.when(slot > 0)
+            def _():
+                part_buf[slot, :, span] = part.astype(jnp.bfloat16)
+
+            return inner
+
+        lax.fori_loop(0, ff_width // WIDE, hidden, 0)
+        for copy in outs(slot):
+            copy.start()
+        lax.fori_loop(0, width // WIDE, result, 0)
+
+        @pl.when(slot > 0)
+        def _():
+            give_back(slot).start()
+
+        return carry
+
+    lax.fori_loop(0, count, work, 0)
+
+    def add(slot, carry):
+        give_back(slot).wait_recv()
+        sum_ref[...] += got[slot].astype(jnp.float32)
+        return carry
+
+    lax.fori_loop(1, count, add, 0)
+    for slot in range(count):
+        for copy in outs(slot):
+            copy.wait()
+        if slot > 0:
+            push(slot).wait_send()
+            give_back(slot).wait_send()
+
+
+def feed(x_rows, up_panel, down_panel, side, is_forward, count, collective_id):
+    rows, width = x_rows.shape
+    ff_width = up_panel.shape[1]
+    kind = jnp.bfloat16
+    by_width = jax.ShapeDtypeStruct((count, rows, width), kind)
+    by_ff = jax.ShapeDtypeStruct((count, rows, ff_width), kind)
+    total = jax.ShapeDtypeStruct((rows, width), jnp.float32)
+    out_shape = (by_width, by_ff, by_ff, total) if is_forward else (by_width, by_ff, total)
+    return pl.pallas_call(
+        functools.partial(feed_kernel, is_forward, count),
+        out_shape=out_shape,
+        in_specs=[IN_VMEM, ANY, ANY, IN_VMEM if is_forward else ANY],
+        out_specs=(ANY,) * (len(out_shape) - 1) + (IN_VMEM,),
+        scratch_shapes=[
+            pltpu.VMEM((count, rows, width), kind),
+            pltpu.VMEM(up_panel.shape, kind),
+            pltpu.VMEM(down_panel.shape, kind),
+            pltpu.VMEM((count, rows, ff_width), kind),
+            pltpu.VMEM((count, rows, ff_width), kind),
+            pltpu.VMEM((count, rows, width), kind),
+            pltpu.VMEM((count, rows, width), kind),
+            pltpu.SemaphoreType.DMA((3,)),
+            pltpu.SemaphoreType.DMA((count,)),
+            pltpu.SemaphoreType.DMA((count,)),
+            pltpu.SemaphoreType.DMA((count,)),
+            pltpu.SemaphoreType.DMA((count,)),
+            pltpu.SemaphoreType.DMA((3, count)),
+        ],
+        compiler_params=pltpu.CompilerParams(
+            collective_id=collective_id, has_side_effects=True, vmem_limit_bytes=VMEM_MOST
+        ),
+        cost_estimate=busy(90),
+        name="feed_forward" if is_forward else "feed_backward",
+    )(x_rows, up_panel, down_panel, side)
 
 
 def normalize(z_rows, gain, shift):
@@ -1096,22 +1306,23 @@
     z_one = inputs_f32 + branch_out + biases[2]
     h_one, normed_one, recip_one = normalize(z_one, gains[0], biases[3])
     h_low = h_one.astype(jnp.bfloat16)
-    h_grp = group_rows(h_low)
-    pre_act = jnp.dot(h_grp, up_panel, preferred_element_type=jnp.float32) + up_bias
-    act = jax.nn.gelu(pre_act, approximate=True).astype(jnp.bfloat16)
-    ff_out = group_sums(jnp.dot(act, down_panel, preferred_element_type=jnp.float32))
+    h_grp, act, pre_act, ff_out = feed(
+        h_low, up_panel, down_panel, up_bias.reshape(1, ff_width), True, head_count, 5
+    )
     z_two = h_one + ff_out + biases[4]
     layer_f32, normed_two, recip_two = normalize(z_two, gains[1], biases[5])
     layer_out = layer_f32.astype(jnp.bfloat16)
     grad_y = cotangent.astype(jnp.float32) * valid_here[:, None].astype(jnp.float32)
     dz_two, dgain_two, dshift_two = normalize_back(grad_y, normed_two, recip_two, gains[1])
     dbias_down = jnp.sum(dz_two, axis=0)
-    dz_two_grp = group_rows(dz_two.astype(jnp.bfloat16))
-    dact = jnp.dot(dz_two_grp, down_panel.T, preferred_element_type=jnp.float32)
-    gelu_value, gelu_pull = jax.vjp(lambda inner: jax.nn.gelu(inner, approximate=True), pre_act)
-    dpre = gelu_pull(dact)[0].astype(jnp.bfloat16)
+    dz_two_grp, dpre, dh_part = feed(
+        dz_two.astype(jnp.bfloat16), up_panel, down_panel, pre_act, False, head_count, 6
+    )
+    h_grp, act, dz_two_grp, dpre = (
+        array.reshape(rows_grp, array.shape[2]) for array in (h_grp, act, dz_two_grp, dpre)
+    )
     up_bias_part = jnp.sum(dpre.astype(jnp.float32), axis=0)
-    dh_one = dz_two + group_sums(jnp.dot(dpre, up_panel.T, preferred_element_type=jnp.float32))
+    dh_one = dz_two + dh_part
     dz_one, dgain_one, dshift_one = normalize_back(dh_one, normed_one, recip_one, gains[0])
     dbias_out = jnp.sum(dz_one, axis=0)
     dz_one_grp = group_rows(dz_one.astype(jnp.bfloat16))
@@ -1146,8 +1357,8 @@
             dgain_two,
         )
     )
-    up_bias_grad = lax.psum(up_bias_part, "seq")
-    vector_grad = lax.psum(local_vectors, ("head", "seq"))
+    up_bias_grad = jnp.sum(lax.all_gather(up_bias_part, "seq"), axis=0)
+    vector_grad = jnp.sum(lax.all_gather(local_vectors, ("head", "seq")), axis=0)
     left_index, right_index = block_operands(own_map[0], width, panel_width, ff_width)
     low_grads = owned_grads(
         left_index,

time: 1520 us -> 1260 us (0.83)
  waiting for transfers between devices: 584 us -> 389 us
  matrix products: 122 us -> 57.3 us
    pallas_call x1, Pallas kernels: 426 us -> 232 us  [owned_grads(): pl.pallas_call(functools.partial(grads_kernel, (chips, slots, left_strips...]
    pallas_call x0 -> x2, Pallas kernels: none -> 193 us  [feed(): pl.pallas_call(functools.partial(feed_kernel, is_forward, count), out_sha...]
    all_gather x4 -> x2, waiting for transfers between devices: 210 us -> 101 us  [group_rows(): return lax.all_gather(rows_low, 'head', axis=0, tiled=True)]
    reduce_scatter x4 -> x2, waiting for transfers between devices: 160 us -> 56.1 us  [group_sums(): lax.psum_scatter(partial_value.astype(jnp.bfloat16), 'head', scatter_dime...]
    dot_general x4 -> x0, matrix products: 61.9 us -> none  [the longest x1 18.6 us: shards(): dact = jnp.dot(dz_two_grp, down_panel.T, preferred_element_type=jnp.float32)]
    psum x1 -> x0, blocking collectives: 32.6 us -> none  [shards(): up_bias_grad = lax.psum(up_bias_part, 'seq')]
    all_gather x0 -> x1, blocking collectives: none -> 29.4 us  [shards(): up_bias_grad = jnp.sum(lax.all_gather(up_bias_part, 'seq'), axis=0)]
  transfers between devices with their start and end apart: 13 -> 9, of which waited for: 10 -> 6; matrix products, arithmetic and copies ran while one was open for 6% -> 6% of each run, Pallas kernels for 38% -> 30%
where the time goes in v3:
time: 1260 us; the launch traced here: 1250 us
  Pallas kernels  706 us (56%)
  waiting for transfers between devices  389 us (31%)
  matrix products  57.3 us (5%)
  other arithmetic  40.6 us (3%)
  blocking collectives  29.4 us (2%)
  between operations  15.7 us (1%)
    pallas_call x1, Pallas kernels, owned_grads(): pl.pallas_call(functools.partial(grads_kernel, (chips, slots, left_strips...  232 us
    pallas_call x2, Pallas kernels, feed(): pl.pallas_call(functools.partial(feed_kernel, is_forward, count), out_sha...  193 us
    all_gather x2, waiting for transfers between devices, group_rows(): return lax.all_gather(rows_low, 'head', axis=0, tiled=True)  101 us
    pallas_call x2, Pallas kernels, collect(): pl.pallas_call(functools.partial(collect_kernel, fields, heads, parts), o...  100 us
    pallas_call x2, Pallas kernels, spread(): pl.pallas_call(functools.partial(spread_kernel, fields, heads, parts), ou...  95 us
    all_gather x1, waiting for transfers between devices, shards(): down_panel = lax.all_gather(w_down, 'seq', axis=1, tiled=True)  82.4 us
    all_gather x1, waiting for transfers between devices, shards(): up_panel = lax.all_gather(w_up, 'seq', axis=0, tiled=True)  79.5 us
    all_gather x1, waiting for transfers between devices, shards(): lax.all_gather(jnp.concatenate([w_query, w_key, w_value], axis=1), 'seq',...  66.9 us
  transfers between devices with their start and end apart: 9, of which 6 were waited for; matrix products, arithmetic and copies ran while one was open for 6% of the time, Pallas kernels for 30%

profile of v3, /device:TPU:0, one launch (start us, length us, event | category | flops | bytes accessed | tf_op | source)
XLA Modules:
  0.0 1249.5 jit_solution(17212845754879705711)
XLA Ops:
  8.0 2.0 pad_maximum_fusion
  13.4 1.2 and_select_fusion.12
  14.5 50.7 %all-gather.12.cloned.1.call-done.refs_0_ = bf16[1024,2048]{1,0:T(8,128)(2,1)} async-done(((bf16[256,2048]{1,0:T(8,128)(2,1)}), bf16[1024,2048]{1,0:T(8,128)(2,1)}) %all-gather.12.cloned.1.call-update) | async-done | bytes 4194320 | tf_op jit(solution)/shard_map/all_gather | solution.py:1215
  65.2 66.9 %all-gather.10.cloned.1.call-done = bf16[2048,1536]{1,0:T(8,128)(2,1)} async-done(((bf16[256,1536]{1,0:T(8,128)(2,1)}), bf16[2048,1536]{1,0:T(8,128)(2,1)}) %all-gather.10.cloned.1.call-update) | async-done | bytes 6291472 | tf_op jit(solution)/shard_map/all_gather | solution.py:1282
  132.1 10.0 fusion.x_ref
  142.2 71.6 %spread.2 = bf16[3,8,1024,128]{3,2,1,0:T(8,128)(2,1)S(1)} custom-call(bf16[1024,1536]{1,0:T(8,128)(2,1)S(1)} %fusion.x_ref), custom_call_target="tpu_custom_call" | custom-call | flops 57600000000 | bytes 1000000 | tf_op jit(solution)/shard_map/spread/pallas_call | solution.py:117
  213.8 2.7 copy-done
  216.5 35.8 %attend_forward.1 = (bf16[32,256,128]{2,1,0:T(8,128)(2,1)}, f32[16,256,128]{2,1,0:T(8,128)}, f32[16,1,256]{2,1,0:T(1,128)}) custom-call(s32[32]{0:T(128)} %select_reduce_fusion.where_ref, s32[32]{0:T(128)} %get-tuple-element.74.low_ref, s32[32]{0:T(128)} %get-tuple-element.73.high_ref, s32[2]{0:T(128)} %bitcast.96, s32[1]{0:T(128)} %bitcast.4.part_ref, ...), custom_call_target="tpu_custom_call" | custom-call | flops 28800000000 | bytes 1000000 | tf_op jit(solution)/shard_map/attend_forward/pallas_call | solution.py:389
  252.3 38.6 %collect.2.refs_1_ = bf16[1024,512]{1,0:T(8,128)(2,1)} custom-call(bf16[1,8,1024,128]{3,2,1,0:T(8,128)(2,1)} %bitcast.103), custom_call_target="tpu_custom_call" | custom-call | flops 19200000000 | bytes 1000000 | tf_op jit(solution)/shard_map/collect/pallas_call | solution.py:218
  290.9 6.3 convolution_convert_fusion.1
  298.6 0.7 compare_convert_fusion
  299.3 56.1 %reduce-scatter.3.cloned.1.call-done = bf16[256,2048]{1,0:T(8,128)(2,1)} async-done(((bf16[1024,2048]{1,0:T(8,128)(2,1)}), bf16[256,2048]{1,0:T(8,128)(2,1)}) %reduce-scatter.3.cloned.1.call-update) | async-done | bytes 1048592 | tf_op jit(solution)/shard_map/reduce_scatter | solution.py:1219
  355.5 1.7 fusion.5
  357.8 1.6 fusion.4.x_ref
  359.5 79.5 %all-gather.16.cloned.1.call-done.up_ref = bf16[2048,2048]{1,0:T(8,128)(2,1)} async-done(((bf16[256,2048]{1,0:T(8,128)(2,1)}), bf16[2048,2048]{1,0:T(8,128)(2,1)}) %all-gather.16.cloned.1.call-update) | async-done | bytes 8388624 | tf_op jit(solution)/shard_map/all_gather | solution.py:1287
  439.0 82.4 %all-gather.18.cloned.1.call-done.down_ref = bf16[2048,2048]{1,0:T(8,128)(2,1)} async-done(((bf16[2048,256]{1,0:T(8,128)(2,1)}), bf16[2048,2048]{1,0:T(8,128)(2,1)}) %all-gather.18.cloned.1.call-update) | async-done | bytes 8388624 | tf_op jit(solution)/shard_map/all_gather | solution.py:1288
  521.4 96.8 %feed_forward.1 = (bf16[4,256,2048]{2,1,0:T(8,128)(2,1)}, bf16[4,256,2048]{2,1,0:T(8,128)(2,1)}, bf16[4,256,2048]{2,1,0:T(8,128)(2,1)}, f32[256,2048]{1,0:T(8,128)}) custom-call(bf16[256,2048]{1,0:T(8,128)(2,1)} %fusion.4.x_ref, bf16[2048,2048]{1,0:T(8,128)(2,1)} %all-gather.16.cloned.1.call-done.up_ref, ...), custom_call_target="tpu_custom_call" | custom-call | flops 71999995904 | bytes 1000000 | tf_op jit(solution)/shard_map/feed_forward/pallas_call | solution.py:1167
  618.2 2.5 fusion.32
  621.1 0.8 copy-done.9
  622.0 1.6 multiply_reduce_fusion
  623.6 2.6 fusion.30
  626.2 1.3 copy-done.7
  627.5 1.1 convert_element_type.65.x_ref
  628.7 95.8 %feed_backward.1 = (bf16[4,256,2048]{2,1,0:T(8,128)(2,1)}, bf16[4,256,2048]{2,1,0:T(8,128)(2,1)}, f32[256,2048]{1,0:T(8,128)}) custom-call(bf16[256,2048]{1,0:T(8,128)(2,1)} %convert_element_type.65.x_ref, bf16[2048,2048]{1,0:T(8,128)(2,1)} %all-gather.16.cloned.1.call-done.up_ref, bf16[2048,2048]{1,0:T(8,128)(2,1)} %all-gather.18.cloned.1.call-done.down_ref, ...), custom_call_target="tpu_custom_call" | custom-call | flops 71999995904 | bytes 1000000 | tf_op jit(solution)/shard_map/feed_backward/pallas_call | solution.py:1167
  724.5 3.5 multiply_reduce_fusion.1
  728.0 0.9 fusion.31
  729.0 1.3 copy-done.5
  730.3 1.1 convert_element_type.66
  731.7 50.6 %all-gather.20.cloned.1.call-done.refs_5_ = bf16[1024,2048]{1,0:T(8,128)(2,1)} async-done(((bf16[256,2048]{1,0:T(8,128)(2,1)}), bf16[1024,2048]{1,0:T(8,128)(2,1)}) %all-gather.20.cloned.1.call-update) | async-done | bytes 4194320 | tf_op jit(solution)/shard_map/all_gather | solution.py:1215
  782.3 4.5 convolution_convert_fusion.2.x_ref
  786.9 23.4 %spread.3 = bf16[1,8,1024,128]{3,2,1,0:T(8,128)(2,1)S(1)} custom-call(bf16[1024,512]{1,0:T(8,128)(2,1)S(1)} %convolution_convert_fusion.2.x_ref), custom_call_target="tpu_custom_call" | custom-call | flops 19200000000 | bytes 1000000 | tf_op jit(solution)/shard_map/spread/pallas_call | solution.py:117
  810.3 1.3 copy-done.1
  811.6 49.7 %attend_backward.1 = bf16[3,32,256,128]{3,2,1,0:T(8,128)(2,1)} custom-call(s32[32]{0:T(128)} %select_reduce_fusion.where_ref, s32[32]{0:T(128)} %get-tuple-element.74.low_ref, s32[32]{0:T(128)} %get-tuple-element.73.high_ref, s32[2]{0:T(128)} %bitcast.97, s32[1]{0:T(128)} %bitcast.4.part_ref, bf16[3,32,256,128]{3,2,1,0:T(8,128)(2,1)} %bitcast.57, ...), custom_call_target="tpu_custom_call" | custom-call | flops 40000000000 | bytes 1000000 | tf_op jit(solution)/shard_map/attend_backward/pallas_call | solution.py:611
  861.3 61.6 %collect.3.refs_4_ = bf16[1024,1536]{1,0:T(8,128)(2,1)} custom-call(bf16[3,8,1024,128]{3,2,1,0:T(8,128)(2,1)} %bitcast.99), custom_call_target="tpu_custom_call" | custom-call | flops 57600000000 | bytes 1000000 | tf_op jit(solution)/shard_map/collect/pallas_call | solution.py:218
  923.0 2.4 convert_reduce_fusion.1
  925.5 0.7 stack.35
  927.6 3.0 convert_reduce_fusion
  930.6 29.4 %all-gather.1 = f32[16384]{0:T(1024)S(1)} all-gather(f32[2048]{0:T(1024)S(1)} %convert_reduce_fusion), channel_id=3, replica_groups=mesh['head'=4,'seq'=8] {'seq'}, dimensions={0}, use_global_device_ids=true | all-gather | bytes 73728 | tf_op jit(solution)/shard_map/all_gather | solution.py:1360
  960.8 11.0 convolution_convert_fusion
  971.8 232.2 %owned_grads.1 = bf16[24,256,256]{2,1,0:T(8,128)(2,1)} custom-call(s32[192]{0:T(256)} %get-tuple-element.70.left_ref, s32[192]{0:T(256)} %get-tuple-element.69.right_ref, bf16[1024,2048]{1,0:T(8,128)(2,1)} %all-gather.12.cloned.1.call-done.refs_0_, bf16[1024,512]{1,0:T(8,128)(2,1)} %collect.2.refs_1_, bf16[1024,2048]{1,0:T(8,128)(2,1)} %bitcast.100, ...), custom_call_target="tpu_custom_call" | custom-call | flops 192000000000 | bytes 1000000 | tf_op jit(solution)/shard_map/owned_grads/pallas_call | solution.py:946
  1204.1 6.0 convert_element_type.70
  1210.9 3.7 fusion.36
  1214.6 4.1 add_multiply_fusion
  1218.8 3.9 add_multiply_fusion.1
  1222.7 13.7 %multiply_subtract_fusion = f32[24,256,256]{2,1,0:T(8,128)} fusion(f32[24,256,256]{2,1,0:T(8,128)S(1)} %bitcast.64, f32[24,256,256]{1,2,0:T(8,128)S(1)} %fusion.36, f32[24,256,256]{2,1,0:T(8,128)} %param.46), kind=kOutput, calls=%fused_computation.2 | convolution fusion | flops 4834983936 | bytes 25165824 | tf_op jit(solution)/shard_map/bij,bjk->bik/dot_general | solution.py:1379
  1236.5 1.9 bitcast_reduce_fusion
  1238.4 0.7 maximum_subtract_fusion
  1239.7 2.8 convert_add_fusion
  (134 shorter events, 9.5 us)
Async XLA Ops:
  7.2 3.7 copy-start.32
  7.2 4.5 copy-start.12
  7.2 5.1 copy-start.19
  7.2 58.0 %all-gather.12.cloned.1.call-start = ((), (), s32[]{:S(2)}) async-start(), calls=%async_computation.3 | async-start | bytes 5242880 | tf_op jit(solution)/shard_map/all_gather | solution.py:1215
  7.9 124.2 %all-gather.10.cloned.1.call-start = ((), (), s32[]{:S(2)}) async-start(), calls=%async_computation.2 | async-start | bytes 7077888 | tf_op jit(solution)/shard_map/all_gather | solution.py:1282
  10.1 280.8 %all-gather.14.cloned.1.call-start = ((), (), s32[]{:S(2)}) async-start(), calls=%async_computation.4 | async-start | bytes 2359296 | tf_op jit(solution)/shard_map/all_gather | solution.py:1286
  10.8 344.7 %reduce-scatter.3.cloned.1.call-start = ((), (), s32[]{:S(2)}) async-start(), calls=%async_computation.5 | async-start | bytes 5242880 | tf_op jit(solution)/shard_map/reduce_scatter | solution.py:1219
  11.1 131.1 %copy-start.30 = (s32[2,1]{0,1:T(1,128)}, s32[2,1]{0,1:T(1,128)S(1)}, u32[]{:S(2)}) copy-start(s32[2,1]{0,1:T(1,128)S(1)} %reduce-window.4) | copy-start | bytes 28
  213.7 2.7 copy-start
  297.2 2.1 copy-start.17
  297.2 58.3 %copy-start.3 = (bf16[256,2048]{1,0:T(8,128)(2,1)S(1)}, bf16[256,2048]{1,0:T(8,128)(2,1)}, u32[]{:S(2)}) copy-start(bf16[256,2048]{1,0:T(8,128)(2,1)} %param.24) | copy-start | bytes 3145732
  297.2 141.8 %all-gather.16.cloned.1.call-start = ((), (), s32[]{:S(2)}) async-start(), calls=%async_computation.6 | async-start | bytes 9437184 | tf_op jit(solution)/shard_map/all_gather | solution.py:1287
  297.8 223.6 %all-gather.18.cloned.1.call-start = ((), (), s32[]{:S(2)}) async-start(), calls=%async_computation.7 | async-start | bytes 9437184 | tf_op jit(solution)/shard_map/all_gather | solution.py:1288
  298.4 483.9 %all-gather.20.cloned.1.call-start = ((), (), s32[]{:S(2)}) async-start(), calls=%async_computation.8 | async-start | bytes 5242880 | tf_op jit(solution)/shard_map/all_gather | solution.py:1215
  355.5 1.7 copy-start.4
  521.4 96.8 %copy-start.21 = (f32[1,2048]{1,0:T(1,128)S(1)}, f32[1,2048]{1,0:T(1,128)}, u32[]{:S(2)}) copy-start(f32[1,2048]{1,0:T(1,128)} %get-tuple-element.60) | copy-start | bytes 24580
  620.7 1.2 copy-start.9
  621.1 2.5 copy-start.20
  626.2 1.3 copy-start.7
  728.9 1.3 copy-start.5
  730.3 52.0 %copy-start.31 = (bf16[512,2048]{1,0:T(8,128)(2,1)S(1)}, bf16[512,2048]{1,0:T(8,128)(2,1)}, u32[]{:S(2)}) copy-start(bf16[512,2048]{1,0:T(8,128)(2,1)} %all-gather.14.cloned.1.call-done) | copy-start | bytes 6291460
  731.4 505.0 %all-gather.22.cloned.1.call-start = ((), (), s32[]{:S(2)}) async-start(), calls=%async_computation.10 | async-start | bytes 2162688 | tf_op jit(solution)/shard_map/all_gather | solution.py:1361
  810.3 1.3 copy-start.1
  923.0 2.5 copy-start.22
  923.0 2.5 copy-start.23
  923.0 2.5 copy-start.24
  923.0 4.0 copy-start.29
  926.3 313.5 %reduce-scatter.5.cloned.1.call-start = ((), (), s32[]{:S(2)}) async-start(), calls=%async_computation.9 | async-start | bytes 5242880 | tf_op jit(solution)/shard_map/reduce_scatter | solution.py:1219
  927.6 32.5 %copy-start.26 = (f32[2048]{0:T(1024)S(1)}, f32[2048]{0:T(1024)}, u32[]{:S(2)}) copy-start(f32[2048]{0:T(1024)} %param.37) | copy-start | bytes 24580
  927.6 32.5 %copy-start.27 = (f32[2048]{0:T(1024)S(1)}, f32[2048]{0:T(1024)}, u32[]{:S(2)}) copy-start(f32[2048]{0:T(1024)} %param.40) | copy-start | bytes 24580
  927.6 32.5 %copy-start.28 = (f32[2048]{0:T(1024)S(1)}, f32[2048]{0:T(1024)}, u32[]{:S(2)}) copy-start(f32[2048]{0:T(1024)} %param.41) | copy-start | bytes 24580
  927.6 33.2 %copy-start.10 = (bf16[1024,1536]{1,0:T(8,128)(2,1)S(1)}, bf16[1024,1536]{1,0:T(8,128)(2,1)}, u32[]{:S(2)}) copy-start(bf16[1024,1536]{1,0:T(8,128)(2,1)} %collect.3.refs_4_) | copy-start | bytes 9437188
  960.1 11.7 copy-start.25
  1204.1 6.0 copy-start.2
  1204.1 6.7 copy-start.8
  1204.1 10.4 slice-start
  1210.9 3.7 slice-start.1
  1210.9 7.9 slice-start.2
  1214.6 4.2 slice-start.3
  1214.6 8.1 slice-start.4
  1218.8 3.9 slice-start.5
  1222.7 15.6 %copy-start.15 = (f32[8,2048]{1,0:T(8,128)S(1)}, f32[8,2048]{1,0:T(8,128)}, u32[]{:S(2)}) copy-start(f32[8,2048]{1,0:T(8,128)} %param.38) | copy-start | bytes 196612
  1222.7 15.6 %copy-start.16 = (f32[8,2048]{1,0:T(8,128)S(1)}, f32[8,2048]{1,0:T(8,128)}, u32[]{:S(2)}) copy-start(f32[8,2048]{1,0:T(8,128)} %param.39) | copy-start | bytes 196612
  1222.7 15.6 %copy-start.18 = (f32[2,2048]{1,0:T(2,128)S(1)}, f32[2,2048]{1,0:T(2,128)}, u32[]{:S(2)}) copy-start(f32[2,2048]{1,0:T(2,128)} %param.35) | copy-start | bytes 49156
  1236.5 1.9 copy-start.13
  1236.5 3.3 copy-start.6
  1238.3 4.2 copy-start.11
  1239.1 3.4 copy-start.14
Sparse Core Ops, SparseCore 0:
  9.9 55.2 all-gather.11
  67.4 64.6 all-gather.9
  133.7 69.8 all-gather.13
  297.3 58.1 reduce-scatter.2
  356.9 82.0 all-gather.15
  440.4 80.9 all-gather.17
  731.5 50.7 all-gather.19
  926.4 72.3 all-gather.21
  1001.8 51.5 reduce-scatter.4

commit v4 on v3

--- a/solution.py
+++ b/solution.py
@@ -7,6 +7,7 @@
 from jax.experimental import pallas as pl
 from jax.experimental.pallas import tpu as pltpu
 from jax.sharding import PartitionSpec as P
+
 
 HDIM = 128
 BLOCK = 256
@@ -212,7 +213,7 @@
 
 
 def collect(x_parts, heads, parts, collective_id):
-    fields, seq_size, rows, _ = x_parts.shape
+    fields, _, rows, _ = x_parts.shape
     kind = x_parts.dtype
     few = max(parts - 1, 1)
     return pl.pallas_call(
@@ -383,7 +384,7 @@
 
 
 def attend_forward(qkv, tables, setup):
-    parts, tile, seq_count, aligned, runs = setup
+    parts, _, _, aligned, runs = setup
     own = runs // parts
     rows = runs * RUN
     return pl.pallas_call(
@@ -605,7 +606,7 @@
 
 
 def attend_backward(qkv, grads, exact, log_total, tables, setup):
-    parts, tile, seq_count, aligned, runs = setup
+    parts, _, _, aligned, runs = setup
     own = runs // parts
     rows = runs * RUN
     return pl.pallas_call(
@@ -640,7 +641,7 @@
     )(*tables, qkv, grads, exact, log_total)
 
 
-def stream_tables(token_order, lengths, head_count, seq_size, parts, tile, part):
+def stream_tables(token_order, lengths, head_count, seq_size, tile, part):
     runs = token_order.shape[0] // RUN
     stream = (token_order.reshape(head_count, seq_size, RUN)[:, :, 0] // RUN).T.reshape(-1)
     places = jnp.arange(runs, dtype=jnp.int32)
@@ -1190,6 +1191,130 @@
         cost_estimate=busy(90),
         name="feed_forward" if is_forward else "feed_backward",
     )(x_rows, up_panel, down_panel, side)
+
+
+def start_kernel(count, chips, x_ref, w_ref, rows_ref, panel_ref, own_sem, row_sems, line_sems, pair_sems):
+    me, place = lax.axis_index("head"), lax.axis_index("seq")
+    chip, core = place // PAIR, place % PAIR
+    sibling = chip * PAIR + (1 - core)
+    neighbours = ((chip + 1) * PAIR + core, (chip - 1) * PAIR + core)
+    has_next = (chip < chips - 1, chip > 0)
+    owns = [
+        pltpu.make_async_copy(x_ref, rows_ref.at[me], own_sem.at[0]),
+        pltpu.make_async_copy(w_ref, panel_ref.at[place], own_sem.at[1]),
+    ]
+    for copy in owns:
+        copy.start()
+
+    barrier = pltpu.get_barrier_semaphore()
+    for slot in range(1, count):
+        pl.semaphore_signal(
+            barrier, inc=1, device_id={"head": group_peer(me, count, slot, 1)}, device_id_type=MESH
+        )
+    pl.semaphore_signal(barrier, inc=1, device_id={"seq": sibling}, device_id_type=MESH)
+    for way in range(2):
+
+        @pl.when(has_next[way])
+        def _():
+            pl.semaphore_signal(
+                barrier, inc=1, device_id={"seq": neighbours[way]}, device_id_type=MESH
+            )
+
+    ends = (chip == 0).astype(jnp.int32) + (chip == chips - 1).astype(jnp.int32)
+    pl.semaphore_wait(barrier, count - 1 + 3 - ends)
+
+    pushes = []
+    for slot in range(1, count):
+        pushes.append(
+            pltpu.make_async_remote_copy(
+                src_ref=x_ref,
+                dst_ref=rows_ref.at[me],
+                send_sem=row_sems.at[0, slot],
+                recv_sem=row_sems.at[1, slot],
+                device_id={"head": group_peer(me, count, slot, 1)},
+                device_id_type=MESH,
+            )
+        )
+
+    def relay(way, step):
+        origin = chip - step if way == 0 else chip + step
+        block = panel_ref.at[origin * PAIR + core]
+        return pltpu.make_async_remote_copy(
+            src_ref=w_ref if step == 0 else block,
+            dst_ref=block,
+            send_sem=line_sems.at[0, way, step],
+            recv_sem=line_sems.at[1, way, step],
+            device_id={"seq": neighbours[way]},
+            device_id_type=MESH,
+        )
+
+    def share(way, step):
+        origin = chip - 1 - step if way == 0 else chip + 1 + step
+        if way == 2:
+            origin = chip
+        block = panel_ref.at[origin * PAIR + core]
+        return pltpu.make_async_remote_copy(
+            src_ref=w_ref if way == 2 else block,
+            dst_ref=block,
+            send_sem=pair_sems.at[0, way, step],
+            recv_sem=pair_sems.at[1, way, step],
+            device_id={"seq": sibling},
+            device_id_type=MESH,
+        )
+
+    def sends(way, step):
+        behind = chip >= step if way == 0 else chip + step <= chips - 1
+        return has_next[way] & behind
+
+    def receives(way, step):
+        return chip - 1 - step >= 0 if way == 0 else chip + 1 + step <= chips - 1
+
+    for way in range(2):
+        pl.when(sends(way, 0))(relay(way, 0).start)
+    for copy in pushes:
+        copy.start()
+    share(2, 0).start()
+    for step in range(chips - 1):
+        for way in range(2):
+
+            @pl.when(receives(way, step))
+            def _():
+                relay(way, step).wait_recv()
+                if step + 1 < chips - 1:
+                    pl.when(sends(way, step + 1))(relay(way, step + 1).start)
+                share(way, step).start()
+
+    for copy in owns + pushes:
+        copy.wait()
+    share(2, 0).wait()
+    for step in range(chips - 1):
+        for way in range(2):
+            pl.when(sends(way, step))(relay(way, step).wait_send)
+            pl.when(receives(way, step))(share(way, step).wait)
+
+
+def start_gathers(x_rows, w_rows, head_count, seq_size, collective_id):
+    chips = seq_size // PAIR
+    return pl.pallas_call(
+        functools.partial(start_kernel, head_count, chips),
+        out_shape=(
+            jax.ShapeDtypeStruct((head_count,) + x_rows.shape, x_rows.dtype),
+            jax.ShapeDtypeStruct((seq_size,) + w_rows.shape, w_rows.dtype),
+        ),
+        in_specs=[IN_VMEM, IN_VMEM],
+        out_specs=(ANY, ANY),
+        scratch_shapes=[
+            pltpu.SemaphoreType.DMA((2,)),
+            pltpu.SemaphoreType.DMA((2, head_count)),
+            pltpu.SemaphoreType.DMA((2, 2, chips)),
+            pltpu.SemaphoreType.DMA((2, 3, chips)),
+        ],
+        compiler_params=pltpu.CompilerParams(
+            collective_id=collective_id, has_side_effects=True, vmem_limit_bytes=16 * 1024 * 1024
+        ),
+        cost_estimate=busy(60),
+        name="start_gathers",
+    )(x_rows, w_rows)
 
 
 def normalize(z_rows, gain, shift):
@@ -1271,18 +1396,17 @@
     aligned = seq_count == 2
     tile = 1024 if aligned else RUN
     setup = (parts, tile, seq_count, aligned, runs)
-    tables = stream_tables(
-        token_order, lengths, head_count, seq_size, parts, tile, group_index % parts
-    )
+    tables = stream_tables(token_order, lengths, head_count, seq_size, tile, group_index % parts)
     own_block = head_index * seq_size + group_index
     order_here = lax.dynamic_slice_in_dim(token_order, own_block * tok_count, tok_count, 0)
     valid_here = order_here < tables[3][seq_count - 1]
     inputs_f32 = hidden_in.astype(jnp.float32)
 
-    qkv_panel = lax.all_gather(
-        jnp.concatenate([w_query, w_key, w_value], axis=1), "seq", axis=0, tiled=True
-    )
-    inputs_grp = group_rows(hidden_in)
+    inputs_grp, qkv_panel = start_gathers(
+        hidden_in, jnp.concatenate([w_query, w_key, w_value], axis=1), head_count, seq_size, 7
+    )
+    inputs_grp = inputs_grp.reshape(head_count * tok_count, width)
+    qkv_panel = qkv_panel.reshape(width, 3 * panel_width)
     o_panel = lax.all_gather(w_out, "seq", axis=1, tiled=True)
     up_panel = lax.all_gather(w_up, "seq", axis=0, tiled=True)
     down_panel = lax.all_gather(w_down, "seq", axis=1, tiled=True)
@@ -1296,7 +1420,8 @@
     qkv_grp = (
         jnp.dot(inputs_grp, qkv_panel, preferred_element_type=jnp.float32) + qkv_bias
     ).astype(jnp.bfloat16)
-    qkv_head = spread(qkv_grp, 3, heads, parts, seq_size, 0).reshape(3, runs, RUN, HDIM)
+    qkv_head = spread(qkv_grp, 3, heads, parts, seq_size, 0)
+    qkv_head = qkv_head.reshape(3, runs, RUN, HDIM)
     attended_part, attended_exact, log_total = attend_forward(qkv_head, tables, setup)
     rows_grp = head_count * tok_count
     attended_grp = collect(
@@ -1357,8 +1482,13 @@
             dgain_two,
         )
     )
-    up_bias_grad = jnp.sum(lax.all_gather(up_bias_part, "seq"), axis=0)
-    vector_grad = jnp.sum(lax.all_gather(local_vectors, ("head", "seq")), axis=0)
+    packed = jnp.concatenate([local_vectors.reshape(-1), up_bias_part])
+    packed_all = lax.all_gather(packed, ("head", "seq"))
+    vector_grad = jnp.sum(packed_all[:, : 8 * width], axis=0).reshape(8, width)
+    up_bias_grad = jnp.sum(
+        lax.dynamic_slice_in_dim(packed_all[:, 8 * width :], head_index * seq_size, seq_size, 0),
+        axis=0,
+    )
     left_index, right_index = block_operands(own_map[0], width, panel_width, ff_width)
     low_grads = owned_grads(
         left_index,
@@ -1375,8 +1505,18 @@
     stat_right_new = 0.5 * stat_right + 0.5 * jnp.einsum(
         "bji,bjk->bik", low_grads, low_grads, preferred_element_type=jnp.float32
     )
-    left_mix = jnp.einsum("bij,bjk->bik", root_left, block_grads, precision=lax.Precision.HIGHEST)
-    direction = jnp.einsum("bij,bjk->bik", left_mix, root_right, precision=lax.Precision.HIGHEST)
+    left_mix = jnp.einsum(
+        "bij,bjk->bik",
+        root_left.astype(jnp.bfloat16),
+        low_grads,
+        preferred_element_type=jnp.float32,
+    )
+    direction = jnp.einsum(
+        "bij,bjk->bik",
+        left_mix.astype(jnp.bfloat16),
+        root_right.astype(jnp.bfloat16),
+        preferred_element_type=jnp.float32,
+    )
     master_new = master - SHAMPOO_RATE * direction
     step_float = step_count[0].astype(jnp.float32)
     vector_params = jnp.concatenate([biases, gains], axis=0)

time: 1260 us -> 1190 us (0.944)
  waiting for transfers between devices: 389 us -> 267 us
  Pallas kernels: 706 us -> 790 us
  blocking collectives: 29.4 us -> 0 us
    pallas_call x0 -> x1, Pallas kernels: none -> 75.8 us  [start_gathers(): pl.pallas_call(functools.partial(start_kernel, head_count, chips), out_sh...]
    all_gather x2 -> x1, waiting for transfers between devices: 66.9 us -> 0.01 us  [shards(): packed_all = lax.all_gather(packed, ('head', 'seq'))]
    all_gather x2 -> x1, waiting for transfers between devices: 101 us -> 48 us  [group_rows(): return lax.all_gather(rows_low, 'head', axis=0, tiled=True)]
    all_gather x1 -> x0, blocking collectives: 29.4 us -> none  [shards(): up_bias_grad = jnp.sum(lax.all_gather(up_bias_part, 'seq'), axis=0)]
    pallas_call x1, Pallas kernels: 232 us -> 254 us  [owned_grads(): pl.pallas_call(functools.partial(grads_kernel, (chips, slots, left_strips...]
    pallas_call x2, Pallas kernels: 95 us -> 81.6 us  [spread(): pl.pallas_call(functools.partial(spread_kernel, fields, heads, parts), ou...]
  transfers between devices with their start and end apart: 9 -> 7, of which waited for: 6 -> 4; matrix products, arithmetic and copies ran while one was open for 6% -> 6% of each run, Pallas kernels for 30% -> 39%
where the time goes in v4:
time: 1190 us; the launch traced here: 1180 us
  Pallas kernels  790 us (66%)
  waiting for transfers between devices  267 us (22%)
  matrix products  47.7 us (4%)
  other arithmetic  41.9 us (4%)
  local copies, waits for them, and re-layouts  18.6 us (2%)
  between operations  15.7 us (1%)
    pallas_call x1, Pallas kernels, owned_grads(): pl.pallas_call(functools.partial(grads_kernel, (chips, slots, left_strips...  254 us
    pallas_call x2, Pallas kernels, feed(): pl.pallas_call(functools.partial(feed_kernel, is_forward, count), out_sha...  193 us
    pallas_call x2, Pallas kernels, collect(): pl.pallas_call(functools.partial(collect_kernel, fields, heads, parts), o...  101 us
    all_gather x1, waiting for transfers between devices, shards(): up_panel = lax.all_gather(w_up, 'seq', axis=0, tiled=True)  81.7 us
    pallas_call x2, Pallas kernels, spread(): pl.pallas_call(functools.partial(spread_kernel, fields, heads, parts), ou...  81.6 us
    all_gather x1, waiting for transfers between devices, shards(): down_panel = lax.all_gather(w_down, 'seq', axis=1, tiled=True)  80.1 us
    pallas_call x1, Pallas kernels, start_gathers(): pl.pallas_call(functools.partial(start_kernel, head_count, chips), out_sh...  75.8 us
    reduce_scatter x2, waiting for transfers between devices, group_sums(): lax.psum_scatter(partial_value.astype(jnp.bfloat16), 'head', scatter_dime...  55 us
  transfers between devices with their start and end apart: 7, of which 4 were waited for; matrix products, arithmetic and copies ran while one was open for 6% of the time, Pallas kernels for 39%

profile of v4, /device:TPU:0, one launch (start us, length us, event | category | flops | bytes accessed | tf_op | source)
XLA Modules:
  0.0 1181.5 jit_solution(18193916896293953996)
XLA Ops:
  8.0 0.8 reduce-window.4
  10.1 1.7 fusion.47
  11.8 1.2 pad_maximum_fusion.w_ref
  13.0 1.2 copy-done
  14.2 75.8 %start_gathers.1 = (bf16[4,256,2048]{2,1,0:T(8,128)(2,1)S(1)}, bf16[8,256,1536]{2,1,0:T(8,128)(2,1)S(1)}) custom-call(bf16[256,2048]{1,0:T(8,128)(2,1)S(1)} %copy-done, bf16[256,1536]{1,0:T(8,128)(2,1)S(1)} %pad_maximum_fusion.w_ref), custom_call_target="tpu_custom_call" | custom-call | flops 48000000000 | bytes 1000000 | tf_op jit(solution)/shard_map/start_gathers/pallas_call | solution.py:1298
  90.1 2.6 copy-done.2
  92.7 6.9 add_convert_fusion.x_ref
  99.7 58.2 %spread.2 = bf16[3,8,1024,128]{3,2,1,0:T(8,128)(2,1)S(1)} custom-call(bf16[1024,1536]{1,0:T(8,128)(2,1)S(1)} %add_convert_fusion.x_ref), custom_call_target="tpu_custom_call" | custom-call | flops 57600000000 | bytes 1000000 | tf_op jit(solution)/shard_map/spread/pallas_call | solution.py:118
  157.9 2.7 copy-done.3
  161.6 1.2 and_select_fusion.12
  162.8 35.8 %attend_forward.1 = (bf16[32,256,128]{2,1,0:T(8,128)(2,1)}, f32[16,256,128]{2,1,0:T(8,128)}, f32[16,1,256]{2,1,0:T(1,128)}) custom-call(s32[32]{0:T(128)} %select_reduce_fusion.where_ref, s32[32]{0:T(128)} %get-tuple-element.78.low_ref, s32[32]{0:T(128)} %get-tuple-element.77.high_ref, s32[2]{0:T(128)} %bitcast.95, s32[1]{0:T(128)} %bitcast.4.part_ref, ...), custom_call_target="tpu_custom_call" | custom-call | flops 28800000000 | bytes 1000000 | tf_op jit(solution)/shard_map/attend_forward/pallas_call | solution.py:390
  198.6 38.9 %collect.2.refs_1_ = bf16[1024,512]{1,0:T(8,128)(2,1)} custom-call(bf16[1,8,1024,128]{3,2,1,0:T(8,128)(2,1)} %bitcast.102), custom_call_target="tpu_custom_call" | custom-call | flops 19200000000 | bytes 1000000 | tf_op jit(solution)/shard_map/collect/pallas_call | solution.py:219
  237.5 6.3 convolution_convert_fusion.1
  245.7 0.7 compare_convert_fusion
  246.4 55.0 %reduce-scatter.3.cloned.1.call-done = bf16[256,2048]{1,0:T(8,128)(2,1)} async-done(((bf16[1024,2048]{1,0:T(8,128)(2,1)}), bf16[256,2048]{1,0:T(8,128)(2,1)}) %reduce-scatter.3.cloned.1.call-update) | async-done | bytes 1048592 | tf_op jit(solution)/shard_map/reduce_scatter | solution.py:1344
  301.5 1.7 fusion.19
  303.8 1.6 fusion.18.x_ref
  305.4 80.1 %all-gather.11.cloned.1.call-done.down_ref = bf16[2048,2048]{1,0:T(8,128)(2,1)} async-done(((bf16[2048,256]{1,0:T(8,128)(2,1)}), bf16[2048,2048]{1,0:T(8,128)(2,1)}) %all-gather.11.cloned.1.call-update) | async-done | bytes 8388624 | tf_op jit(solution)/shard_map/all_gather | solution.py:1412
  385.5 81.7 %all-gather.9.cloned.1.call-done.up_ref = bf16[2048,2048]{1,0:T(8,128)(2,1)} async-done(((bf16[256,2048]{1,0:T(8,128)(2,1)}), bf16[2048,2048]{1,0:T(8,128)(2,1)}) %all-gather.9.cloned.1.call-update) | async-done | bytes 8388624 | tf_op jit(solution)/shard_map/all_gather | solution.py:1411
  467.3 96.7 %feed_forward.1 = (bf16[4,256,2048]{2,1,0:T(8,128)(2,1)}, bf16[4,256,2048]{2,1,0:T(8,128)(2,1)}, bf16[4,256,2048]{2,1,0:T(8,128)(2,1)}, f32[256,2048]{1,0:T(8,128)}) custom-call(bf16[256,2048]{1,0:T(8,128)(2,1)} %fusion.18.x_ref, bf16[2048,2048]{1,0:T(8,128)(2,1)} %all-gather.9.cloned.1.call-done.up_ref, ...), custom_call_target="tpu_custom_call" | custom-call | flops 71999995904 | bytes 1000000 | tf_op jit(solution)/shard_map/feed_forward/pallas_call | solution.py:1168
  564.0 2.5 fusion.46
  566.9 0.8 copy-done.12
  567.7 1.6 multiply_reduce_fusion
  569.3 2.6 fusion.44
  572.0 1.3 copy-done.10
  573.3 1.1 convert_element_type.72.x_ref
  574.4 95.8 %feed_backward.1 = (bf16[4,256,2048]{2,1,0:T(8,128)(2,1)}, bf16[4,256,2048]{2,1,0:T(8,128)(2,1)}, f32[256,2048]{1,0:T(8,128)}) custom-call(bf16[256,2048]{1,0:T(8,128)(2,1)} %convert_element_type.72.x_ref, bf16[2048,2048]{1,0:T(8,128)(2,1)} %all-gather.9.cloned.1.call-done.up_ref, bf16[2048,2048]{1,0:T(8,128)(2,1)} %all-gather.11.cloned.1.call-done.down_ref, ...), custom_call_target="tpu_custom_call" | custom-call | flops 71999995904 | bytes 1000000 | tf_op jit(solution)/shard_map/feed_backward/pallas_call | solution.py:1168
  670.3 3.5 multiply_reduce_fusion.1
  673.8 0.9 fusion.45
  674.7 1.3 copy-done.8
  676.0 1.1 convert_element_type.73
  677.4 3.0 convert_reduce_fusion
  680.4 48.0 %all-gather.13.cloned.1.call-done.refs_5_ = bf16[1024,2048]{1,0:T(8,128)(2,1)} async-done(((bf16[256,2048]{1,0:T(8,128)(2,1)}), bf16[1024,2048]{1,0:T(8,128)(2,1)}) %all-gather.13.cloned.1.call-update) | async-done | bytes 4194320 | tf_op jit(solution)/shard_map/all_gather | solution.py:1340
  728.4 4.5 convolution_convert_fusion.2.x_ref
  732.9 23.4 %spread.3 = bf16[1,8,1024,128]{3,2,1,0:T(8,128)(2,1)S(1)} custom-call(bf16[1024,512]{1,0:T(8,128)(2,1)S(1)} %convolution_convert_fusion.2.x_ref), custom_call_target="tpu_custom_call" | custom-call | flops 19200000000 | bytes 1000000 | tf_op jit(solution)/shard_map/spread/pallas_call | solution.py:118
  756.4 1.3 copy-done.5
  757.7 49.7 %attend_backward.1 = bf16[3,32,256,128]{3,2,1,0:T(8,128)(2,1)} custom-call(s32[32]{0:T(128)} %select_reduce_fusion.where_ref, s32[32]{0:T(128)} %get-tuple-element.78.low_ref, s32[32]{0:T(128)} %get-tuple-element.77.high_ref, s32[2]{0:T(128)} %bitcast.96, s32[1]{0:T(128)} %bitcast.4.part_ref, bf16[3,32,256,128]{3,2,1,0:T(8,128)(2,1)} %bitcast.56, ...), custom_call_target="tpu_custom_call" | custom-call | flops 40000000000 | bytes 1000000 | tf_op jit(solution)/shard_map/attend_backward/pallas_call | solution.py:612
  807.4 61.6 %collect.3.refs_4_ = bf16[1024,1536]{1,0:T(8,128)(2,1)} custom-call(bf16[3,8,1024,128]{3,2,1,0:T(8,128)(2,1)} %bitcast.98), custom_call_target="tpu_custom_call" | custom-call | flops 57600000000 | bytes 1000000 | tf_op jit(solution)/shard_map/collect/pallas_call | solution.py:219
  869.1 2.5 convert_reduce_fusion.1
  873.9 11.0 convolution_convert_fusion
  885.0 253.9 %owned_grads.1 = bf16[24,256,256]{2,1,0:T(8,128)(2,1)} custom-call(s32[192]{0:T(256)} %get-tuple-element.74.left_ref, s32[192]{0:T(256)} %get-tuple-element.73.right_ref, bf16[1024,2048]{1,0:T(8,128)(2,1)} %bitcast.58, bf16[1024,512]{1,0:T(8,128)(2,1)} %collect.2.refs_1_, bf16[1024,2048]{1,0:T(8,128)(2,1)} %bitcast.99, bf16[1024,2048]{1,0:T(8,128)(2,1)} %bitcast.100, ...), custom_call_target="tpu_custom_call" | custom-call | flops 192000000000 | bytes 1000000 | tf_op jit(solution)/shard_map/owned_grads/pallas_call | solution.py:947
  1138.9 6.0 convert_element_type.77
  1145.6 4.0 add_multiply_fusion
  1149.6 3.7 add_multiply_fusion.1
  1153.3 11.3 multiply_subtract_fusion
  1164.6 2.9 reshape.169
  1167.5 1.9 slice_reduce_fusion
  1171.6 2.8 convert_add_fusion
  (128 shorter events, 10.5 us)
Async XLA Ops:
  7.2 230.3 %all-gather.7.cloned.1.call-start = ((), (), s32[]{:S(2)}) async-start(), calls=%async_computation.2 | async-start | bytes 2359296 | tf_op jit(solution)/shard_map/all_gather | solution.py:1410
  7.9 293.5 %reduce-scatter.3.cloned.1.call-start = ((), (), s32[]{:S(2)}) async-start(), calls=%async_computation.3 | async-start | bytes 5242880 | tf_op jit(solution)/shard_map/reduce_scatter | solution.py:1344
  8.8 152.7 %copy-start.34 = (s32[2,1]{0,1:T(1,128)}, s32[2,1]{0,1:T(1,128)S(1)}, u32[]{:S(2)}) copy-start(s32[2,1]{0,1:T(1,128)S(1)} %reduce-window.4) | copy-start | bytes 28
  13.0 1.2 copy-start
  90.0 2.7 copy-start.2
  90.0 9.6 copy-start.4
  99.6 60.9 %copy-start.23 = (s32[8192]{0:T(1024)S(1)}, s32[8192]{0:T(1024)}, u32[]{:S(2)}) copy-start(s32[8192]{0:T(1024)} %param.27) | copy-start | bytes 98308
  157.9 2.7 copy-start.3
  243.8 2.6 copy-start.21
  243.8 57.6 %copy-start.1 = (bf16[256,2048]{1,0:T(8,128)(2,1)S(1)}, bf16[256,2048]{1,0:T(8,128)(2,1)}, u32[]{:S(2)}) copy-start(bf16[256,2048]{1,0:T(8,128)(2,1)} %x_ref.1) | copy-start | bytes 3145732
  243.8 57.6 %copy-start.14 = (f32[1,2048]{1,0:T(1,128)S(1)}, f32[1,2048]{1,0:T(1,128)}, u32[]{:S(2)}) copy-start(f32[1,2048]{1,0:T(1,128)} %get-tuple-element.66) | copy-start | bytes 24580
  243.9 141.7 %all-gather.11.cloned.1.call-start = ((), (), s32[]{:S(2)}) async-start(), calls=%async_computation.5 | async-start | bytes 9437184 | tf_op jit(solution)/shard_map/all_gather | solution.py:1412
  244.6 222.7 %all-gather.9.cloned.1.call-start = ((), (), s32[]{:S(2)}) async-start(), calls=%async_computation.4 | async-start | bytes 9437184 | tf_op jit(solution)/shard_map/all_gather | solution.py:1411
  245.2 483.2 %all-gather.13.cloned.1.call-start = ((), (), s32[]{:S(2)}) async-start(), calls=%async_computation.6 | async-start | bytes 5242880 | tf_op jit(solution)/shard_map/all_gather | solution.py:1340
  301.5 1.8 copy-start.7
  301.5 2.3 copy-start.18
  467.2 96.8 %copy-start.25 = (f32[1,2048]{1,0:T(1,128)S(1)}, f32[1,2048]{1,0:T(1,128)}, u32[]{:S(2)}) copy-start(f32[1,2048]{1,0:T(1,128)} %get-tuple-element.64) | copy-start | bytes 24580
  566.5 1.2 copy-start.12
  566.9 2.5 copy-start.24
  572.0 1.3 copy-start.10
  674.7 1.3 copy-start.8
  677.2 487.4 %all-gather.15.cloned.1.call-start = ((), (), s32[]{:S(2)}) async-start(), calls=%async_computation.8 | async-start | bytes 2433024 | tf_op jit(solution)/shard_map/all_gather | solution.py:1486
  677.4 51.0 %copy-start.35 = (bf16[512,2048]{1,0:T(8,128)(2,1)S(1)}, bf16[512,2048]{1,0:T(8,128)(2,1)}, u32[]{:S(2)}) copy-start(bf16[512,2048]{1,0:T(8,128)(2,1)} %all-gather.7.cloned.1.call-done) | copy-start | bytes 6291460
  756.4 1.3 copy-start.5
  869.1 2.7 copy-start.26
  869.1 2.7 copy-start.27
  869.1 2.7 copy-start.28
  869.1 4.2 copy-start.33
  869.1 4.8 copy-start.13
  872.5 299.0 %reduce-scatter.5.cloned.1.call-start = ((), (), s32[]{:S(2)}) async-start(), calls=%async_computation.7 | async-start | bytes 5242880 | tf_op jit(solution)/shard_map/reduce_scatter | solution.py:1344
  1138.9 6.0 copy-start.6
  1138.9 6.7 copy-start.11
  1138.9 10.7 slice-start.1
  1145.6 4.0 slice-start.2
  1167.4 2.1 copy-start.16
  1167.4 2.1 copy-start.19
  1167.4 2.1 copy-start.20
  1167.4 2.1 copy-start.22
  1167.4 3.4 slice-start
  1167.5 3.4 copy-start.30
  1167.5 3.4 copy-start.31
  1167.5 3.4 copy-start.32
  1167.5 4.1 copy-start.9
  1169.5 4.9 copy-start.15
  1170.2 4.1 copy-start.17
  1170.9 3.5 copy-start.29
Sparse Core Ops, SparseCore 0:
  9.6 47.3 all-gather.6
  243.9 57.4 reduce-scatter.2
  303.0 82.4 all-gather.10
  387.0 80.2 all-gather.8
  677.3 51.0 all-gather.12
  872.7 74.6 all-gather.14
  950.4 52.0 reduce-scatter.4

commit v5 on v4

--- a/solution.py
+++ b/solution.py
@@ -1158,6 +1158,8 @@
 
 
 def feed(x_rows, up_panel, down_panel, side, is_forward, count, collective_id):
+    if count == 4:
+        return square_feed(x_rows, up_panel, down_panel, side, is_forward, collective_id)
     rows, width = x_rows.shape
     ff_width = up_panel.shape[1]
     kind = jnp.bfloat16
@@ -1190,6 +1192,293 @@
         ),
         cost_estimate=busy(90),
         name="feed_forward" if is_forward else "feed_backward",
+    )(x_rows, up_panel, down_panel, side)
+
+
+def square_places(me):
+    far, near = me // 2, me % 2
+    return far * 2 + 1 - near, (1 - far) * 2 + near
+
+
+def square_barrier(me):
+    barrier = pltpu.get_barrier_semaphore()
+    for peer in square_places(me):
+        pl.semaphore_signal(barrier, inc=1, device_id={"head": peer}, device_id_type=MESH)
+    pl.semaphore_wait(barrier, 2)
+
+
+def square_copy(source, target, sems, index, peer):
+    return pltpu.make_async_remote_copy(
+        src_ref=source,
+        dst_ref=target,
+        send_sem=sems.at[0, index],
+        recv_sem=sems.at[1, index],
+        device_id={"head": peer},
+        device_id_type=MESH,
+    )
+
+
+def square_gather(me, rows, x_ref, land, at_target, at_self, sems):
+    one, two = square_places(me)
+    low, high = pl.ds(0, rows // 2), pl.ds(rows // 2, rows // 2)
+    return (
+        square_copy(x_ref.at[low], land.at[at_target[0], low], sems, 0, one),
+        square_copy(x_ref.at[high], land.at[at_target[0], high], sems, 1, one),
+        square_copy(x_ref.at[high], land.at[at_target[1], high], sems, 2, two),
+        square_copy(x_ref.at[low], land.at[at_target[1], low], sems, 3, two),
+        square_copy(land.at[at_self[0], low], land.at[at_target[2], low], sems, 4, two),
+        square_copy(land.at[at_self[1], high], land.at[at_target[3], high], sems, 5, one),
+    )
+
+
+def square_sums(me, rows, part_buf, relay, got, sems):
+    one, two = square_places(me)
+    low, high = pl.ds(0, rows // 2), pl.ds(rows // 2, rows // 2)
+    return (
+        square_copy(part_buf.at[3, low], relay.at[0], sems, 0, one),
+        square_copy(part_buf.at[3, high], relay.at[1], sems, 1, two),
+        square_copy(part_buf.at[1, low], got.at[0, low], sems, 2, one),
+        square_copy(part_buf.at[1, high], got.at[0, high], sems, 3, one),
+        square_copy(part_buf.at[2, high], got.at[1, high], sems, 4, two),
+        square_copy(part_buf.at[2, low], got.at[1, low], sems, 5, two),
+    )
+
+
+def square_finish(rows, sums, part_buf, relay, got, sum_ref):
+    low, high = pl.ds(0, rows // 2), pl.ds(rows // 2, rows // 2)
+
+    def join(slot, span, index):
+        total = part_buf[slot, span, :].astype(jnp.float32) + relay[index].astype(jnp.float32)
+        part_buf[slot, span, :] = total.astype(jnp.bfloat16)
+
+    sums[1].wait_recv()
+    join(1, high, 1)
+    sums[3].start()
+    sums[0].wait_recv()
+    join(2, low, 0)
+    sums[5].start()
+    for index in (2, 4, 3, 5):
+        sums[index].wait_recv()
+    sum_ref[...] += got[0].astype(jnp.float32) + got[1].astype(jnp.float32)
+    for copy in sums:
+        copy.wait_send()
+
+
+def square_rows_kernel(x_ref, rows_ref, own_sem, sems):
+    me = lax.axis_index("head")
+    one, two = square_places(me)
+    own = pltpu.make_async_copy(x_ref, rows_ref.at[me], own_sem)
+    own.start()
+    square_barrier(me)
+    copies = square_gather(
+        me, x_ref.shape[0], x_ref, rows_ref, (me, me, one, two), (one, two), sems
+    )
+    for index in (0, 2, 1, 3):
+        copies[index].start()
+    copies[0].wait_recv()
+    copies[4].start()
+    copies[2].wait_recv()
+    copies[5].start()
+    for index in (1, 3, 4, 5):
+        copies[index].wait_recv()
+    for copy in copies:
+        copy.wait_send()
+    own.wait()
+
+
+def square_rows(x_rows, collective_id):
+    return pl.pallas_call(
+        square_rows_kernel,
+        out_shape=jax.ShapeDtypeStruct((4,) + x_rows.shape, x_rows.dtype),
+        in_specs=[IN_VMEM],
+        out_specs=ANY,
+        scratch_shapes=[pltpu.SemaphoreType.DMA, pltpu.SemaphoreType.DMA((2, 6))],
+        compiler_params=pltpu.CompilerParams(
+            collective_id=collective_id, has_side_effects=True, vmem_limit_bytes=8 * 1024 * 1024
+        ),
+        cost_estimate=busy(36),
+        name="square_rows",
+    )(x_rows)
+
+
+def square_project_kernel(x_ref, w_ref, sum_ref, part_buf, relay, got, sems):
+    me = lax.axis_index("head")
+    one, two = square_places(me)
+    rows, width = sum_ref.shape
+    square_barrier(me)
+    sums = square_sums(me, rows, part_buf, relay, got, sems)
+
+    def work(slot, origin):
+        def result(index, carry):
+            span = pl.ds(pl.multiple_of(index * WIDE, WIDE), WIDE)
+            part = nn(x_ref[origin], w_ref[:, span])
+            if slot == 0:
+                sum_ref[:, span] = part
+            else:
+                part_buf[slot, :, span] = part.astype(jnp.bfloat16)
+            return carry
+
+        lax.fori_loop(0, width // WIDE, result, 0)
+
+    work(3, 3 - me)
+    sums[0].start()
+    sums[1].start()
+    work(1, one)
+    sums[2].start()
+    work(2, two)
+    sums[4].start()
+    work(0, me)
+    square_finish(rows, sums, part_buf, relay, got, sum_ref)
+
+
+def square_project(x_rows, weights, collective_id):
+    _, rows, _ = x_rows.shape
+    width = weights.shape[1]
+    kind = jnp.bfloat16
+    return pl.pallas_call(
+        square_project_kernel,
+        out_shape=jax.ShapeDtypeStruct((rows, width), jnp.float32),
+        in_specs=[IN_VMEM, IN_VMEM],
+        out_specs=IN_VMEM,
+        scratch_shapes=[
+            pltpu.VMEM((4, rows, width), kind),
+            pltpu.VMEM((2, rows // 2, width), kind),
+            pltpu.VMEM((2, rows, width), kind),
+            pltpu.SemaphoreType.DMA((2, 6)),
+        ],
+        compiler_params=pltpu.CompilerParams(
+            collective_id=collective_id, has_side_effects=True, vmem_limit_bytes=24 * 1024 * 1024
+        ),
+        cost_estimate=busy(45),
+        name="square_project",
+    )(x_rows, weights)
+
+
+def square_feed_kernel(is_forward, x_ref, up_ref, down_ref, side_ref, *refs):
+    if is_forward:
+        rows_ref, mid_ref, pre_ref, sum_ref = refs[:4]
+        refs = refs[4:]
+    else:
+        rows_ref, mid_ref, sum_ref = refs[:3]
+        refs = refs[3:]
+    land, up_buf, down_buf, mid_buf, pre_buf, part_buf, relay, got, load_sem, in_sems, sum_sems, out_sem = refs
+    me = lax.axis_index("head")
+    rows = x_ref.shape[0]
+    width, ff_width = up_buf.shape
+    loads = [
+        pltpu.make_async_copy(up_ref, up_buf, load_sem.at[0]),
+        pltpu.make_async_copy(down_ref, down_buf, load_sem.at[1]),
+    ]
+    if not is_forward:
+        loads.append(pltpu.make_async_copy(side_ref, pre_buf, load_sem.at[2]))
+    for copy in loads:
+        copy.start()
+    square_barrier(me)
+    gathers = square_gather(me, rows, x_ref, land, (1, 2, 3, 3), (1, 2), in_sems)
+    sums = square_sums(me, rows, part_buf, relay, got, sum_sems)
+
+    def outs(slot):
+        copies = [
+            pltpu.make_async_copy(land.at[slot], rows_ref.at[slot], out_sem.at[0, slot]),
+            pltpu.make_async_copy(mid_buf.at[slot], mid_ref.at[slot], out_sem.at[1, slot]),
+        ]
+        if is_forward:
+            copies.append(
+                pltpu.make_async_copy(pre_buf.at[slot], pre_ref.at[slot], out_sem.at[2, slot])
+            )
+        return copies
+
+    def work(slot):
+        def hidden(index, inner):
+            span = pl.ds(pl.multiple_of(index * WIDE, WIDE), WIDE)
+            if is_forward:
+                pre = nn(land[slot], up_buf[:, span]) + side_ref[:, span]
+                pre_buf[slot, :, span] = pre.astype(jnp.bfloat16)
+                mid_buf[slot, :, span] = gelu(pre).astype(jnp.bfloat16)
+            else:
+                grad = nt(land[slot], down_buf[span, :])
+                slope = gelu_slope(pre_buf[slot, :, span].astype(jnp.float32))
+                mid_buf[slot, :, span] = (grad * slope).astype(jnp.bfloat16)
+            return inner
+
+        def result(index, inner):
+            span = pl.ds(pl.multiple_of(index * WIDE, WIDE), WIDE)
+            if is_forward:
+                part = nn(mid_buf[slot], down_buf[:, span])
+            else:
+                part = nt(mid_buf[slot], up_buf[span, :])
+            if slot == 0:
+                sum_ref[:, span] = part
+            else:
+                part_buf[slot, :, span] = part.astype(jnp.bfloat16)
+            return inner
+
+        lax.fori_loop(0, ff_width // WIDE, hidden, 0)
+        for copy in outs(slot):
+            copy.start()
+        lax.fori_loop(0, width // WIDE, result, 0)
+
+    for index in (0, 2, 1, 3):
+        gathers[index].start()
+    land[0] = x_ref[...]
+    for copy in loads:
+        copy.wait()
+    work(0)
+    gathers[0].wait_recv()
+    gathers[4].start()
+    gathers[2].wait_recv()
+    gathers[5].start()
+    gathers[1].wait_recv()
+    work(1)
+    sums[2].start()
+    gathers[3].wait_recv()
+    work(2)
+    sums[4].start()
+    gathers[4].wait_recv()
+    gathers[5].wait_recv()
+    work(3)
+    sums[0].start()
+    sums[1].start()
+    square_finish(rows, sums, part_buf, relay, got, sum_ref)
+    for copy in gathers:
+        copy.wait_send()
+    for slot in range(4):
+        for copy in outs(slot):
+            copy.wait()
+
+
+def square_feed(x_rows, up_panel, down_panel, side, is_forward, collective_id):
+    rows, width = x_rows.shape
+    ff_width = up_panel.shape[1]
+    kind = jnp.bfloat16
+    by_width = jax.ShapeDtypeStruct((4, rows, width), kind)
+    by_ff = jax.ShapeDtypeStruct((4, rows, ff_width), kind)
+    total = jax.ShapeDtypeStruct((rows, width), jnp.float32)
+    out_shape = (by_width, by_ff, by_ff, total) if is_forward else (by_width, by_ff, total)
+    return pl.pallas_call(
+        functools.partial(square_feed_kernel, is_forward),
+        out_shape=out_shape,
+        in_specs=[IN_VMEM, ANY, ANY, IN_VMEM if is_forward else ANY],
+        out_specs=(ANY,) * (len(out_shape) - 1) + (IN_VMEM,),
+        scratch_shapes=[
+            pltpu.VMEM((4, rows, width), kind),
+            pltpu.VMEM(up_panel.shape, kind),
+            pltpu.VMEM(down_panel.shape, kind),
+            pltpu.VMEM((4, rows, ff_width), kind),
+            pltpu.VMEM((4, rows, ff_width), kind),
+            pltpu.VMEM((4, rows, width), kind),
+            pltpu.VMEM((2, rows // 2, width), kind),
+            pltpu.VMEM((2, rows, width), kind),
+            pltpu.SemaphoreType.DMA((3,)),
+            pltpu.SemaphoreType.DMA((2, 6)),
+            pltpu.SemaphoreType.DMA((2, 6)),
+            pltpu.SemaphoreType.DMA((3, 4)),
+        ],
+        compiler_params=pltpu.CompilerParams(
+            collective_id=collective_id, has_side_effects=True, vmem_limit_bytes=VMEM_MOST
+        ),
+        cost_estimate=busy(80),
+        name="square_forward" if is_forward else "square_backward",
     )(x_rows, up_panel, down_panel, side)
 
 
@@ -1427,7 +1716,14 @@
     attended_grp = collect(
         attended_part.reshape(1, seq_size, rows_grp, HDIM), heads, parts, 1
     )
-    branch_out = group_sums(jnp.dot(attended_grp, o_panel, preferred_element_type=jnp.float32))
+    if head_count == 4:
+        branch_out = square_project(
+            attended_grp.reshape(head_count, tok_count, panel_width), o_panel, 8
+        )
+    else:
+        branch_out = group_sums(
+            jnp.dot(attended_grp, o_panel, preferred_element_type=jnp.float32)
+        )
     z_one = inputs_f32 + branch_out + biases[2]
     h_one, normed_one, recip_one = normalize(z_one, gains[0], biases[3])
     h_low = h_one.astype(jnp.bfloat16)
@@ -1450,7 +1746,11 @@
     dh_one = dz_two + dh_part
     dz_one, dgain_one, dshift_one = normalize_back(dh_one, normed_one, recip_one, gains[0])
     dbias_out = jnp.sum(dz_one, axis=0)
-    dz_one_grp = group_rows(dz_one.astype(jnp.bfloat16))
+    dz_one_low = dz_one.astype(jnp.bfloat16)
+    if head_count == 4:
+        dz_one_grp = square_rows(dz_one_low, 9).reshape(rows_grp, width)
+    else:
+        dz_one_grp = group_rows(dz_one_low)
     dattended = jnp.dot(dz_one_grp, o_panel.T, preferred_element_type=jnp.float32).astype(
         jnp.bfloat16
     )

time: 1190 us -> 1070 us (0.90)
  waiting for transfers between devices: 267 us -> 2.12 us
  Pallas kernels: 790 us -> 934 us
    all_gather x1, waiting for transfers between devices: 81.7 us -> 0.01 us  [shards(): up_panel = lax.all_gather(w_up, 'seq', axis=0, tiled=True)]
    all_gather x1, waiting for transfers between devices: 80.1 us -> 0.01 us  [shards(): down_panel = lax.all_gather(w_down, 'seq', axis=1, tiled=True)]
    pallas_call x1, Pallas kernels: 75.8 us -> 135 us  [start_gathers(): pl.pallas_call(functools.partial(start_kernel, head_count, chips), out_sh...]
    reduce_scatter x2 -> x1, waiting for transfers between devices: 55 us -> 0.01 us  [group_sums(): lax.psum_scatter(partial_value.astype(jnp.bfloat16), 'head', scatter_dime...]
    all_gather x1 -> x0, waiting for transfers between devices: 48 us -> none  [group_rows(): return lax.all_gather(rows_low, 'head', axis=0, tiled=True)]
    pallas_call x2, Pallas kernels: 81.6 us -> 118 us  [spread(): pl.pallas_call(functools.partial(spread_kernel, fields, heads, parts), ou...]
    pallas_call x2, Pallas kernels: 101 us -> 130 us  [collect(): pl.pallas_call(functools.partial(collect_kernel, fields, heads, parts), o...]
    pallas_call x2 -> x4, Pallas kernels: 193 us -> 212 us  [the longest x2 144 us: square_feed(): pl.pallas_call(functools.partial(square_feed_kernel, is_forward), out_sha...]
  transfers between devices with their start and end apart: 7 -> 5, of which waited for: 4 -> 0; matrix products, arithmetic and copies ran while one was open for 6% -> 6% of each run, Pallas kernels for 39% -> 59%
where the time goes in v5:
time: 1070 us; the launch traced here: 1060 us
  Pallas kernels  934 us (87%)
  matrix products  42.3 us (4%)
  other arithmetic  37.5 us (4%)
  local copies, waits for them, and re-layouts  24 us (2%)
  between operations  15.5 us (1%)
    pallas_call x1, Pallas kernels, owned_grads(): pl.pallas_call(functools.partial(grads_kernel, (chips, slots, left_strips...  254 us
    pallas_call x2, Pallas kernels, square_feed(): pl.pallas_call(functools.partial(square_feed_kernel, is_forward), out_sha...  144 us
    pallas_call x1, Pallas kernels, start_gathers(): pl.pallas_call(functools.partial(start_kernel, head_count, chips), out_sh...  135 us
    pallas_call x2, Pallas kernels, collect(): pl.pallas_call(functools.partial(collect_kernel, fields, heads, parts), o...  130 us
    pallas_call x2, Pallas kernels, spread(): pl.pallas_call(functools.partial(spread_kernel, fields, heads, parts), ou...  118 us
    pallas_call x1, Pallas kernels, attend_backward(): pl.pallas_call(functools.partial(backward_kernel, setup), grid=(own,), ou...  49.7 us
    pallas_call x1, Pallas kernels, square_project(): pl.pallas_call(square_project_kernel, out_shape=jax.ShapeDtypeStruct((row...  37.5 us
    pallas_call x1, Pallas kernels, attend_forward(): pl.pallas_call(functools.partial(forward_kernel, setup), grid=(own,), out...  35.9 us
  transfers between devices with their start and end apart: 5, of which 0 were waited for; matrix products, arithmetic and copies ran while one was open for 6% of the time, Pallas kernels for 59%

profile of v5, /device:TPU:0, one launch (start us, length us, event | category | flops | bytes accessed | tf_op | source)
XLA Modules:
  0.0 1055.8 jit_solution(4429299242106490096)
XLA Ops:
  7.3 0.7 all-gather.6.cloned.1.call-update
  8.0 0.7 all-gather.10.cloned.1.call-update
  8.8 0.7 all-gather.8.cloned.1.call-update
  12.7 134.8 %start_gathers.1 = (bf16[4,256,2048]{2,1,0:T(8,128)(2,1)S(1)}, bf16[8,256,1536]{2,1,0:T(8,128)(2,1)S(1)}) custom-call(bf16[256,2048]{1,0:T(8,128)(2,1)S(1)} %copy-done, bf16[256,1536]{1,0:T(8,128)(2,1)S(1)} %pad_maximum_fusion.w_ref), custom_call_target="tpu_custom_call" | custom-call | flops 48000000000 | bytes 1000000 | tf_op jit(solution)/shard_map/start_gathers/pallas_call | solution.py:1587
  147.5 2.7 copy-done.3
  150.2 2.0 copy-done.5
  152.2 1.3 compare_convert_fusion
  153.6 1.2 and_select_fusion.12
  154.8 10.0 add_convert_fusion.x_ref
  164.8 91.5 %spread.2 = bf16[3,8,1024,128]{3,2,1,0:T(8,128)(2,1)S(1)} custom-call(bf16[1024,1536]{1,0:T(8,128)(2,1)S(1)} %add_convert_fusion.x_ref), custom_call_target="tpu_custom_call" | custom-call | flops 57600000000 | bytes 1000000 | tf_op jit(solution)/shard_map/spread/pallas_call | solution.py:118
  256.3 2.7 copy-done.4
  259.0 35.9 %attend_forward.1 = (bf16[32,256,128]{2,1,0:T(8,128)(2,1)}, f32[16,256,128]{2,1,0:T(8,128)}, f32[16,1,256]{2,1,0:T(1,128)}) custom-call(s32[32]{0:T(128)} %select_reduce_fusion.where_ref, s32[32]{0:T(128)} %get-tuple-element.80.low_ref, s32[32]{0:T(128)} %get-tuple-element.79.high_ref, s32[2]{0:T(128)} %bitcast.93, s32[1]{0:T(128)} %bitcast.4.part_ref, ...), custom_call_target="tpu_custom_call" | custom-call | flops 28800000000 | bytes 1000000 | tf_op jit(solution)/shard_map/attend_forward/pallas_call | solution.py:390
  294.9 69.0 %collect.2.refs_1_ = bf16[1024,512]{1,0:T(8,128)(2,1)} custom-call(bf16[1,8,1024,128]{3,2,1,0:T(8,128)(2,1)} %bitcast.100), custom_call_target="tpu_custom_call" | custom-call | flops 19200000000 | bytes 1000000 | tf_op jit(solution)/shard_map/collect/pallas_call | solution.py:219
  363.9 1.6 copy-done.1
  365.5 1.2 copy-done.8
  366.8 37.5 %square_project.1 = f32[256,2048]{1,0:T(8,128)S(1)} custom-call(bf16[4,256,512]{2,1,0:T(8,128)(2,1)S(1)} %bitcast.62, bf16[512,2048]{1,0:T(8,128)(2,1)S(1)} %copy-done.1), custom_call_target="tpu_custom_call" | custom-call | flops 35999997952 | bytes 1000000 | tf_op jit(solution)/shard_map/square_project/pallas_call | solution.py:1338
  405.3 1.4 fusion.18.x_ref
  406.8 72.8 %square_forward.1 = (bf16[4,256,2048]{2,1,0:T(8,128)(2,1)}, bf16[4,256,2048]{2,1,0:T(8,128)(2,1)}, bf16[4,256,2048]{2,1,0:T(8,128)(2,1)}, f32[256,2048]{1,0:T(8,128)}) custom-call(bf16[256,2048]{1,0:T(8,128)(2,1)} %fusion.18.x_ref, bf16[2048,2048]{1,0:T(8,128)(2,1)} %all-gather.8.cloned.1.call-done.up_ref, ...), custom_call_target="tpu_custom_call" | custom-call | flops 64000000000 | bytes 1000000 | tf_op jit(solution)/shard_map/square_forward/pallas_call | solution.py:1458
  479.6 2.3 fusion.45
  482.3 0.8 copy-done.14
  483.1 1.6 multiply_reduce_fusion
  484.7 2.6 fusion.43
  487.4 1.3 copy-done.10
  488.7 1.1 convert_element_type.64.x_ref
  489.8 71.4 %square_backward.1 = (bf16[4,256,2048]{2,1,0:T(8,128)(2,1)}, bf16[4,256,2048]{2,1,0:T(8,128)(2,1)}, f32[256,2048]{1,0:T(8,128)}) custom-call(bf16[256,2048]{1,0:T(8,128)(2,1)} %convert_element_type.64.x_ref, bf16[2048,2048]{1,0:T(8,128)(2,1)} %all-gather.8.cloned.1.call-done.up_ref, bf16[2048,2048]{1,0:T(8,128)(2,1)} %all-gather.10.cloned.1.call-done.down_ref, ...), custom_call_target="tpu_custom_call" | custom-call | flops 64000000000 | bytes 1000000 | tf_op jit(solution)/shard_map/square_backward/pallas_call | solution.py:1458
  561.2 3.8 multiply_reduce_fusion.1
  565.0 1.3 fusion.44
  566.3 1.3 copy-done.11
  567.8 29.8 %square_rows.1 = bf16[4,256,2048]{2,1,0:T(8,128)(2,1)S(1)} custom-call(bf16[256,2048]{1,0:T(8,128)(2,1)S(1)} %convert_element_type.65.x_ref), custom_call_target="tpu_custom_call" | custom-call | flops 28800000000 | bytes 1000000 | tf_op jit(solution)/shard_map/square_rows/pallas_call | solution.py:1290
  597.6 2.0 copy-done.6
  599.6 2.4 convolution_convert_fusion.1.x_ref
  601.9 27.0 %spread.3 = bf16[1,8,1024,128]{3,2,1,0:T(8,128)(2,1)S(1)} custom-call(bf16[1024,512]{1,0:T(8,128)(2,1)S(1)} %convolution_convert_fusion.1.x_ref), custom_call_target="tpu_custom_call" | custom-call | flops 19200000000 | bytes 1000000 | tf_op jit(solution)/shard_map/spread/pallas_call | solution.py:118
  628.9 1.3 copy-done.7
  630.2 49.7 %attend_backward.1 = bf16[3,32,256,128]{3,2,1,0:T(8,128)(2,1)} custom-call(s32[32]{0:T(128)} %select_reduce_fusion.where_ref, s32[32]{0:T(128)} %get-tuple-element.80.low_ref, s32[32]{0:T(128)} %get-tuple-element.79.high_ref, s32[2]{0:T(128)} %bitcast.94, s32[1]{0:T(128)} %bitcast.4.part_ref, bf16[3,32,256,128]{3,2,1,0:T(8,128)(2,1)} %bitcast.56, ...), custom_call_target="tpu_custom_call" | custom-call | flops 40000000000 | bytes 1000000 | tf_op jit(solution)/shard_map/attend_backward/pallas_call | solution.py:612
  679.9 60.8 %collect.3.refs_4_ = bf16[1024,1536]{1,0:T(8,128)(2,1)} custom-call(bf16[3,8,1024,128]{3,2,1,0:T(8,128)(2,1)} %bitcast.96), custom_call_target="tpu_custom_call" | custom-call | flops 57600000000 | bytes 1000000 | tf_op jit(solution)/shard_map/collect/pallas_call | solution.py:219
  740.8 2.4 convert_reduce_fusion.1
  743.4 3.0 convert_reduce_fusion
  748.5 11.0 %convolution_convert_fusion = bf16[1024,2048]{1,0:T(8,128)(2,1)} fusion(bf16[1024,1536]{1,0:T(8,128)(2,1)S(1)} %copy-done.15, bf16[2048,1536]{1,0:T(8,128)(2,1)} %bitcast.54), kind=kOutput, calls=%fused_computation.6 | convolution fusion | flops 6444548096 | bytes 13631488 | tf_op jit(solution)/shard_map/dot_general | solution.py:1763
  759.5 253.9 %owned_grads.1 = bf16[24,256,256]{2,1,0:T(8,128)(2,1)} custom-call(s32[192]{0:T(256)} %get-tuple-element.76.left_ref, s32[192]{0:T(256)} %get-tuple-element.75.right_ref, bf16[1024,2048]{1,0:T(8,128)(2,1)} %bitcast.58, bf16[1024,512]{1,0:T(8,128)(2,1)} %collect.2.refs_1_, bf16[1024,2048]{1,0:T(8,128)(2,1)} %bitcast.97, bf16[1024,2048]{1,0:T(8,128)(2,1)} %bitcast.98, ...), custom_call_target="tpu_custom_call" | custom-call | flops 192000000000 | bytes 1000000 | tf_op jit(solution)/shard_map/owned_grads/pallas_call | solution.py:947
  1013.5 6.0 convert_element_type.69
  1019.5 0.7 copy-done.13
  1020.2 4.0 add_multiply_fusion
  1024.2 3.7 add_multiply_fusion.1
  1027.9 11.3 %multiply_subtract_fusion = f32[24,256,256]{2,1,0:T(8,128)} fusion(f32[24,256,256]{2,1,0:T(8,128)} %param.47, f32[24,256,256]{2,1,0:T(8,128)} %param.46, bf16[24,256,256]{2,1,0:T(8,128)(2,1)S(1)} %copy-done.9, f32[24,256,256]{2,1,0:T(8,128)} %param.45), kind=kOutput, calls=%fused_computation.2 | convolution fusion | flops 1618477056 | bytes 28311552 | tf_op jit(solution)/shard_map/bij,bjk->bik/dot_general | solution.py:1814
  1039.2 2.9 reshape.177
  1042.1 1.9 slice_reduce_fusion
  1044.1 0.7 maximum_subtract_fusion
  1046.2 2.8 convert_add_fusion
  (147 shorter events, 7.9 us)
Async XLA Ops:
  7.2 2.4 copy-start.47
  7.2 3.1 copy-start.21
  7.2 3.8 copy-start.30
  7.2 4.8 copy-start.28
  7.2 5.4 copy-start.18
  7.2 5.3 copy-start.17
  7.2 5.3 copy-start.16
  7.3 5.4 copy-start
  7.3 356.7 %all-gather.6.cloned.1.call-start = ((), (), s32[]{:S(2)}) async-start(), calls=%async_computation.1 | async-start | bytes 2359296 | tf_op jit(solution)/shard_map/all_gather | solution.py:1699
  8.0 398.8 %all-gather.10.cloned.1.call-start = ((), (), s32[]{:S(2)}) async-start(), calls=%async_computation.3 | async-start | bytes 9437184 | tf_op jit(solution)/shard_map/all_gather | solution.py:1701
  8.8 398.0 %all-gather.8.cloned.1.call-start = ((), (), s32[]{:S(2)}) async-start(), calls=%async_computation.2 | async-start | bytes 9437184 | tf_op jit(solution)/shard_map/all_gather | solution.py:1700
  9.5 1029.7 %all-gather.12.cloned.1.call-start = ((), (), s32[]{:S(2)}) async-start(), calls=%async_computation.5 | async-start | bytes 2433024 | tf_op jit(solution)/shard_map/all_gather | solution.py:1786
  9.7 143.7 %copy-start.46 = (s32[2,1]{0,1:T(1,128)}, s32[2,1]{0,1:T(1,128)S(1)}, u32[]{:S(2)}) copy-start(s32[2,1]{0,1:T(1,128)S(1)} %reduce-window.4) | copy-start | bytes 28
  147.5 2.7 copy-start.3
  150.2 2.0 copy-start.5
  256.3 2.7 copy-start.4
  363.9 1.6 copy-start.1
  366.8 37.5 %copy-start.33 = (f32[1,2048]{1,0:T(1,128)S(1)}, f32[1,2048]{1,0:T(1,128)}, u32[]{:S(2)}) copy-start(f32[1,2048]{1,0:T(1,128)} %get-tuple-element.68) | copy-start | bytes 24580
  406.8 72.8 %copy-start.32 = (f32[1,2048]{1,0:T(1,128)S(1)}, f32[1,2048]{1,0:T(1,128)}, u32[]{:S(2)}) copy-start(f32[1,2048]{1,0:T(1,128)} %get-tuple-element.66) | copy-start | bytes 24580
  482.3 2.5 copy-start.31
  566.3 1.3 copy-start.11
  567.8 31.8 %copy-start.2 = (bf16[512,2048]{1,0:T(8,128)(2,1)S(1)}, bf16[512,2048]{1,0:T(8,128)(2,1)}, u32[]{:S(2)}) copy-start(bf16[512,2048]{1,0:T(8,128)(2,1)} %all-gather.6.cloned.1.call-done.w_ref) | copy-start | bytes 6291460
  597.6 2.0 copy-start.6
  740.7 2.5 copy-start.34
  740.7 2.5 copy-start.35
  740.7 2.5 copy-start.36
  740.7 2.5 copy-start.37
  740.7 2.5 copy-start.38
  740.7 2.5 copy-start.39
  743.4 4.5 copy-start.45
  743.4 5.0 copy-start.15
  747.1 299.1 %reduce-scatter.2.cloned.1.call-start = ((), (), s32[]{:S(2)}) async-start(), calls=%async_computation.4 | async-start | bytes 5242880 | tf_op jit(solution)/shard_map/reduce_scatter | solution.py:1633
  1013.5 6.0 copy-start.9
  1013.5 6.7 copy-start.13
  1013.5 10.7 %slice-start.1 = ((s8[6291456]{0:T(1024)(128)(4,1)}), s8[4194304]{0:T(1024)(128)(4,1)S(1)}, s32[]{:S(2)}) async-start(s8[6291456]{0:T(1024)(128)(4,1)} %bitcast.63), calls=%async_computation.7 | async-start | bytes 8388608
  1020.2 4.0 slice-start.2
  1042.0 2.1 copy-start.22
  1042.0 2.1 copy-start.26
  1042.0 2.1 copy-start.27
  1042.0 2.1 copy-start.29
  1042.1 3.4 slice-start
  1042.1 3.4 copy-start.42
  1042.1 3.4 copy-start.43
  1042.1 3.4 copy-start.44
  1042.1 4.1 copy-start.12
  1044.1 4.9 copy-start.19
  1044.9 4.1 copy-start.23
  1045.5 3.5 copy-start.40
  (8 other events, 8.9 us)
Sparse Core Ops, SparseCore 0:
  9.7 46.7 all-gather.5
  58.0 106.1 all-gather.9
  165.8 142.1 all-gather.7
  747.2 73.5 all-gather.11
  823.6 52.1 reduce-scatter.1

commit v6 on v5

--- a/solution.py
+++ b/solution.py
@@ -1301,7 +1301,7 @@
     )(x_rows)
 
 
-def square_project_kernel(x_ref, w_ref, sum_ref, part_buf, relay, got, sems):
+def square_project_kernel(by_slot, x_ref, w_ref, sum_ref, part_buf, relay, got, sems):
     me = lax.axis_index("head")
     one, two = square_places(me)
     rows, width = sum_ref.shape
@@ -1309,9 +1309,11 @@
     sums = square_sums(me, rows, part_buf, relay, got, sems)
 
     def work(slot, origin):
+        place = slot if by_slot else origin
+
         def result(index, carry):
             span = pl.ds(pl.multiple_of(index * WIDE, WIDE), WIDE)
-            part = nn(x_ref[origin], w_ref[:, span])
+            part = nn(x_ref[place], w_ref[:, span])
             if slot == 0:
                 sum_ref[:, span] = part
             else:
@@ -1331,12 +1333,12 @@
     square_finish(rows, sums, part_buf, relay, got, sum_ref)
 
 
-def square_project(x_rows, weights, collective_id):
+def square_project(x_rows, weights, by_slot, collective_id):
     _, rows, _ = x_rows.shape
     width = weights.shape[1]
     kind = jnp.bfloat16
     return pl.pallas_call(
-        square_project_kernel,
+        functools.partial(square_project_kernel, by_slot),
         out_shape=jax.ShapeDtypeStruct((rows, width), jnp.float32),
         in_specs=[IN_VMEM, IN_VMEM],
         out_specs=IN_VMEM,
@@ -1347,11 +1349,85 @@
             pltpu.SemaphoreType.DMA((2, 6)),
         ],
         compiler_params=pltpu.CompilerParams(
-            collective_id=collective_id, has_side_effects=True, vmem_limit_bytes=24 * 1024 * 1024
+            collective_id=collective_id, has_side_effects=True, vmem_limit_bytes=40 * 1024 * 1024
         ),
         cost_estimate=busy(45),
         name="square_project",
     )(x_rows, weights)
+
+
+def square_hidden_kernel(x_ref, up_ref, bias_ref, rows_ref, mid_ref, pre_ref, land, mid_buf, pre_buf, in_sems, out_sem):
+    me = lax.axis_index("head")
+    rows = x_ref.shape[0]
+    ff_width = up_ref.shape[1]
+    square_barrier(me)
+    gathers = square_gather(me, rows, x_ref, land, (1, 2, 3, 3), (1, 2), in_sems)
+
+    def outs(slot):
+        return (
+            pltpu.make_async_copy(land.at[slot], rows_ref.at[slot], out_sem.at[0, slot]),
+            pltpu.make_async_copy(mid_buf.at[slot], mid_ref.at[slot], out_sem.at[1, slot]),
+            pltpu.make_async_copy(pre_buf.at[slot], pre_ref.at[slot], out_sem.at[2, slot]),
+        )
+
+    def work(slot):
+        def hidden(index, inner):
+            span = pl.ds(pl.multiple_of(index * WIDE, WIDE), WIDE)
+            pre = nn(land[slot], up_ref[:, span]) + bias_ref[:, span]
+            pre_buf[slot, :, span] = pre.astype(jnp.bfloat16)
+            mid_buf[slot, :, span] = gelu(pre).astype(jnp.bfloat16)
+            return inner
+
+        lax.fori_loop(0, ff_width // WIDE, hidden, 0)
+        for copy in outs(slot):
+            copy.start()
+
+    for index in (0, 2, 1, 3):
+        gathers[index].start()
+    land[0] = x_ref[...]
+    work(0)
+    gathers[0].wait_recv()
+    gathers[4].start()
+    gathers[2].wait_recv()
+    gathers[5].start()
+    gathers[1].wait_recv()
+    work(1)
+    gathers[3].wait_recv()
+    work(2)
+    gathers[4].wait_recv()
+    gathers[5].wait_recv()
+    work(3)
+    for copy in gathers:
+        copy.wait_send()
+    for slot in range(4):
+        for copy in outs(slot):
+            copy.wait()
+
+
+def square_hidden(x_rows, up_panel, bias, collective_id):
+    rows, width = x_rows.shape
+    ff_width = up_panel.shape[1]
+    kind = jnp.bfloat16
+    by_width = jax.ShapeDtypeStruct((4, rows, width), kind)
+    by_ff = jax.ShapeDtypeStruct((4, rows, ff_width), kind)
+    return pl.pallas_call(
+        square_hidden_kernel,
+        out_shape=(by_width, by_ff, by_ff),
+        in_specs=[IN_VMEM] * 3,
+        out_specs=(ANY,) * 3,
+        scratch_shapes=[
+            pltpu.VMEM((4, rows, width), kind),
+            pltpu.VMEM((4, rows, ff_width), kind),
+            pltpu.VMEM((4, rows, ff_width), kind),
+            pltpu.SemaphoreType.DMA((2, 6)),
+            pltpu.SemaphoreType.DMA((3, 4)),
+        ],
+        compiler_params=pltpu.CompilerParams(
+            collective_id=collective_id, has_side_effects=True, vmem_limit_bytes=40 * 1024 * 1024
+        ),
+        cost_estimate=busy(45),
+        name="square_hidden",
+    )(x_rows, up_panel, bias)
 
 
 def square_feed_kernel(is_forward, x_ref, up_ref, down_ref, side_ref, *refs):
@@ -1718,7 +1794,7 @@
     )
     if head_count == 4:
         branch_out = square_project(
-            attended_grp.reshape(head_count, tok_count, panel_width), o_panel, 8
+            attended_grp.reshape(head_count, tok_count, panel_width), o_panel, False, 8
         )
     else:
         branch_out = group_sums(
@@ -1727,9 +1803,14 @@
     z_one = inputs_f32 + branch_out + biases[2]
     h_one, normed_one, recip_one = normalize(z_one, gains[0], biases[3])
     h_low = h_one.astype(jnp.bfloat16)
-    h_grp, act, pre_act, ff_out = feed(
-        h_low, up_panel, down_panel, up_bias.reshape(1, ff_width), True, head_count, 5
-    )
+    hidden_bias = up_bias.reshape(1, ff_width)
+    if head_count == 4:
+        h_grp, act, pre_act = square_hidden(h_low, up_panel, hidden_bias, 5)
+        ff_out = square_project(act, down_panel, True, 10)
+    else:
+        h_grp, act, pre_act, ff_out = feed(
+            h_low, up_panel, down_panel, hidden_bias, True, head_count, 5
+        )
     z_two = h_one + ff_out + biases[4]
     layer_f32, normed_two, recip_two = normalize(z_two, gains[1], biases[5])
     layer_out = layer_f32.astype(jnp.bfloat16)

time: 1070 us -> 1070 us (level)
    pallas_call x1 -> x3, Pallas kernels: 37.5 us -> 121 us  [the longest x2 78.3 us: square_project(): pl.pallas_call(functools.partial(square_project_kernel, by_slot), out_sha...]
    pallas_call x2 -> x1, Pallas kernels: 144 us -> 71.8 us  [square_feed(): pl.pallas_call(functools.partial(square_feed_kernel, is_forward), out_sha...]
    unnamed x101 -> x105, local copies, waits for them, and re-layouts: 18.2 us -> 23 us
  transfers between devices with their start and end apart: 5 -> 5, of which waited for: 0 -> 0; matrix products, arithmetic and copies ran while one was open for 6% -> 5% of each run, Pallas kernels for 59% -> 62%
where the time goes in v6:
time: 1070 us; the launch traced here: 1060 us
  Pallas kernels  940 us (88%)
  matrix products  39.9 us (4%)
  other arithmetic  37.5 us (4%)
  local copies, waits for them, and re-layouts  28.8 us (3%)
  between operations  15.6 us (1%)
    pallas_call x1, Pallas kernels, owned_grads(): pl.pallas_call(functools.partial(grads_kernel, (chips, slots, left_strips...  254 us
    pallas_call x1, Pallas kernels, start_gathers(): pl.pallas_call(functools.partial(start_kernel, head_count, chips), out_sh...  130 us
    pallas_call x2, Pallas kernels, spread(): pl.pallas_call(functools.partial(spread_kernel, fields, heads, parts), ou...  124 us
    pallas_call x2, Pallas kernels, collect(): pl.pallas_call(functools.partial(collect_kernel, fields, heads, parts), o...  122 us
    pallas_call x2, Pallas kernels, square_project(): pl.pallas_call(functools.partial(square_project_kernel, by_slot), out_sha...  78.3 us
    pallas_call x1, Pallas kernels, square_feed(): pl.pallas_call(functools.partial(square_feed_kernel, is_forward), out_sha...  71.8 us
    pallas_call x1, Pallas kernels, attend_backward(): pl.pallas_call(functools.partial(backward_kernel, setup), grid=(own,), ou...  49.7 us
    pallas_call x1, Pallas kernels, square_hidden(): pl.pallas_call(square_hidden_kernel, out_shape=(by_width, by_ff, by_ff),...  42.3 us
  transfers between devices with their start and end apart: 5, of which 0 were waited for; matrix products, arithmetic and copies ran while one was open for 5% of the time, Pallas kernels for 62%

profile of v6, /device:TPU:0, one launch (start us, length us, event | category | flops | bytes accessed | tf_op | source)
XLA Modules:
  0.0 1064.1 jit_solution(17552719341350988934)
XLA Ops:
  8.0 0.7 all-gather.8.cloned.1.call-update
  8.8 0.7 all-gather.10.cloned.1.call-update
  10.2 129.9 %start_gathers.1 = (bf16[4,256,2048]{2,1,0:T(8,128)(2,1)S(1)}, bf16[8,256,1536]{2,1,0:T(8,128)(2,1)S(1)}) custom-call(bf16[256,2048]{1,0:T(8,128)(2,1)S(1)} %copy-done, bf16[256,1536]{1,0:T(8,128)(2,1)S(1)} %pad_maximum_fusion.w_ref), custom_call_target="tpu_custom_call" | custom-call | flops 48000000000 | bytes 1000000 | tf_op jit(solution)/shard_map/start_gathers/pallas_call | solution.py:1663
  140.2 2.6 copy-done.4
  142.9 6.9 add_convert_fusion.x_ref
  149.8 97.0 %spread.2 = bf16[3,8,1024,128]{3,2,1,0:T(8,128)(2,1)S(1)} custom-call(bf16[1024,1536]{1,0:T(8,128)(2,1)S(1)} %add_convert_fusion.x_ref), custom_call_target="tpu_custom_call" | custom-call | flops 57600000000 | bytes 1000000 | tf_op jit(solution)/shard_map/spread/pallas_call | solution.py:118
  246.8 2.7 copy-done.5
  250.6 1.3 compare_convert_fusion
  252.6 1.2 and_select_fusion.12
  254.4 36.0 %attend_forward.1 = (bf16[32,256,128]{2,1,0:T(8,128)(2,1)}, f32[16,256,128]{2,1,0:T(8,128)}, f32[16,1,256]{2,1,0:T(1,128)}) custom-call(s32[32]{0:T(128)} %select_reduce_fusion.where_ref, s32[32]{0:T(128)} %get-tuple-element.78.low_ref, s32[32]{0:T(128)} %get-tuple-element.77.high_ref, s32[2]{0:T(128)} %bitcast.95, s32[1]{0:T(128)} %bitcast.4.part_ref, ...), custom_call_target="tpu_custom_call" | custom-call | flops 28800000000 | bytes 1000000 | tf_op jit(solution)/shard_map/attend_forward/pallas_call | solution.py:390
  290.4 61.5 %collect.2.refs_1_ = bf16[1024,512]{1,0:T(8,128)(2,1)} custom-call(bf16[1,8,1024,128]{3,2,1,0:T(8,128)(2,1)} %bitcast.100), custom_call_target="tpu_custom_call" | custom-call | flops 19200000000 | bytes 1000000 | tf_op jit(solution)/shard_map/collect/pallas_call | solution.py:219
  352.0 1.6 copy-done.2
  353.6 1.2 copy-done.12
  354.8 37.5 %square_project.2 = f32[256,2048]{1,0:T(8,128)S(1)} custom-call(bf16[4,256,512]{2,1,0:T(8,128)(2,1)S(1)} %bitcast.65, bf16[512,2048]{1,0:T(8,128)(2,1)S(1)} %copy-done.2), custom_call_target="tpu_custom_call" | custom-call | flops 35999997952 | bytes 1000000 | tf_op jit(solution)/shard_map/square_project/pallas_call | solution.py:1340
  393.9 42.3 %square_hidden.1 = (bf16[4,256,2048]{2,1,0:T(8,128)(2,1)S(1)}, bf16[4,256,2048]{2,1,0:T(8,128)(2,1)S(1)}, bf16[4,256,2048]{2,1,0:T(8,128)(2,1)S(1)}) custom-call(bf16[256,2048]{1,0:T(8,128)(2,1)S(1)} %fusion.18.x_ref, bf16[2048,2048]{1,0:T(8,128)(2,1)} %all-gather.8.cloned.1.call-done.up_ref, f32[1,2048]{1,0:T(1,128)S(1)} %bitcast.53), custom_call_target="tpu_custom_call" | custom-call | flops 35999997952 | bytes 1000000 | tf_op jit(solution)/shard_map/square_hidden/pallas_call | solution.py:1413
  436.1 2.0 copy-done.7
  438.1 2.0 copy-done.8
  440.1 2.0 copy-done.13
  442.1 2.2 copy-done.9
  444.3 40.8 %square_project.3 = f32[256,2048]{1,0:T(8,128)S(1)} custom-call(bf16[4,256,2048]{2,1,0:T(8,128)(2,1)S(1)} %copy-done.9, bf16[2048,2048]{1,0:T(8,128)(2,1)} %all-gather.10.cloned.1.call-done.w_ref.down_ref), custom_call_target="tpu_custom_call" | custom-call | flops 35999997952 | bytes 1000000 | tf_op jit(solution)/shard_map/square_project/pallas_call | solution.py:1340
  486.3 0.8 copy-done.18
  487.1 1.6 multiply_reduce_fusion
  488.7 3.3 fusion.43
  492.0 2.8 convert_element_type.64.x_ref
  494.8 71.8 %square_backward.1 = (bf16[4,256,2048]{2,1,0:T(8,128)(2,1)}, bf16[4,256,2048]{2,1,0:T(8,128)(2,1)}, f32[256,2048]{1,0:T(8,128)}) custom-call(bf16[256,2048]{1,0:T(8,128)(2,1)} %convert_element_type.64.x_ref, bf16[2048,2048]{1,0:T(8,128)(2,1)} %all-gather.8.cloned.1.call-done.up_ref, bf16[2048,2048]{1,0:T(8,128)(2,1)} %all-gather.10.cloned.1.call-done.w_ref.down_ref, ...), custom_call_target="tpu_custom_call" | custom-call | flops 64000000000 | bytes 1000000 | tf_op jit(solution)/shard_map/square_backward/pallas_call | solution.py:1534
  566.6 3.9 multiply_reduce_fusion.1
  570.6 1.3 fusion.44
  571.9 1.3 copy-done.15
  573.4 31.3 %square_rows.1 = bf16[4,256,2048]{2,1,0:T(8,128)(2,1)S(1)} custom-call(bf16[256,2048]{1,0:T(8,128)(2,1)S(1)} %convert_element_type.65.x_ref), custom_call_target="tpu_custom_call" | custom-call | flops 28800000000 | bytes 1000000 | tf_op jit(solution)/shard_map/square_rows/pallas_call | solution.py:1290
  604.7 1.9 copy-done.10
  606.7 2.4 convolution_convert_fusion.1.x_ref
  609.1 27.4 %spread.3 = bf16[1,8,1024,128]{3,2,1,0:T(8,128)(2,1)S(1)} custom-call(bf16[1024,512]{1,0:T(8,128)(2,1)S(1)} %convolution_convert_fusion.1.x_ref), custom_call_target="tpu_custom_call" | custom-call | flops 19200000000 | bytes 1000000 | tf_op jit(solution)/shard_map/spread/pallas_call | solution.py:118
  636.4 1.3 copy-done.11
  637.7 49.7 %attend_backward.1 = bf16[3,32,256,128]{3,2,1,0:T(8,128)(2,1)} custom-call(s32[32]{0:T(128)} %select_reduce_fusion.where_ref, s32[32]{0:T(128)} %get-tuple-element.78.low_ref, s32[32]{0:T(128)} %get-tuple-element.77.high_ref, s32[2]{0:T(128)} %bitcast.96, s32[1]{0:T(128)} %bitcast.4.part_ref, bf16[3,32,256,128]{3,2,1,0:T(8,128)(2,1)} %bitcast.57, ...), custom_call_target="tpu_custom_call" | custom-call | flops 40000000000 | bytes 1000000 | tf_op jit(solution)/shard_map/attend_backward/pallas_call | solution.py:612
  687.4 60.9 %collect.3.refs_4_ = bf16[1024,1536]{1,0:T(8,128)(2,1)} custom-call(bf16[3,8,1024,128]{3,2,1,0:T(8,128)(2,1)} %bitcast.98), custom_call_target="tpu_custom_call" | custom-call | flops 57600000000 | bytes 1000000 | tf_op jit(solution)/shard_map/collect/pallas_call | solution.py:219
  748.4 2.4 convert_reduce_fusion.1
  751.1 3.0 convert_reduce_fusion
  756.1 11.0 %convolution_convert_fusion = bf16[1024,2048]{1,0:T(8,128)(2,1)} fusion(bf16[1024,1536]{1,0:T(8,128)(2,1)S(1)} %copy-done.19, bf16[2048,1536]{1,0:T(8,128)(2,1)} %bitcast.55), kind=kOutput, calls=%fused_computation.6 | convolution fusion | flops 6444548096 | bytes 13631488 | tf_op jit(solution)/shard_map/dot_general | solution.py:1844
  767.2 253.9 %owned_grads.1 = bf16[24,256,256]{2,1,0:T(8,128)(2,1)} custom-call(s32[192]{0:T(256)} %get-tuple-element.74.left_ref, s32[192]{0:T(256)} %get-tuple-element.73.right_ref, bf16[1024,2048]{1,0:T(8,128)(2,1)} %bitcast.59, bf16[1024,512]{1,0:T(8,128)(2,1)} %collect.2.refs_1_, bf16[1024,2048]{1,0:T(8,128)(2,1)} %bitcast.60, bf16[1024,2048]{1,0:T(8,128)(2,1)} %bitcast.61, ...), custom_call_target="tpu_custom_call" | custom-call | flops 192000000000 | bytes 1000000 | tf_op jit(solution)/shard_map/owned_grads/pallas_call | solution.py:947
  1021.1 6.0 convert_element_type.69
  1027.1 0.7 copy-done.17
  1027.9 4.2 add_multiply_fusion
  1032.1 4.0 add_multiply_fusion.1
  1036.1 11.4 %multiply_subtract_fusion = f32[24,256,256]{2,1,0:T(8,128)} fusion(f32[24,256,256]{2,1,0:T(8,128)} %param.47, f32[24,256,256]{2,1,0:T(8,128)} %param.46, bf16[24,256,256]{2,1,0:T(8,128)(2,1)S(1)} %copy-done.14, f32[24,256,256]{2,1,0:T(8,128)} %param.45), kind=kOutput, calls=%fused_computation.2 | convolution fusion | flops 1618477056 | bytes 28311552 | tf_op jit(solution)/shard_map/bij,bjk->bik/dot_general | solution.py:1895
  1047.4 2.9 reshape.177
  1050.4 2.0 slice_reduce_fusion
  1052.4 0.7 maximum_subtract_fusion
  1054.5 2.8 convert_add_fusion
  (152 shorter events, 9.7 us)
Async XLA Ops:
  7.2 2.3 copy-start.24
  7.2 3.0 copy-start.22
  7.2 3.0 copy-start.21
  7.2 3.0 copy-start.20
  7.2 3.0 copy-start
  7.2 344.7 %all-gather.6.cloned.1.call-start = ((), (), s32[]{:S(2)}) async-start(), calls=%async_computation.1 | async-start | bytes 2359296 | tf_op jit(solution)/shard_map/all_gather | solution.py:1775
  8.0 385.9 %all-gather.8.cloned.1.call-start = ((), (), s32[]{:S(2)}) async-start(), calls=%async_computation.2 | async-start | bytes 9437184 | tf_op jit(solution)/shard_map/all_gather | solution.py:1776
  8.7 433.4 %all-gather.10.cloned.1.call-start = ((), (), s32[]{:S(2)}) async-start(), calls=%async_computation.3 | async-start | bytes 9437184 | tf_op jit(solution)/shard_map/all_gather | solution.py:1777
  9.5 1038.0 %all-gather.12.cloned.1.call-start = ((), (), s32[]{:S(2)}) async-start(), calls=%async_computation.5 | async-start | bytes 2433024 | tf_op jit(solution)/shard_map/all_gather | solution.py:1867
  140.2 2.7 copy-start.4
  140.2 9.6 copy-start.6
  149.8 99.8 %copy-start.49 = (s32[2]{0:T(128)S(1)}, s32[2]{0:T(128)}, u32[]{:S(2)}) copy-start(s32[2]{0:T(128)} %param.26) | copy-start | bytes 28
  149.8 100.5 %copy-start.33 = (s32[8192]{0:T(1024)S(1)}, s32[8192]{0:T(1024)}, u32[]{:S(2)}) copy-start(s32[8192]{0:T(1024)} %param.27) | copy-start | bytes 98308
  149.8 104.0 %copy-start.31 = (f32[2,2048]{1,0:T(2,128)S(1)}, f32[2,2048]{1,0:T(2,128)}, u32[]{:S(2)}) copy-start(f32[2,2048]{1,0:T(2,128)} %param.35) | copy-start | bytes 49156
  246.8 2.7 copy-start.5
  249.7 4.7 copy-start.48
  354.8 37.5 %copy-start.36 = (f32[1,2048]{1,0:T(1,128)S(1)}, f32[1,2048]{1,0:T(1,128)}, u32[]{:S(2)}) copy-start(f32[1,2048]{1,0:T(1,128)} %get-tuple-element.66) | copy-start | bytes 24580
  436.1 2.0 copy-start.7
  438.1 2.0 copy-start.8
  440.1 2.0 copy-start.13
  442.1 2.2 copy-start.9
  444.3 40.8 %copy-start.35 = (f32[1,2048]{1,0:T(1,128)S(1)}, f32[1,2048]{1,0:T(1,128)}, u32[]{:S(2)}) copy-start(f32[1,2048]{1,0:T(1,128)} %get-tuple-element.64) | copy-start | bytes 24580
  486.2 2.5 copy-start.34
  573.4 33.3 %copy-start.3 = (bf16[512,2048]{1,0:T(8,128)(2,1)S(1)}, bf16[512,2048]{1,0:T(8,128)(2,1)}, u32[]{:S(2)}) copy-start(bf16[512,2048]{1,0:T(8,128)(2,1)} %all-gather.6.cloned.1.call-done.w_ref) | copy-start | bytes 6291460
  748.3 2.5 copy-start.37
  748.3 2.5 copy-start.38
  748.4 2.5 copy-start.39
  748.4 2.5 copy-start.40
  748.4 2.5 copy-start.41
  748.4 2.5 copy-start.42
  751.1 4.4 copy-start.47
  751.1 5.0 copy-start.19
  754.7 299.7 %reduce-scatter.2.cloned.1.call-start = ((), (), s32[]{:S(2)}) async-start(), calls=%async_computation.4 | async-start | bytes 5242880 | tf_op jit(solution)/shard_map/reduce_scatter | solution.py:1709
  1021.1 6.0 copy-start.14
  1021.1 6.7 copy-start.17
  1021.1 10.9 %slice-start.1 = ((s8[6291456]{0:T(1024)(128)(4,1)}), s8[4194304]{0:T(1024)(128)(4,1)S(1)}, s32[]{:S(2)}) async-start(s8[6291456]{0:T(1024)(128)(4,1)} %bitcast.66), calls=%async_computation.7 | async-start | bytes 8388608
  1027.9 4.2 slice-start.2
  1050.3 2.1 copy-start.25
  1050.3 2.1 copy-start.29
  1050.3 2.1 copy-start.30
  1050.3 2.1 copy-start.32
  1050.3 3.4 slice-start
  1050.3 3.4 copy-start.45
  1050.4 3.4 copy-start.46
  1050.4 4.1 copy-start.16
  1052.4 4.9 copy-start.23
  1053.1 4.2 copy-start.26
  1053.8 3.5 copy-start.43
  (10 other events, 12.6 us)
Sparse Core Ops, SparseCore 0:
  9.6 45.7 all-gather.5
  57.0 95.9 all-gather.7
  154.6 136.2 all-gather.9
  754.9 73.1 all-gather.11
  830.9 52.2 reduce-scatter.1
